TPU v7x, 32 devices: a whole 2x2x4 slice. The times are simulated.
32 devices in a mesh: gz: 8 (over z, x), gy: 4 (over y, core).
Axes of the slice: x: 2, y: 2, z: 4, core: 2. Of those that a mesh axis runs over, the one named last changes fastest.
Arguments:
- ranks: float32 [64, 64, 512], P('gz', 'gy'), may hold values from 1 to 2
- seeds: float32 [3, 64, 64, 512], P(None, 'gz', 'gy'), may hold values from 0.25 to 1
- flags: int32 [64, 64, 512], P('gz', 'gy'), may hold values 0 or 1
Outputs:
- states: int32 [64, 64, 512], P('gz', 'gy')
- undecided: int32 [3], replicated
All inputs are finite; a program needn't handle non-finite values. No bound on the sum of `flags` on one device may be relied on, other than what follows from the above.
Results may differ from a plain program's by a relative error of at most 0.000001.
Values sent between devices are 32-bit elements; how exact they have to be, the bound alone decides.
No kernel may reach another device: no remote copies, remote signals or barrier semaphores. Data moves between devices by JAX's collectives and lax.ppermute only.
A program may use at most 64 MiB of HBM per device.

v0:
```python
import jax
import jax.numpy as jnp
from jax import lax
from jax.sharding import PartitionSpec as P

ROUNDS = 3


def passed_along(value, axis, steps):
    count = lax.axis_size(axis)
    initial, last = (max(0, -steps), min(count, count - steps))
    return lax.ppermute(value, axis, [(source, source + steps) for source in range(initial, last)])


def extended(cells, sides, width):
    for axis, dim in sides:
        count = lax.axis_size(axis)
        ends = count - 1
        head = lax.slice_in_dim(cells, 0, width, axis=dim)
        tail = lax.slice_in_dim(cells, cells.shape[dim] - width, cells.shape[dim], axis=dim)
        cells = jnp.concatenate(
            [
                lax.ppermute(tail, axis, [(i, (i + 1) % count) for i in range(ends)]),
                cells,
                lax.ppermute(head, axis, [((i + 1) % count, i) for i in range(ends)]),
            ],
            axis=dim,
        )
    return cells


def beside_all(ext, fill):
    wide = jnp.pad(ext, ((0, 0), (0, 0), (1, 1)), constant_values=fill)
    return [
        wide[1:-1, 1:-1, 2:],
        wide[1:-1, 1:-1, :-2],
        wide[1:-1, 2:, 1:-1],
        wide[1:-1, :-2, 1:-1],
        wide[2:, 1:-1, 1:-1],
        wide[:-2, 1:-1, 1:-1],
    ]


def bit_of(bits, number):
    return bits // 2**number % 2


def strength(couplings, rowmax, others):
    bits = jnp.zeros(rowmax.shape, jnp.int32)
    scale = jnp.ones(rowmax.shape, jnp.float32)
    for direction in range(6):
        cost = couplings[direction]
        depends = ((cost > 0) & (2.0 * cost >= rowmax)).astype(jnp.int32)
        feeds = ((cost > 0) & (2.0 * cost >= others[direction])).astype(jnp.int32)
        bits = bits + depends * 2**direction + feeds * 2 ** (direction + 6)
        scale = scale * jnp.where(feeds == 1, 2.0, 1.0).astype(jnp.float32)
    return (bits, scale)


def select(packed_ext, bits):
    center = packed_ext[1:-1, 1:-1]
    values = beside_all(packed_ext, -3.0)
    nearest = jnp.full(center.shape, -3.0, center.dtype)
    for direction in range(6):
        linked = bit_of(bits, direction) + bit_of(bits, direction + 6) > 0
        nearest = jnp.maximum(nearest, jnp.where(linked, values[direction], -3.0))
    return ((center >= 0) & (center > nearest)).astype(jnp.int32)


def finer(coarse_ext, bits):
    values = beside_all(coarse_ext, 0)
    hit = jnp.zeros(bits.shape, jnp.int32)
    for direction in range(6):
        hit = hit + bit_of(bits, direction) * values[direction]
    return hit


def per_device(ranks, seeds, flags):
    depth, rows, width = ranks.shape
    zpos = lax.axis_index("gz") * depth + jnp.arange(depth, dtype=jnp.int32)[:, None, None]
    ypos = lax.axis_index("gy") * rows + jnp.arange(rows, dtype=jnp.int32)[None, :, None]
    xpos = jnp.arange(width, dtype=jnp.int32)[None, None, :]
    total_z = depth * lax.axis_size("gz")
    total_y = rows * lax.axis_size("gy")
    zero = jnp.zeros((), jnp.float32)
    c0 = jnp.where(xpos < width - 1, seeds[0], zero)
    c2 = jnp.where(ypos < total_y - 1, seeds[1], zero)
    c4 = jnp.where(zpos < total_z - 1, seeds[2], zero)
    c1 = jnp.pad(c0[:, :, :-1], ((0, 0), (0, 0), (1, 0)))
    below_row = passed_along(c2[:, -1:], "gy", 1)
    c3 = jnp.concatenate([below_row, c2[:, :-1]], axis=1)
    below_plane = passed_along(c4[-1:], "gz", 1)
    c5 = jnp.concatenate([below_plane, c4[:-1]], axis=0)
    couplings = [c0, c1, c2, c3, c4, c5]
    rowmax = c0
    for item in couplings[1:]:
        rowmax = jnp.maximum(rowmax, item)
    rowmax_ext = extended(rowmax, (("gz", 0), ("gy", 1)), 1)
    others = beside_all(rowmax_ext, 0.0)
    bits, scale = strength(couplings, rowmax, others)
    measure = ranks * scale
    bits_inner = extended(bits, (("gz", 0), ("gy", 1)), 1)
    state = flags
    totals = []
    for step in range(ROUNDS):
        packed = jnp.where(state == 0, measure, jnp.where(state == 2, -2.0, -1.0))
        packed_wide = extended(packed, (("gz", 0), ("gy", 1)), 2)
        coarse_ext = select(packed_wide, bits_inner)
        coarse = coarse_ext[1:-1, 1:-1]
        hit = finer(coarse_ext, bits)
        state = jnp.where(coarse == 1, 2, jnp.where((state == 0) & (hit > 0), 1, state))
        local = jnp.sum((state == 0).astype(jnp.int32))
        totals.append(lax.psum(local, ("gz", "gy")))
    undecided = jnp.stack(totals)
    return (state, undecided)


def solution(mesh):
    return jax.shard_map(
        per_device,
        mesh=mesh,
        in_specs=(P("gz", "gy", None), P(None, "gz", "gy", None), P("gz", "gy", None)),
        out_specs=(P("gz", "gy", None), P()),
        check_vma=False,
    )
```

profile of v0, /device:TPU:0, one launch (start us, length us, event | category | flops | bytes accessed | tf_op | source)
XLA Modules:
  0.0 158.5 jit_solution(13082738382440049864)
XLA Ops:
  1.9 4.9 %collective-permute-start.1 = (f32[1,16,512]{2,1,0:T(8,128)S(1)}, f32[1,16,512]{2,1,0:T(8,128)S(1)}, u32[]{:S(2)}, u32[]{:S(2)}) collective-permute-start(f32[1,16,512]{2,1,0:T(8,128)S(1)} %slice.347), channel_id=1, source_target_pairs={{0,4},{4,8},{8,12},{12,16},{16,20},{20,24},{24,28},{1,5},{5,9},{9,... | collective-permute-start | bytes 98312 | tf_op jit(solution)/shard_map/ppermute | solution.py:12
  10.6 4.5 %collective-permute-start.2 = (f32[1,16,512]{2,1,0:T(8,128)S(1)}, f32[1,16,512]{2,1,0:T(8,128)S(1)}, u32[]{:S(2)}, u32[]{:S(2)}) collective-permute-start(f32[1,16,512]{2,1,0:T(8,128)S(1)} %get-tuple-element.38), channel_id=1, source_target_pairs={{0,4},{4,8},{8,12},{12,16},{16,20},{20,24},{24,28},{1,5},{5,9},{9,... | collective-permute-start | bytes 98312 | tf_op jit(solution)/shard_map/ppermute | solution.py:23
  18.1 3.5 %collective-permute-start.4 = (f32[10,1,512]{2,1,0:T(1,128)S(1)}, f32[10,1,512]{2,1,0:T(1,128)S(1)}, u32[]{:S(2)}, u32[]{:S(2)}) collective-permute-start(f32[10,1,512]{2,1,0:T(1,128)S(1)} %get-tuple-element.28), channel_id=1, source_target_pairs={{0,1},{1,2},{2,3},{4,5},{5,6},{6,7},{8,9},{9,10},{10,11},{12,13},{... | collective-permute-start | bytes 61448 | tf_op jit(solution)/shard_map/ppermute | solution.py:23
  24.3 4.4 %collective-permute-start.6 = (f32[2,16,512]{2,1,0:T(8,128)S(1)}, f32[2,16,512]{2,1,0:T(8,128)S(1)}, u32[]{:S(2)}, u32[]{:S(2)}) collective-permute-start(f32[2,16,512]{2,1,0:T(8,128)S(1)} %get-tuple-element.35), channel_id=1, source_target_pairs={{0,4},{4,8},{8,12},{12,16},{16,20},{20,24},{24,28},{1,5},{5,9},{9,... | collective-permute-start | bytes 196616 | tf_op jit(solution)/shard_map/ppermute | solution.py:23
  29.9 5.5 %collective-permute-start.10 = (s32[1,16,512]{2,1,0:T(8,128)S(1)}, s32[1,16,512]{2,1,0:T(8,128)S(1)}, u32[]{:S(2)}, u32[]{:S(2)}) collective-permute-start(s32[1,16,512]{2,1,0:T(8,128)S(1)} %get-tuple-element.33), channel_id=1, source_target_pairs={{0,4},{4,8},{8,12},{12,16},{16,20},{20,24},{24,28},{1,5},{5,9},{9,... | collective-permute-start | bytes 98312 | tf_op jit(solution)/shard_map/ppermute | solution.py:23
  36.8 5.1 %collective-permute-start.8 = (f32[12,2,512]{2,1,0:T(2,128)S(1)}, f32[12,2,512]{2,1,0:T(2,128)S(1)}, u32[]{:S(2)}, u32[]{:S(2)}) collective-permute-start(f32[12,2,512]{2,1,0:T(2,128)S(1)} %get-tuple-element.23), channel_id=1, source_target_pairs={{0,1},{1,2},{2,3},{4,5},{5,6},{6,7},{8,9},{9,10},{10,11},{12,13},{... | collective-permute-start | bytes 147464 | tf_op jit(solution)/shard_map/ppermute | solution.py:23
  43.3 5.4 %collective-permute-start.12 = (s32[10,1,512]{2,1,0:T(1,128)S(1)}, s32[10,1,512]{2,1,0:T(1,128)S(1)}, u32[]{:S(2)}, u32[]{:S(2)}) collective-permute-start(s32[10,1,512]{2,1,0:T(1,128)S(1)} %get-tuple-element.25), channel_id=1, source_target_pairs={{0,1},{1,2},{2,3},{4,5},{5,6},{6,7},{8,9},{9,10},{10,11},{12,13},{... | collective-permute-start | bytes 61448 | tf_op jit(solution)/shard_map/ppermute | solution.py:23
  50.1 2.9 %collective-permute-done.13 = s32[10,1,512]{2,1,0:T(1,128)S(1)} collective-permute-done((s32[10,1,512]{2,1,0:T(1,128)S(1)}, s32[10,1,512]{2,1,0:T(1,128)S(1)}, u32[]{:S(2)}, u32[]{:S(2)}) %collective-permute-start.13) | collective-permute-done | bytes 20512 | tf_op jit(solution)/shard_map/ppermute | solution.py:25
  53.0 5.5 %and_convert_fusion.2 = s32[10,18,512]{2,1,0:T(8,128)S(1)} fusion(f32[12,20,512]{2,1,0:T(8,128)S(1)} %pad_maximum_fusion, f32[2,16,512]{2,1,0:T(8,128)S(1)} %collective-permute-done.7, f32[8,16,512]{2,1,0:T(8,128)S(1)} %get-tuple-element.14, f32[2,16,512]{2,1,0:T(8,128)S(1)} %collective-permute-done.6, f32[12,2,512]{2,1,0:T(2,128)S(1)} %collective-permute-done.8, ...), kind=kLoop, calls=%fused_computation.194 | loop fusion | flops 25620480 | bytes 3293184 | tf_op jit(solution)/shard_map/convert_element_type | solution.py:67
  58.5 2.0 %convert_reduce_fusion.2 = (s32[]{:T(128)}, s32[8,16,512]{2,1,0:T(8,128)S(1)}) fusion(s32[8,16,512]{2,1,0:T(8,128)S(1)} %copy-done, s32[10,18,512]{2,1,0:T(8,128)S(1)} %and_convert_fusion.2, s32[8,16,512]{2,1,0:T(8,128)S(1)} %get-tuple-element.11), kind=kLoop, calls=%fused_computation.297 | loop fusion | flops 8781823 | bytes 2588676 | tf_op jit(solution)/shard_map/reduce_sum | solution.py:112
  60.6 5.5 %collective-permute-start.14 = (f32[2,16,512]{2,1,0:T(8,128)S(1)}, f32[2,16,512]{2,1,0:T(8,128)S(1)}, u32[]{:S(2)}, u32[]{:S(2)}) collective-permute-start(f32[2,16,512]{2,1,0:T(8,128)S(1)} %get-tuple-element.31), channel_id=1, source_target_pairs={{0,4},{4,8},{8,12},{12,16},{16,20},{20,24},{24,28},{1,5},{5,9},{9,... | collective-permute-start | bytes 196616 | tf_op jit(solution)/shard_map/ppermute | solution.py:23
  67.9 5.2 %collective-permute-done.15 = f32[2,16,512]{2,1,0:T(8,128)S(1)} collective-permute-done((f32[2,16,512]{2,1,0:T(8,128)S(1)}, f32[2,16,512]{2,1,0:T(8,128)S(1)}, u32[]{:S(2)}, u32[]{:S(2)}) %collective-permute-start.15) | collective-permute-done | bytes 65568 | tf_op jit(solution)/shard_map/ppermute | solution.py:25
  73.1 3.3 %collective-permute-start.16 = (f32[12,2,512]{2,1,0:T(2,128)S(1)}, f32[12,2,512]{2,1,0:T(2,128)S(1)}, u32[]{:S(2)}, u32[]{:S(2)}) collective-permute-start(f32[12,2,512]{2,1,0:T(2,128)S(1)} %get-tuple-element.21), channel_id=1, source_target_pairs={{0,1},{1,2},{2,3},{4,5},{5,6},{6,7},{8,9},{9,10},{10,11},{12,13},{... | collective-permute-start | bytes 147464 | tf_op jit(solution)/shard_map/ppermute | solution.py:23
  77.9 2.3 %collective-permute-done.17 = f32[12,2,512]{2,1,0:T(2,128)S(1)} collective-permute-done((f32[12,2,512]{2,1,0:T(2,128)S(1)}, f32[12,2,512]{2,1,0:T(2,128)S(1)}, u32[]{:S(2)}, u32[]{:S(2)}) %collective-permute-start.17) | collective-permute-done | bytes 49184 | tf_op jit(solution)/shard_map/ppermute | solution.py:25
  80.3 5.5 %and_convert_fusion.1 = s32[10,18,512]{2,1,0:T(8,128)S(1)} fusion(f32[12,20,512]{2,1,0:T(8,128)S(1)} %pad_maximum_fusion.1, f32[2,16,512]{2,1,0:T(8,128)S(1)} %collective-permute-done.15, f32[8,16,512]{2,1,0:T(8,128)S(1)} %select_select_fusion.3, f32[2,16,512]{2,1,0:T(8,128)S(1)} %collective-permute-done.14, f32[12,2,512]{2,1,0:T(2,128)S(1)} %collective-permute-done.16, ...), kind=kLoop, calls=%fused_computation.193 | loop fusion | flops 25620480 | bytes 3293184 | tf_op jit(solution)/shard_map/convert_element_type | solution.py:67
  85.9 2.0 %convert_reduce_fusion.1 = (s32[]{:T(128)}, s32[8,16,512]{2,1,0:T(8,128)S(1)}) fusion(s32[8,16,512]{2,1,0:T(8,128)S(1)} %get-tuple-element.6, s32[10,18,512]{2,1,0:T(8,128)S(1)} %and_convert_fusion.1, s32[8,16,512]{2,1,0:T(8,128)S(1)} %get-tuple-element.11), kind=kLoop, calls=%fused_computation.296 | loop fusion | flops 8781823 | bytes 2588676 | tf_op jit(solution)/shard_map/reduce_sum | solution.py:112
  87.9 4.8 %collective-permute-start.18 = (f32[2,16,512]{2,1,0:T(8,128)S(1)}, f32[2,16,512]{2,1,0:T(8,128)S(1)}, u32[]{:S(2)}, u32[]{:S(2)}) collective-permute-start(f32[2,16,512]{2,1,0:T(8,128)S(1)} %get-tuple-element.29), channel_id=1, source_target_pairs={{0,4},{4,8},{8,12},{12,16},{16,20},{20,24},{24,28},{1,5},{5,9},{9,... | collective-permute-start | bytes 196616 | tf_op jit(solution)/shard_map/ppermute | solution.py:23
  94.7 4.3 %collective-permute-done.19 = f32[2,16,512]{2,1,0:T(8,128)S(1)} collective-permute-done((f32[2,16,512]{2,1,0:T(8,128)S(1)}, f32[2,16,512]{2,1,0:T(8,128)S(1)}, u32[]{:S(2)}, u32[]{:S(2)}) %collective-permute-start.19) | collective-permute-done | bytes 65568 | tf_op jit(solution)/shard_map/ppermute | solution.py:25
  99.0 3.3 %collective-permute-start.20 = (f32[12,2,512]{2,1,0:T(2,128)S(1)}, f32[12,2,512]{2,1,0:T(2,128)S(1)}, u32[]{:S(2)}, u32[]{:S(2)}) collective-permute-start(f32[12,2,512]{2,1,0:T(2,128)S(1)} %get-tuple-element.19), channel_id=1, source_target_pairs={{0,1},{1,2},{2,3},{4,5},{5,6},{6,7},{8,9},{9,10},{10,11},{12,13},{... | collective-permute-start | bytes 147464 | tf_op jit(solution)/shard_map/ppermute | solution.py:23
  103.6 2.7 %collective-permute-done.21 = f32[12,2,512]{2,1,0:T(2,128)S(1)} collective-permute-done((f32[12,2,512]{2,1,0:T(2,128)S(1)}, f32[12,2,512]{2,1,0:T(2,128)S(1)}, u32[]{:S(2)}, u32[]{:S(2)}) %collective-permute-start.21) | collective-permute-done | bytes 49184 | tf_op jit(solution)/shard_map/ppermute | solution.py:25
  106.4 5.5 %and_convert_fusion = s32[10,18,512]{2,1,0:T(8,128)S(1)} fusion(f32[12,20,512]{2,1,0:T(8,128)S(1)} %pad_maximum_fusion.2, f32[2,16,512]{2,1,0:T(8,128)S(1)} %collective-permute-done.19, f32[8,16,512]{2,1,0:T(8,128)S(1)} %select_select_fusion.1, f32[2,16,512]{2,1,0:T(8,128)S(1)} %collective-permute-done.18, f32[12,2,512]{2,1,0:T(2,128)S(1)} %collective-permute-done.20, ...), kind=kLoop, calls=%fused_computation.192 | loop fusion | flops 25620480 | bytes 3293184 | tf_op jit(solution)/shard_map/convert_element_type | solution.py:67
  111.9 2.7 %convert_reduce_fusion = (s32[]{:T(128)}, s32[8,16,512]{2,1,0:T(8,128)}) fusion(s32[8,16,512]{2,1,0:T(8,128)S(1)} %get-tuple-element.8, s32[10,18,512]{2,1,0:T(8,128)S(1)} %and_convert_fusion, s32[8,16,512]{2,1,0:T(8,128)S(1)} %get-tuple-element.11), kind=kLoop, calls=%fused_computation.295 | loop fusion | flops 8781823 | bytes 2588676 | tf_op jit(solution)/shard_map/reduce_sum | solution.py:112
  114.6 41.4 %all-reduce.8 = (s32[1]{0:T(128)}, s32[1]{0:T(128)}, s32[1]{0:T(128)}) all-reduce(s32[1]{0:T(128)} %bitcast.5, s32[1]{0:T(128)} %bitcast.4, s32[1]{0:T(128)} %bitcast.3), channel_id=1, replica_groups=mesh['gz'=8,'gy'=4] {'gz','gy'}, use_global_device_ids=true, to_apply=%region_5.6 | all-reduce | flops 3 | bytes 24 | tf_op jit(solution)/shard_map/psum | solution.py:113
  156.0 2.5 %pad_add_fusion.4 = s32[3]{0:T(128)} fusion(s32[1]{0:T(128)} %get-tuple-element.2, s32[1]{0:T(128)} %get-tuple-element.3, s32[1]{0:T(128)} %get-tuple-element.4), kind=kLoop, calls=%fused_computation.350 | loop fusion | flops 6 | bytes 24 | tf_op jit(solution)/shard_map/stack | solution.py:114
  (58 shorter events, 22.8 us)
Async XLA Ops:
  1.9 7.2 %collective-permute-start.1 = (f32[1,16,512]{2,1,0:T(8,128)S(1)}, f32[1,16,512]{2,1,0:T(8,128)S(1)}, u32[]{:S(2)}, u32[]{:S(2)}) collective-permute-start(f32[1,16,512]{2,1,0:T(8,128)S(1)} %slice.347), channel_id=1, source_target_pairs={{0,4},{4,8},{8,12},{12,16},{16,20},{20,24},{24,28},{1,5},{5,9},{9,... | collective-permute-start | bytes 98312 | tf_op jit(solution)/shard_map/ppermute | solution.py:12
  6.8 2.3 %collective-permute-start = (f32[8,1,512]{2,1,0:T(1,128)S(1)}, f32[8,1,512]{2,1,0:T(1,128)S(1)}, u32[]{:S(2)}, u32[]{:S(2)}) collective-permute-start(f32[8,1,512]{2,1,0:T(1,128)S(1)} %slice.345), channel_id=1, source_target_pairs={{0,1},{1,2},{2,3},{4,5},{5,6},{6,7},{8,9},{9,10},{10,11},{12,13},{... | collective-permute-start | bytes 49160 | tf_op jit(solution)/shard_map/ppermute | solution.py:12
  9.3 5.9 %collective-permute-start.3 = (f32[1,16,512]{2,1,0:T(8,128)S(1)}, f32[1,16,512]{2,1,0:T(8,128)S(1)}, u32[]{:S(2)}, u32[]{:S(2)}) collective-permute-start(f32[1,16,512]{2,1,0:T(8,128)S(1)} %get-tuple-element.37), channel_id=1, source_target_pairs={{4,0},{8,4},{12,8},{16,12},{20,16},{24,20},{28,24},{5,1},{9,5},{13... | collective-permute-start | bytes 98312 | tf_op jit(solution)/shard_map/ppermute | solution.py:25
  10.6 6.1 %collective-permute-start.2 = (f32[1,16,512]{2,1,0:T(8,128)S(1)}, f32[1,16,512]{2,1,0:T(8,128)S(1)}, u32[]{:S(2)}, u32[]{:S(2)}) collective-permute-start(f32[1,16,512]{2,1,0:T(8,128)S(1)} %get-tuple-element.38), channel_id=1, source_target_pairs={{0,4},{4,8},{8,12},{12,16},{16,20},{20,24},{24,28},{1,5},{5,9},{9,... | collective-permute-start | bytes 98312 | tf_op jit(solution)/shard_map/ppermute | solution.py:23
  16.8 4.8 %collective-permute-start.5 = (f32[10,1,512]{2,1,0:T(1,128)S(1)}, f32[10,1,512]{2,1,0:T(1,128)S(1)}, u32[]{:S(2)}, u32[]{:S(2)}) collective-permute-start(f32[10,1,512]{2,1,0:T(1,128)S(1)} %get-tuple-element.27), channel_id=1, source_target_pairs={{1,0},{2,1},{3,2},{5,4},{6,5},{7,6},{9,8},{10,9},{11,10},{13,12},{... | collective-permute-start | bytes 61448 | tf_op jit(solution)/shard_map/ppermute | solution.py:25
  18.1 4.3 %collective-permute-start.4 = (f32[10,1,512]{2,1,0:T(1,128)S(1)}, f32[10,1,512]{2,1,0:T(1,128)S(1)}, u32[]{:S(2)}, u32[]{:S(2)}) collective-permute-start(f32[10,1,512]{2,1,0:T(1,128)S(1)} %get-tuple-element.28), channel_id=1, source_target_pairs={{0,1},{1,2},{2,3},{4,5},{5,6},{6,7},{8,9},{9,10},{10,11},{12,13},{... | collective-permute-start | bytes 61448 | tf_op jit(solution)/shard_map/ppermute | solution.py:23
  22.8 1.0 copy-start
  22.8 1.0 copy-start.1
  24.3 12.4 %collective-permute-start.6 = (f32[2,16,512]{2,1,0:T(8,128)S(1)}, f32[2,16,512]{2,1,0:T(8,128)S(1)}, u32[]{:S(2)}, u32[]{:S(2)}) collective-permute-start(f32[2,16,512]{2,1,0:T(8,128)S(1)} %get-tuple-element.35), channel_id=1, source_target_pairs={{0,4},{4,8},{8,12},{12,16},{16,20},{20,24},{24,28},{1,5},{5,9},{9,... | collective-permute-start | bytes 196616 | tf_op jit(solution)/shard_map/ppermute | solution.py:23
  28.6 8.1 %collective-permute-start.7 = (f32[2,16,512]{2,1,0:T(8,128)S(1)}, f32[2,16,512]{2,1,0:T(8,128)S(1)}, u32[]{:S(2)}, u32[]{:S(2)}) collective-permute-start(f32[2,16,512]{2,1,0:T(8,128)S(1)} %get-tuple-element.36), channel_id=1, source_target_pairs={{4,0},{8,4},{12,8},{16,12},{20,16},{24,20},{28,24},{5,1},{9,5},{13... | collective-permute-start | bytes 196616 | tf_op jit(solution)/shard_map/ppermute | solution.py:25
  29.9 13.3 %collective-permute-start.10 = (s32[1,16,512]{2,1,0:T(8,128)S(1)}, s32[1,16,512]{2,1,0:T(8,128)S(1)}, u32[]{:S(2)}, u32[]{:S(2)}) collective-permute-start(s32[1,16,512]{2,1,0:T(8,128)S(1)} %get-tuple-element.33), channel_id=1, source_target_pairs={{0,4},{4,8},{8,12},{12,16},{16,20},{20,24},{24,28},{1,5},{5,9},{9,... | collective-permute-start | bytes 98312 | tf_op jit(solution)/shard_map/ppermute | solution.py:23
  35.4 7.8 %collective-permute-start.11 = (s32[1,16,512]{2,1,0:T(8,128)S(1)}, s32[1,16,512]{2,1,0:T(8,128)S(1)}, u32[]{:S(2)}, u32[]{:S(2)}) collective-permute-start(s32[1,16,512]{2,1,0:T(8,128)S(1)} %get-tuple-element.34), channel_id=1, source_target_pairs={{4,0},{8,4},{12,8},{16,12},{20,16},{24,20},{28,24},{5,1},{9,5},{13... | collective-permute-start | bytes 98312 | tf_op jit(solution)/shard_map/ppermute | solution.py:25
  36.8 13.2 %collective-permute-start.8 = (f32[12,2,512]{2,1,0:T(2,128)S(1)}, f32[12,2,512]{2,1,0:T(2,128)S(1)}, u32[]{:S(2)}, u32[]{:S(2)}) collective-permute-start(f32[12,2,512]{2,1,0:T(2,128)S(1)} %get-tuple-element.23), channel_id=1, source_target_pairs={{0,1},{1,2},{2,3},{4,5},{5,6},{6,7},{8,9},{9,10},{10,11},{12,13},{... | collective-permute-start | bytes 147464 | tf_op jit(solution)/shard_map/ppermute | solution.py:23
  41.9 8.1 %collective-permute-start.9 = (f32[12,2,512]{2,1,0:T(2,128)S(1)}, f32[12,2,512]{2,1,0:T(2,128)S(1)}, u32[]{:S(2)}, u32[]{:S(2)}) collective-permute-start(f32[12,2,512]{2,1,0:T(2,128)S(1)} %get-tuple-element.24), channel_id=1, source_target_pairs={{1,0},{2,1},{3,2},{5,4},{6,5},{7,6},{9,8},{10,9},{11,10},{13,12},{... | collective-permute-start | bytes 147464 | tf_op jit(solution)/shard_map/ppermute | solution.py:25
  43.3 6.8 %collective-permute-start.12 = (s32[10,1,512]{2,1,0:T(1,128)S(1)}, s32[10,1,512]{2,1,0:T(1,128)S(1)}, u32[]{:S(2)}, u32[]{:S(2)}) collective-permute-start(s32[10,1,512]{2,1,0:T(1,128)S(1)} %get-tuple-element.25), channel_id=1, source_target_pairs={{0,1},{1,2},{2,3},{4,5},{5,6},{6,7},{8,9},{9,10},{10,11},{12,13},{... | collective-permute-start | bytes 61448 | tf_op jit(solution)/shard_map/ppermute | solution.py:23
  48.7 4.3 %collective-permute-start.13 = (s32[10,1,512]{2,1,0:T(1,128)S(1)}, s32[10,1,512]{2,1,0:T(1,128)S(1)}, u32[]{:S(2)}, u32[]{:S(2)}) collective-permute-start(s32[10,1,512]{2,1,0:T(1,128)S(1)} %get-tuple-element.26), channel_id=1, source_target_pairs={{1,0},{2,1},{3,2},{5,4},{6,5},{7,6},{9,8},{10,9},{11,10},{13,12},{... | collective-permute-start | bytes 61448 | tf_op jit(solution)/shard_map/ppermute | solution.py:25
  60.6 7.3 %collective-permute-start.14 = (f32[2,16,512]{2,1,0:T(8,128)S(1)}, f32[2,16,512]{2,1,0:T(8,128)S(1)}, u32[]{:S(2)}, u32[]{:S(2)}) collective-permute-start(f32[2,16,512]{2,1,0:T(8,128)S(1)} %get-tuple-element.31), channel_id=1, source_target_pairs={{0,4},{4,8},{8,12},{12,16},{16,20},{20,24},{24,28},{1,5},{5,9},{9,... | collective-permute-start | bytes 196616 | tf_op jit(solution)/shard_map/ppermute | solution.py:23
  66.0 7.1 %collective-permute-start.15 = (f32[2,16,512]{2,1,0:T(8,128)S(1)}, f32[2,16,512]{2,1,0:T(8,128)S(1)}, u32[]{:S(2)}, u32[]{:S(2)}) collective-permute-start(f32[2,16,512]{2,1,0:T(8,128)S(1)} %get-tuple-element.32), channel_id=1, source_target_pairs={{4,0},{8,4},{12,8},{16,12},{20,16},{24,20},{28,24},{5,1},{9,5},{13... | collective-permute-start | bytes 196616 | tf_op jit(solution)/shard_map/ppermute | solution.py:25
  73.1 4.8 %collective-permute-start.16 = (f32[12,2,512]{2,1,0:T(2,128)S(1)}, f32[12,2,512]{2,1,0:T(2,128)S(1)}, u32[]{:S(2)}, u32[]{:S(2)}) collective-permute-start(f32[12,2,512]{2,1,0:T(2,128)S(1)} %get-tuple-element.21), channel_id=1, source_target_pairs={{0,1},{1,2},{2,3},{4,5},{5,6},{6,7},{8,9},{9,10},{10,11},{12,13},{... | collective-permute-start | bytes 147464 | tf_op jit(solution)/shard_map/ppermute | solution.py:23
  76.4 3.8 %collective-permute-start.17 = (f32[12,2,512]{2,1,0:T(2,128)S(1)}, f32[12,2,512]{2,1,0:T(2,128)S(1)}, u32[]{:S(2)}, u32[]{:S(2)}) collective-permute-start(f32[12,2,512]{2,1,0:T(2,128)S(1)} %get-tuple-element.22), channel_id=1, source_target_pairs={{1,0},{2,1},{3,2},{5,4},{6,5},{7,6},{9,8},{10,9},{11,10},{13,12},{... | collective-permute-start | bytes 147464 | tf_op jit(solution)/shard_map/ppermute | solution.py:25
  87.9 6.7 %collective-permute-start.18 = (f32[2,16,512]{2,1,0:T(8,128)S(1)}, f32[2,16,512]{2,1,0:T(8,128)S(1)}, u32[]{:S(2)}, u32[]{:S(2)}) collective-permute-start(f32[2,16,512]{2,1,0:T(8,128)S(1)} %get-tuple-element.29), channel_id=1, source_target_pairs={{0,4},{4,8},{8,12},{12,16},{16,20},{20,24},{24,28},{1,5},{5,9},{9,... | collective-permute-start | bytes 196616 | tf_op jit(solution)/shard_map/ppermute | solution.py:23
  92.8 6.2 %collective-permute-start.19 = (f32[2,16,512]{2,1,0:T(8,128)S(1)}, f32[2,16,512]{2,1,0:T(8,128)S(1)}, u32[]{:S(2)}, u32[]{:S(2)}) collective-permute-start(f32[2,16,512]{2,1,0:T(8,128)S(1)} %get-tuple-element.30), channel_id=1, source_target_pairs={{4,0},{8,4},{12,8},{16,12},{20,16},{24,20},{28,24},{5,1},{9,5},{13... | collective-permute-start | bytes 196616 | tf_op jit(solution)/shard_map/ppermute | solution.py:25
  99.0 4.6 %collective-permute-start.20 = (f32[12,2,512]{2,1,0:T(2,128)S(1)}, f32[12,2,512]{2,1,0:T(2,128)S(1)}, u32[]{:S(2)}, u32[]{:S(2)}) collective-permute-start(f32[12,2,512]{2,1,0:T(2,128)S(1)} %get-tuple-element.19), channel_id=1, source_target_pairs={{0,1},{1,2},{2,3},{4,5},{5,6},{6,7},{8,9},{9,10},{10,11},{12,13},{... | collective-permute-start | bytes 147464 | tf_op jit(solution)/shard_map/ppermute | solution.py:23
  102.2 4.0 %collective-permute-start.21 = (f32[12,2,512]{2,1,0:T(2,128)S(1)}, f32[12,2,512]{2,1,0:T(2,128)S(1)}, u32[]{:S(2)}, u32[]{:S(2)}) collective-permute-start(f32[12,2,512]{2,1,0:T(2,128)S(1)} %get-tuple-element.20), channel_id=1, source_target_pairs={{1,0},{2,1},{3,2},{5,4},{6,5},{7,6},{9,8},{10,9},{11,10},{13,12},{... | collective-permute-start | bytes 147464 | tf_op jit(solution)/shard_map/ppermute | solution.py:25
where the time goes:
time: 159 us; the launch traced here: 158 us
  starting transfers between devices  64.6 us (41%)
  blocking collectives  41.4 us (26%)
  other arithmetic  29.5 us (19%)
  waiting for transfers between devices  21.8 us (14%)
    ppermute x10, starting transfers between devices, extended(): lax.ppermute(tail, axis, [(i, (i + 1) % count) for i in range(ends)])  45.2 us
    psum x1, blocking collectives, per_device(): totals.append(lax.psum(local, ('gz', 'gy')))  41.4 us
    ppermute x10, waiting for transfers between devices, extended(): lax.ppermute(head, axis, [((i + 1) % count, i) for i in range(ends)])  17.4 us
    convert_element_type x3, other arithmetic, select(): return ((center >= 0) & (center > nearest)).astype(jnp.int32)  16.5 us
    ppermute x10, starting transfers between devices, extended(): lax.ppermute(head, axis, [((i + 1) % count, i) for i in range(ends)])  13.1 us
    reduce_sum x3, other arithmetic, per_device(): local = jnp.sum((state == 0).astype(jnp.int32))  6.73 us
    ppermute x2, starting transfers between devices, passed_along(): lax.ppermute(value, axis, [(source, source + steps) for source in range(i...  6.33 us
    ppermute x10, waiting for transfers between devices, extended(): lax.ppermute(tail, axis, [(i, (i + 1) % count) for i in range(ends)])  3.57 us
  transfers between devices with their start and end apart: 22, of which 10 were waited for; matrix products, arithmetic and copies ran while one was open for 0% of the time, Pallas kernels for 0%

commit v1 on v0

v1 whole, which is shorter than its diff:
```python
import functools

import jax
import jax.numpy as jnp
from jax import lax
from jax.experimental import pallas as pl
from jax.experimental.pallas import tpu as pltpu
from jax.sharding import PartitionSpec as P

ROUNDS = 3
H = 2 * ROUNDS
T = 8
BIG = 3.0e38


def whole():
    return pl.BlockSpec(memory_space=pltpu.VMEM)


def pad8(n):
    return -(-n // 8) * 8


def doubled(s):
    return jnp.where(s > 0, 2.0 * s, -1.0)


def has_neighbour(axis):
    i = lax.axis_index(axis)
    return i > 0, i < lax.axis_size(axis) - 1


def strength_kernel(seeds, ranks, flags, sz_low, sy_low, up, dn, e_out, r_out, top_row, rm):
    depth, rows, width = ranks.shape
    zlo, zhi = has_neighbour("gz")
    ylo, yhi = has_neighbour("gy")
    shape = (rows, width)
    row = lax.broadcasted_iota(jnp.int32, shape, 0)
    col = lax.broadcasted_iota(jnp.int32, shape, 1)
    x_in = col < width - 1
    y_in = (row < rows - 1) | yhi
    y_first = row == 0
    y_last = row == rows - 1

    def sx_of(z):
        return jnp.where(x_in, seeds[0, z], 0.0)

    def sy_of(z):
        return jnp.where(y_in, seeds[1, z], 0.0)

    def sz_of(z):
        if z < 0:
            return jnp.where(zlo, sz_low[...], 0.0)
        s = seeds[2, z]
        return jnp.where(zhi, s, 0.0) if z == depth - 1 else s

    for z in range(depth):
        sx, sy, sz = sx_of(z), sy_of(z), sz_of(z)
        below = jnp.where(ylo, sy_low[pl.ds(z, 1), :], 0.0)
        sy_prev = jnp.where(y_first, below, pltpu.roll(sy, 1, 0))
        r = jnp.maximum(jnp.maximum(sx, pltpu.roll(sx, 1, 1)), jnp.maximum(sy, sy_prev))
        rm[z] = jnp.maximum(r, jnp.maximum(sz, sz_of(z - 1)))
    for z in range(depth):
        r = rm[z]
        tx, ty, tz = doubled(sx_of(z)), doubled(sy_of(z)), doubled(sz_of(z))
        e = jnp.where(tx >= r, 1, 0) + jnp.where(tx >= pltpu.roll(r, width - 1, 1), 2, 0)
        e += jnp.where(ty >= r, 4, 0)
        e += jnp.where((ty >= pltpu.roll(r, rows - 1, 0)) & ~y_last, 8, 0)
        e += jnp.where(tz >= r, 16, 0)
        if z < depth - 1:
            e += jnp.where(tz >= rm[z + 1], 32, 0)
        f = flags[z]
        p = jnp.where(f == 0, ranks[z], jnp.where(f == 2, -2.0, -1.0))
        ef = e.astype(jnp.float32)
        e_out[z] = e
        r_out[z] = p
        top_row[pl.ds(z, 1), :] = r[0:1]
        sl = sy_of(z)[rows - 1 : rows]
        k = depth - z
        if k <= H + 1:
            up[pl.ds((k - 1) * rows, rows), :] = ef
        base = (H + 1) * rows
        if k <= H:
            up[pl.ds(base + (k - 1) * rows, rows), :] = p
            up[pl.ds(base + H * rows + k - 1, 1), :] = sl
            up[pl.ds(base + H * rows + H + k - 1, 1), :] = r[0:1]
        if z == 0:
            dn[pl.ds(H * rows, rows), :] = r
        if z < H:
            dn[pl.ds(z * rows, rows), :] = ef
            dn[pl.ds(base + z * rows, rows), :] = p
            dn[pl.ds(base + H * rows + z, 1), :] = sl
            dn[pl.ds(base + H * rows + H + z, 1), :] = r[0:1]


def planes_kernel(zb, za, e_own, p_own, top_row, sz_low, sz_top, sy_last, dn_own, yup, ydn, e_ext, p_ext, strips):
    depth, rows, width = p_own.shape
    zlo, zhi = has_neighbour("gz")
    _, yhi = has_neighbour("gy")
    planes = depth + 2 * H
    base = (H + 1) * rows
    tail = base + H * rows
    half = rows - T

    def put(z, e, p):
        i = z + H
        e_ext[i + 1] = e
        ef = e.astype(jnp.float32)
        yup[pl.ds(i * T, T), :] = ef[half:]
        ydn[pl.ds(i * T, T), :] = ef[:T]
        p_ext[i] = p
        yup[pl.ds((planes + i) * T, T), :] = p[half:]
        ydn[pl.ds((planes + i) * T, T), :] = p[:T]

    def strip(z, s, r):
        i = z + H
        s = jnp.where(yhi, s, 0.0)
        strips[pl.ds(i, 1), :] = s
        strips[pl.ds(pad8(planes) + i, 1), :] = r
        yup[pl.ds(2 * planes * T + i, 1), :] = s
        ydn[pl.ds(2 * planes * T + i, 1), :] = r

    def from_below(k):
        e = jnp.where(zlo, zb[pl.ds((k - 1) * rows, rows), :], 0.0).astype(jnp.int32)
        if k == 1:
            r0 = dn_own[pl.ds(H * rows, rows), :]
            e = e + jnp.where((doubled(sz_low[...]) >= r0) & zlo, 32, 0)
        return e

    e_ext[0] = from_below(H + 1)
    for k in range(H, 0, -1):
        put(-k, from_below(k), zb[pl.ds(base + (k - 1) * rows, rows), :])
        strip(-k, zb[pl.ds(tail + k - 1, 1), :], zb[pl.ds(tail + H + k - 1, 1), :])
    for z in range(depth):
        e = e_own[z]
        if z == depth - 1:
            e = e + jnp.where((doubled(sz_top[...]) >= za[pl.ds(H * rows, rows), :]) & zhi, 32, 0)
        put(z, e, p_own[z])
        strip(z, sy_last[pl.ds(z, 1), :], top_row[pl.ds(z, 1), :])
    for k in range(H):
        put(depth + k, za[pl.ds(k * rows, rows), :].astype(jnp.int32), za[pl.ds(base + k * rows, rows), :])
        strip(depth + k, za[pl.ds(tail + k, 1), :], za[pl.ds(tail + H + k, 1), :])


def rounds_kernel(yb, ya, e_ext, p_ext, strips, state_out, count_out, es, ps, ns, bs, caps):
    depth, rows, width = state_out.shape
    planes = depth + 2 * H
    ylo, _ = has_neighbour("gy")
    own = 2 * T
    chunks = range(T, own + rows + T, T)
    shape = (T, width)
    row = lax.broadcasted_iota(jnp.int32, shape, 0)

    es[0, pl.ds(own, rows), :] = e_ext[0]

    @pl.loop(0, planes)
    def _(i):
        at = pl.multiple_of(i * T, T)
        eb = jnp.where(ylo, yb[pl.ds(at, T), :], 0.0).astype(jnp.int32)
        sb = yb[pl.ds(2 * planes * T + i, 1), :]
        r0 = strips[pl.ds(pad8(planes) + i, 1), :]
        feeds = jnp.where((doubled(sb) >= r0) & ylo, 8, 0)
        es[i + 1, pl.ds(T, T), :] = eb + jnp.where(row == T - 1, feeds, 0)
        e = e_ext[i + 1]
        s15 = strips[pl.ds(i, 1), :]
        feeds = jnp.where(doubled(s15) >= ya[pl.ds(2 * planes * T + i, 1), :], 8, 0)
        es[i + 1, pl.ds(own, rows - T), :] = e[: rows - T]
        es[i + 1, pl.ds(own + rows - T, T), :] = e[rows - T :] + jnp.where(row == T - 1, feeds, 0)
        es[i + 1, pl.ds(own + rows, T), :] = ya[pl.ds(at, T), :].astype(jnp.int32)
        at = pl.multiple_of((planes + i) * T, T)
        ps[i, pl.ds(T, T), :] = yb[pl.ds(at, T), :]
        ps[i, pl.ds(own, rows), :] = p_ext[i]
        ps[i, pl.ds(own + rows, T), :] = ya[pl.ds(at, T), :]

    @pl.loop(0, planes)
    def _(i):
        for c in chunks:
            here = pl.ds(c, T)
            e = es[i + 1, here, :]
            ex = pltpu.roll(e, 1, 1)
            ey = es[i + 1, pl.ds(c - 1, T), :]
            ez = es[i, here, :]
            bs[i, here, :] = (e & 21) | (ex & 2) | (ey & 8) | (ez & 32)
            infl = (e & 42) | (ex & 1) | (ey & 4) | (ez & 16)
            pairs = (infl & 21) + ((infl >> 1) & 21)
            many = (pairs & 3) + ((pairs >> 2) & 3) + (pairs >> 4)
            p = ps[i, here, :]
            ps[i, here, :] = jnp.where(p >= 0, p * (1 << many).astype(jnp.float32), p)
            for d, (v, m) in enumerate(((e, 3), (ex, 3), (e, 12), (ey, 12), (e, 48), (ez, 48))):
                caps[d, i, here, :] = jnp.where((v & m) != 0, BIG, -3.0)

    totals = []
    for step in range(ROUNDS):
        reach = H - 2 * step - 1
        last = step == ROUNDS - 1

        @pl.loop(H - reach, H + depth + reach)
        def _(i):
            for c in chunks:
                here = pl.ds(c, T)
                p = ps[i, here, :]
                near = jnp.minimum(pltpu.roll(p, width - 1, 1), caps[0, i, here, :])
                near = jnp.maximum(near, jnp.minimum(pltpu.roll(p, 1, 1), caps[1, i, here, :]))
                near = jnp.maximum(near, jnp.minimum(ps[i, pl.ds(c + 1, T), :], caps[2, i, here, :]))
                near = jnp.maximum(near, jnp.minimum(ps[i, pl.ds(c - 1, T), :], caps[3, i, here, :]))
                near = jnp.maximum(near, jnp.minimum(ps[i + 1, here, :], caps[4, i, here, :]))
                near = jnp.maximum(near, jnp.minimum(ps[i - 1, here, :], caps[5, i, here, :]))
                ns[i, here, :] = jnp.where((p >= 0) & (p > near), 63, 0)

        def hits(i, c):
            here = pl.ds(c, T)
            n = ns[i, here, :]
            hit = (pltpu.roll(n, width - 1, 1) & 1) | (pltpu.roll(n, 1, 1) & 2)
            hit |= (ns[i, pl.ds(c + 1, T), :] & 4) | (ns[i, pl.ds(c - 1, T), :] & 8)
            hit |= (ns[i + 1, here, :] & 16) | (ns[i - 1, here, :] & 32)
            return n != 0, (hit & bs[i, here, :]) != 0, ps[i, here, :]

        reach -= 1
        zero = jnp.zeros(shape, jnp.int32)
        if last:

            def body(z, total):
                for j in range(0, rows, T):
                    new, hit, p = hits(z + H, own + j)
                    old = jnp.where(p >= 0, jnp.where(hit, 1, 0), jnp.where(p == -2.0, 2, 1))
                    state = jnp.where(new, 2, old)
                    state_out[z, pl.ds(j, T), :] = state
                    total = total + jnp.where(state == 0, 1, 0)
                return total

            total = lax.fori_loop(0, depth, body, zero)
        else:

            def body(i, total):
                mine = ((i >= H) & (i < H + depth)).astype(jnp.int32)
                for c in chunks:
                    new, hit, p = hits(i, c)
                    p = jnp.where(new, -2.0, jnp.where((p >= 0) & hit, -1.0, p))
                    ps[i, pl.ds(c, T), :] = p
                    if own <= c < own + rows:
                        total = total + jnp.where(p >= 0, mine, 0)
                return total

            total = lax.fori_loop(H - reach, H + depth + reach, body, zero)
        totals.append(jnp.sum(total))
    lane = lax.broadcasted_iota(jnp.int32, count_out.shape, 2)
    count_out[...] = jnp.where(lane == 0, totals[0], jnp.where(lane == 1, totals[1], jnp.where(lane == 2, totals[2], 0)))


def shift(value, axis, step):
    count = lax.axis_size(axis)
    return lax.ppermute(value, axis, [(i, (i + step) % count) for i in range(count)])


def call(kernel, outs, scratch, limit, args):
    return pl.pallas_call(
        kernel,
        out_shape=outs,
        in_specs=[whole()] * len(args),
        out_specs=[whole()] * len(outs),
        scratch_shapes=scratch,
        compiler_params=pltpu.CompilerParams(vmem_limit_bytes=limit * 2**20),
    )(*args)


def per_device(ranks, seeds, flags):
    depth, rows, width = ranks.shape
    assert depth > H and rows >= 2 * T and H < T
    planes = depth + 2 * H
    devices = lax.axis_size("gz") * lax.axis_size("gy")
    f32, i32 = jnp.float32, jnp.int32
    of = jax.ShapeDtypeStruct
    sz_top = seeds[2, depth - 1]
    sy_last = seeds[1, :, rows - 1]
    sz_low = shift(sz_top, "gz", 1)
    sy_low = shift(sy_last, "gy", 1)
    message = of((pad8((2 * H + 1) * rows + 2 * H), width), f32)
    up, dn, e_own, p_own, top_row = call(
        strength_kernel,
        [message, message, of(ranks.shape, i32), of(ranks.shape, f32), of((depth, width), f32)],
        [pltpu.VMEM(ranks.shape, f32)],
        12,
        (seeds, ranks, flags, sz_low, sy_low),
    )
    zb = shift(up, "gz", 1)
    za = shift(dn, "gz", -1)
    message = of((2 * planes * T + pad8(planes), width), f32)
    yup, ydn, e_ext, p_ext, strips = call(
        planes_kernel,
        [
            message,
            message,
            of((planes + 1, rows, width), i32),
            of((planes, rows, width), f32),
            of((2 * pad8(planes), width), f32),
        ],
        [],
        12,
        (zb, za, e_own, p_own, top_row, sz_low, sz_top, sy_last, dn),
    )
    yb = shift(yup, "gy", 1)
    ya = shift(ydn, "gy", -1)
    tall = rows + 4 * T
    state, counts = call(
        rounds_kernel,
        [of(ranks.shape, i32), of((devices, 1, 128), i32)],
        [
            pltpu.VMEM((planes + 1, tall, width), i32),
            pltpu.VMEM((planes, tall, width), f32),
            pltpu.VMEM((planes, tall, width), i32),
            pltpu.VMEM((planes, tall, width), i32),
            pltpu.VMEM((6, planes, tall, width), f32),
        ],
        30,
        (yb, ya, e_ext, p_ext, strips),
    )
    everyone = lax.all_to_all(counts, ("gz", "gy"), 0, 0, tiled=True)
    undecided = jnp.sum(everyone, axis=(0, 1))[:ROUNDS]
    return (state, undecided)


def solution(mesh):
    return jax.shard_map(
        per_device,
        mesh=mesh,
        in_specs=(P("gz", "gy", None), P(None, "gz", "gy", None), P("gz", "gy", None)),
        out_specs=(P("gz", "gy", None), P()),
        check_vma=False,
    )
```

time: 159 us -> 77.1 us (0.48)
  starting transfers between devices: 64.6 us -> 9.59 us
  blocking collectives: 41.4 us -> 11 us
  other arithmetic: 29.5 us -> 0.56 us
  waiting for transfers between devices: 21.8 us -> 36.6 us
  Pallas kernels: 0 us -> 13.6 us
  local copies, waits for them, and re-layouts: 0.1 us -> 4.72 us
    ppermute x22 -> x6, starting transfers between devices: 64.6 us -> 9.59 us  [shift(): lax.ppermute(value, axis, [(i, (i + step) % count) for i in range(count)])]
    psum x1 -> x0, blocking collectives: 41.4 us -> none  [per_device(): totals.append(lax.psum(local, ('gz', 'gy')))]
    convert_element_type x3 -> x0, other arithmetic: 16.5 us -> none  [select(): return ((center >= 0) & (center > nearest)).astype(jnp.int32)]
    ppermute x22 -> x6, waiting for transfers between devices: 21.8 us -> 36.6 us  [shift(): lax.ppermute(value, axis, [(i, (i + step) % count) for i in range(count)])]
    pallas_call x0 -> x3, Pallas kernels: none -> 13.6 us  [call(): pl.pallas_call(kernel, out_shape=outs, in_specs=[whole()] * len(args), ou...]
    all_to_all x0 -> x1, blocking collectives: none -> 11 us  [per_device(): everyone = lax.all_to_all(counts, ('gz', 'gy'), 0, 0, tiled=True)]
    reduce_sum x3 -> x1, other arithmetic: 6.73 us -> 0.56 us  [per_device(): undecided = jnp.sum(everyone, axis=(0, 1))[:ROUNDS]]
    unnamed x4 -> x7, local copies, waits for them, and re-layouts: 0.01 us -> 3.04 us
  transfers between devices with their start and end apart: 22 -> 6, of which waited for: 10 -> 5; matrix products, arithmetic and copies ran while one was open for 0% -> 1% of each run, Pallas kernels for 0% -> 0%
where the time goes in v1:
time: 77.1 us; the launch traced here: 76.7 us
  waiting for transfers between devices  36.6 us (47%)
  Pallas kernels  13.6 us (18%)
  blocking collectives  11 us (14%)
  starting transfers between devices  9.59 us (12%)
  local copies, waits for them, and re-layouts  4.72 us (6%)
    ppermute x6, waiting for transfers between devices, shift(): lax.ppermute(value, axis, [(i, (i + step) % count) for i in range(count)])  36.6 us
    pallas_call x3, Pallas kernels, call(): pl.pallas_call(kernel, out_shape=outs, in_specs=[whole()] * len(args), ou...  13.6 us
    all_to_all x1, blocking collectives, per_device(): everyone = lax.all_to_all(counts, ('gz', 'gy'), 0, 0, tiled=True)  11 us
    ppermute x6, starting transfers between devices, shift(): lax.ppermute(value, axis, [(i, (i + step) % count) for i in range(count)])  9.59 us
    unnamed x7, local copies, waits for them, and re-layouts  3.04 us
  transfers between devices with their start and end apart: 6, of which 5 were waited for; matrix products, arithmetic and copies ran while one was open for 1% of the time, Pallas kernels for 0%

profile of v1, /device:TPU:0, one launch (start us, length us, event | category | flops | bytes accessed | tf_op | source)
XLA Modules:
  0.0 76.7 jit_solution(18160265292822407353)
XLA Ops:
  0.6 0.8 slice_bitcast_fusion.sz_top
  1.4 3.0 %collective-permute-start = (f32[16,512]{1,0:T(8,128)S(1)}, f32[16,512]{1,0:T(8,128)S(1)}, u32[]{:S(2)}, u32[]{:S(2)}) collective-permute-start(f32[16,512]{1,0:T(8,128)S(1)} %slice_bitcast_fusion.sz_top), channel_id=1, source_target_pairs={{0,4},{4,8},{8,12},{12,16},{16,20},{20,24},{24,28},{28,0},{1,5},{5... | collective-permute-start | bytes 98312 | tf_op jit(solution)/shard_map/ppermute | solution.py:252
  4.4 0.9 %slice.10 = f32[1,8,1,512]{3,2,1,0:T(1,128)S(1)} slice(f32[3,8,16,512]{3,2,1,0:T(8,128)} %seeds.1), slice={[1:2], [0:8], [15:16], [0:512]} | slice | bytes 32768 | tf_op jit(solution)/shard_map/slice | solution.py:274
  5.3 0.1 collective-permute-start.1
  5.4 3.2 %collective-permute-done.1.sy_low = f32[8,512]{1,0:T(8,128)S(1)} collective-permute-done((f32[8,512]{1,0:T(8,128)S(1)}, f32[8,512]{1,0:T(8,128)S(1)}, u32[]{:S(2)}, u32[]{:S(2)}) %collective-permute-start.1) | collective-permute-done | bytes 16416 | tf_op jit(solution)/shard_map/ppermute | solution.py:252
  8.5 0.8 %collective-permute-done.sz_low = f32[16,512]{1,0:T(8,128)S(1)} collective-permute-done((f32[16,512]{1,0:T(8,128)S(1)}, f32[16,512]{1,0:T(8,128)S(1)}, u32[]{:S(2)}, u32[]{:S(2)}) %collective-permute-start) | collective-permute-done | bytes 32800 | tf_op jit(solution)/shard_map/ppermute | solution.py:252
  9.3 0.0 copy-start
  9.3 1.1 %copy-done = f32[3,8,16,512]{3,2,1,0:T(8,128)S(1)} copy-done((f32[3,8,16,512]{3,2,1,0:T(8,128)S(1)}, f32[3,8,16,512]{3,2,1,0:T(8,128)}, u32[]{:S(2)}) %copy-start) | copy-done | bytes 786456
  10.4 0.0 copy-start.1
  10.4 0.9 %copy-done.1 = f32[8,16,512]{2,1,0:T(8,128)S(1)} copy-done((f32[8,16,512]{2,1,0:T(8,128)S(1)}, f32[8,16,512]{2,1,0:T(8,128)}, u32[]{:S(2)}) %copy-start.1) | copy-done | bytes 262168
  11.4 0.9 %copy-done.2 = s32[8,16,512]{2,1,0:T(8,128)S(1)} copy-done((s32[8,16,512]{2,1,0:T(8,128)S(1)}, s32[8,16,512]{2,1,0:T(8,128)}, u32[]{:S(2)}) %copy-start.2) | copy-done | bytes 262168
  12.3 0.4 shard_map.50
  12.8 0.8 %collective-permute-start.2 = (f32[224,512]{1,0:T(8,128)S(1)}, f32[224,512]{1,0:T(8,128)S(1)}, u32[]{:S(2)}, u32[]{:S(2)}) collective-permute-start(f32[224,512]{1,0:T(8,128)S(1)} %get-tuple-element.14), channel_id=1, source_target_pairs={{0,4},{4,8},{8,12},{12,16},{16,20},{20,24},{24,28},{28,0},{1,5},{5... | collective-permute-start | bytes 1376264 | tf_op jit(solution)/shard_map/ppermute | solution.py:252
  13.6 4.0 %collective-permute-start.3 = (f32[224,512]{1,0:T(8,128)S(1)}, f32[224,512]{1,0:T(8,128)S(1)}, u32[]{:S(2)}, u32[]{:S(2)}) collective-permute-start(f32[224,512]{1,0:T(8,128)S(1)} %get-tuple-element.15.dn_own), channel_id=1, source_target_pairs={{0,28},{4,0},{8,4},{12,8},{16,12},{20,16},{24,20},{28,24},{1,29},{... | collective-permute-start | bytes 1376264 | tf_op jit(solution)/shard_map/ppermute | solution.py:252
  17.5 15.2 %collective-permute-done.2.zb = f32[224,512]{1,0:T(8,128)S(1)} collective-permute-done((f32[224,512]{1,0:T(8,128)S(1)}, f32[224,512]{1,0:T(8,128)S(1)}, u32[]{:S(2)}, u32[]{:S(2)}) %collective-permute-start.2) | collective-permute-done | bytes 458784 | tf_op jit(solution)/shard_map/ppermute | solution.py:252
  32.7 2.2 %collective-permute-done.3.za = f32[224,512]{1,0:T(8,128)S(1)} collective-permute-done((f32[224,512]{1,0:T(8,128)S(1)}, f32[224,512]{1,0:T(8,128)S(1)}, u32[]{:S(2)}, u32[]{:S(2)}) %collective-permute-start.3) | collective-permute-done | bytes 458784 | tf_op jit(solution)/shard_map/ppermute | solution.py:252
  34.9 0.2 shard_map.51
  35.1 0.1 collective-permute-start.4
  35.2 1.7 %collective-permute-start.5 = (f32[344,512]{1,0:T(8,128)S(1)}, f32[344,512]{1,0:T(8,128)S(1)}, u32[]{:S(2)}, u32[]{:S(2)}) collective-permute-start(f32[344,512]{1,0:T(8,128)S(1)} %get-tuple-element.20), channel_id=1, source_target_pairs={{0,3},{1,0},{2,1},{3,2},{4,7},{5,4},{6,5},{7,6},{8,11},{9,8},{10,9... | collective-permute-start | bytes 2113544 | tf_op jit(solution)/shard_map/ppermute | solution.py:252
  36.9 15.3 %collective-permute-done.4.yb = f32[344,512]{1,0:T(8,128)S(1)} collective-permute-done((f32[344,512]{1,0:T(8,128)S(1)}, f32[344,512]{1,0:T(8,128)S(1)}, u32[]{:S(2)}, u32[]{:S(2)}) %collective-permute-start.4) | collective-permute-done | bytes 704544 | tf_op jit(solution)/shard_map/ppermute | solution.py:252
  52.2 0.0 collective-permute-done.5.ya
  52.2 13.0 %shard_map.52 = (s32[8,16,512]{2,1,0:T(8,128)}, s32[32,1,128]{2,1,0:T(1,128)S(1)}) custom-call(f32[344,512]{1,0:T(8,128)S(1)} %collective-permute-done.4.yb, f32[344,512]{1,0:T(8,128)S(1)} %collective-permute-done.5.ya, s32[21,16,512]{2,1,0:T(8,128)S(1)} %get-tuple-element.21.e_ext, f32[20,16,512]{2,1,0:T(8,128)S(1)} %get-tuple-element.22.p_ext, ...), custom_call_target="tpu_custom_call" | custom-call | tf_op jit(solution)/shard_map/pallas_call | solution.py:256
  65.2 11.0 %all_to_all.5 = s32[32,1,128]{2,1,0:T(1,128)S(1)} all-to-all(s32[32,1,128]{2,1,0:T(1,128)S(1)} %get-tuple-element.25), channel_id=1, replica_groups=mesh['gz'=8,'gy'=4] {'gz','gy'}, dimensions={0} | all-to-all | bytes 32768 | tf_op jit(solution)/shard_map/all_to_all | solution.py:317
  76.2 0.6 reduce_sum.9
  (2 shorter events, 0.0 us)
Async XLA Ops:
  1.4 7.9 %collective-permute-start = (f32[16,512]{1,0:T(8,128)S(1)}, f32[16,512]{1,0:T(8,128)S(1)}, u32[]{:S(2)}, u32[]{:S(2)}) collective-permute-start(f32[16,512]{1,0:T(8,128)S(1)} %slice_bitcast_fusion.sz_top), channel_id=1, source_target_pairs={{0,4},{4,8},{8,12},{12,16},{16,20},{20,24},{24,28},{28,0},{1,5},{5... | collective-permute-start | bytes 98312 | tf_op jit(solution)/shard_map/ppermute | solution.py:252
  5.3 3.2 %collective-permute-start.1 = (f32[8,512]{1,0:T(8,128)S(1)}, f32[8,512]{1,0:T(8,128)S(1)}, u32[]{:S(2)}, u32[]{:S(2)}) collective-permute-start(f32[8,512]{1,0:T(8,128)S(1)} %bitcast.6), channel_id=1, source_target_pairs={{0,1},{1,2},{2,3},{3,0},{4,5},{5,6},{6,7},{7,4},{8,9},{9,10},{10,1... | collective-permute-start | bytes 49160 | tf_op jit(solution)/shard_map/ppermute | solution.py:252
  9.3 1.1 %copy-start = (f32[3,8,16,512]{3,2,1,0:T(8,128)S(1)}, f32[3,8,16,512]{3,2,1,0:T(8,128)}, u32[]{:S(2)}) copy-start(f32[3,8,16,512]{3,2,1,0:T(8,128)} %seeds.1) | copy-start | bytes 2359300
  10.4 0.9 %copy-start.1 = (f32[8,16,512]{2,1,0:T(8,128)S(1)}, f32[8,16,512]{2,1,0:T(8,128)}, u32[]{:S(2)}) copy-start(f32[8,16,512]{2,1,0:T(8,128)} %ranks.1) | copy-start | bytes 786436
  11.4 0.9 %copy-start.2 = (s32[8,16,512]{2,1,0:T(8,128)S(1)}, s32[8,16,512]{2,1,0:T(8,128)}, u32[]{:S(2)}) copy-start(s32[8,16,512]{2,1,0:T(8,128)} %flags.1) | copy-start | bytes 786436
  12.8 19.9 %collective-permute-start.2 = (f32[224,512]{1,0:T(8,128)S(1)}, f32[224,512]{1,0:T(8,128)S(1)}, u32[]{:S(2)}, u32[]{:S(2)}) collective-permute-start(f32[224,512]{1,0:T(8,128)S(1)} %get-tuple-element.14), channel_id=1, source_target_pairs={{0,4},{4,8},{8,12},{12,16},{16,20},{20,24},{24,28},{28,0},{1,5},{5... | collective-permute-start | bytes 1376264 | tf_op jit(solution)/shard_map/ppermute | solution.py:252
  13.6 21.3 %collective-permute-start.3 = (f32[224,512]{1,0:T(8,128)S(1)}, f32[224,512]{1,0:T(8,128)S(1)}, u32[]{:S(2)}, u32[]{:S(2)}) collective-permute-start(f32[224,512]{1,0:T(8,128)S(1)} %get-tuple-element.15.dn_own), channel_id=1, source_target_pairs={{0,28},{4,0},{8,4},{12,8},{16,12},{20,16},{24,20},{28,24},{1,29},{... | collective-permute-start | bytes 1376264 | tf_op jit(solution)/shard_map/ppermute | solution.py:252
  35.1 17.1 %collective-permute-start.4 = (f32[344,512]{1,0:T(8,128)S(1)}, f32[344,512]{1,0:T(8,128)S(1)}, u32[]{:S(2)}, u32[]{:S(2)}) collective-permute-start(f32[344,512]{1,0:T(8,128)S(1)} %get-tuple-element.19), channel_id=1, source_target_pairs={{0,1},{1,2},{2,3},{3,0},{4,5},{5,6},{6,7},{7,4},{8,9},{9,10},{10,1... | collective-permute-start | bytes 2113544 | tf_op jit(solution)/shard_map/ppermute | solution.py:252
  35.2 17.1 %collective-permute-start.5 = (f32[344,512]{1,0:T(8,128)S(1)}, f32[344,512]{1,0:T(8,128)S(1)}, u32[]{:S(2)}, u32[]{:S(2)}) collective-permute-start(f32[344,512]{1,0:T(8,128)S(1)} %get-tuple-element.20), channel_id=1, source_target_pairs={{0,3},{1,0},{2,1},{3,2},{4,7},{5,4},{6,5},{7,6},{8,11},{9,8},{10,9... | collective-permute-start | bytes 2113544 | tf_op jit(solution)/shard_map/ppermute | solution.py:252

commit v2 on v0

v2 whole, which is shorter than its diff:
```python
import jax
import jax.numpy as jnp
from jax import lax
from jax.experimental import pallas as pl
from jax.experimental.pallas import tpu as pltpu
from jax.sharding import PartitionSpec as P

ROUNDS = 3
H = 2 * ROUNDS
T = 8
L = 128
BIG = 3.0e38
F32, I32 = jnp.float32, jnp.int32
CAPS, STATE, PATTERN, NEW = 0, 6, 0, 0


def vmem():
    return pl.BlockSpec(memory_space=pltpu.VMEM)


def neighbours(axis):
    i = lax.axis_index(axis)
    return i > 0, i < lax.axis_size(axis) - 1


def doubled(s):
    return jnp.where(s > 0, 2.0 * s, -1.0)


def scaled(p, bit):
    return jnp.where((bit != 0) & (p >= 0), 2.0 * p, p)


def edge_kernel(seeds, sz_top, sy_last, twice, rm):
    depth, rows, width = rm.shape
    _, zhi = neighbours("gz")
    _, yhi = neighbours("gy")
    shape = (rows, width)
    row = lax.broadcasted_iota(I32, shape, 0)
    x_in = lax.broadcasted_iota(I32, shape, 1) < width - 1
    y_in = (row < rows - 1) | yhi
    sz_top[...] = seeds[2, depth - 1]
    sz_prev = None
    for z in range(depth):
        sy_last[pl.ds(z, 1), :] = seeds[1, z, pl.ds(rows - 1, 1), :]
        sx = jnp.where(x_in, seeds[0, z], 0.0)
        sy = jnp.where(y_in, seeds[1, z], 0.0)
        sz = seeds[2, z]
        if z == depth - 1:
            sz = jnp.where(zhi, sz, 0.0)
        r = jnp.maximum(jnp.maximum(sx, pltpu.roll(sx, 1, 1)), jnp.maximum(sy, sz))
        r = jnp.maximum(r, jnp.where(row == 0, 0.0, pltpu.roll(sy, 1, 0)))
        rm[z] = r if z == 0 else jnp.maximum(r, sz_prev)
        sz_prev = sz
        for d, s in enumerate((sx, sy, sz)):
            twice[d, z] = doubled(s)


def packed_kernel(ranks, flags, packed):
    f = flags[...]
    packed[...] = jnp.where(f == 0, ranks[...], jnp.where(f == 2, -2.0, -1.0))


def strength_kernel(twice, rm, packed, sz_low, sy_low, up, dn, d_out, m_out):
    depth, rows, width = packed.shape
    zlo, _ = neighbours("gz")
    ylo, _ = neighbours("gy")
    row = lax.broadcasted_iota(I32, (rows, width), 0)
    tz_prev = doubled(jnp.where(zlo, sz_low[...], 0.0))
    for z in range(depth):
        sy_prev = jnp.where(ylo, sy_low[pl.ds(z, 1), :], 0.0)
        r = jnp.maximum(rm[z], jnp.where(row == 0, sy_prev, 0.0))
        if z == 0:
            r = jnp.maximum(r, jnp.where(zlo, sz_low[...], 0.0))
        tx, ty, tz = twice[0, z], twice[1, z], twice[2, z]
        ty_prev = jnp.where(row == 0, doubled(sy_prev), pltpu.roll(ty, 1, 0))
        d = jnp.where(tx >= r, 1, 0) + jnp.where(pltpu.roll(tx, 1, 1) >= r, 2, 0)
        d += jnp.where(ty >= r, 4, 0) + jnp.where(ty_prev >= r, 8, 0)
        d += jnp.where(tz >= r, 16, 0) + jnp.where(tz_prev >= r, 32, 0)
        d_out[z] = d
        tz_prev = tz
    for z in range(depth):
        d = d_out[z]
        i = (pltpu.roll(d, width - 1, 1) & 2) | (pltpu.roll(d, 1, 1) & 1)
        i |= jnp.where(row == rows - 1, 0, pltpu.roll(d, rows - 1, 0) & 8)
        i |= jnp.where(row == 0, 0, pltpu.roll(d, 1, 0) & 4)
        if z < depth - 1:
            i |= d_out[z + 1] & 32
        if z > 0:
            i |= d_out[z - 1] & 16
        pairs = (i & 21) + ((i >> 1) & 21)
        many = (pairs & 3) + ((pairs >> 2) & 3) + (pairs >> 4)
        p = packed[z]
        m = jnp.where(p >= 0, p * (1 << many).astype(F32), p)
        m_out[z] = m
        k = depth - z
        if k <= H:
            up[pl.ds((k - 1) * rows, rows), :] = d.astype(F32)
            up[pl.ds((H + k - 1) * rows, rows), :] = m
        if z < H:
            dn[pl.ds(z * rows, rows), :] = d.astype(F32)
            dn[pl.ds((H + z) * rows, rows), :] = m


def y_layout(depth):
    patterns, measures, at = [], [], 0
    for out, least in ((patterns, 1), (measures, 0)):
        for z in range(-H, depth + H):
            k = max(-z, z - depth + 1, 0)
            n = max(H - k, least)
            if n:
                out.append((z, n, at))
                at += n
    return patterns, measures, -(-at // T) * T


def planes_kernel(zb, za, d_own, m_own, ye, yo, d_ext, m_ext):
    depth, rows, _ = m_own.shape
    zlo, zhi = neighbours("gz")
    even = lax.axis_index("gy") % 2 == 0
    for k in range(1, H + 1):
        at, am = pl.ds((k - 1) * rows, rows), pl.ds((H + k - 1) * rows, rows)
        d_ext[H - k] = jnp.where(zlo, zb[at, :], 0.0).astype(I32)
        d_ext[H + depth + k - 1] = jnp.where(zhi, za[at, :], 0.0).astype(I32)
        m_ext[H - k] = zb[am, :]
        m_ext[H + depth + k - 1] = za[am, :]
    for z in range(depth):
        d_ext[H + z] = d_own[z]
        m_ext[H + z] = m_own[z]
    first, last = H, H + depth - 1
    m_ext[first - 1] = scaled(m_ext[first - 1], d_ext[first] & 32)
    m_ext[first] = scaled(m_ext[first], d_ext[first - 1] & 16)
    m_ext[last] = scaled(m_ext[last], d_ext[last + 1] & 32)
    m_ext[last + 1] = scaled(m_ext[last + 1], d_ext[last] & 16)
    patterns, measures, _ = y_layout(depth)

    def send(upward, downward):
        for z, n, at in patterns:
            e = d_ext[z + H].astype(F32)
            upward[pl.ds(at, n), :] = e[rows - n :]
            downward[pl.ds(at, n), :] = e[:n]
        for z, n, at in measures:
            e = m_ext[z + H]
            upward[pl.ds(at, n), :] = e[rows - n :]
            downward[pl.ds(at, n), :] = e[:n]

    @pl.when(even)
    def _():
        send(ye, yo)

    @pl.when(jnp.logical_not(even))
    def _():
        send(yo, ye)


def blocks(v):
    return jnp.stack([v[:, j : j + L] for j in range(0, v.shape[1], L)])


def x_next(v):
    r = pltpu.roll(v, L - 1, 2)
    lane = lax.broadcasted_iota(I32, v.shape, 2)
    return jnp.where(lane == L - 1, jnp.concatenate([r[1:], r[:1]], 0), r)


def x_prev(v):
    r = pltpu.roll(v, 1, 2)
    lane = lax.broadcasted_iota(I32, v.shape, 2)
    return jnp.where(lane == 0, jnp.concatenate([r[-1:], r[:-1]], 0), r)


def set_caps(fw, iw, i, at, n):
    def d_at(plane, row):
        return iw[PATTERN, plane, :, pl.ds(row, n), :]

    d = d_at(i, at)
    others = (x_next(d), x_prev(d), d_at(i, at + 1), d_at(i, at - 1), d_at(i + 1, at), d_at(i - 1, at))
    for j, other in enumerate(others):
        linked = (d & (1 << j)) | (other & (1 << (j ^ 1)))
        fw[CAPS + j, i, :, pl.ds(at, n), :] = jnp.where(linked != 0, BIG, -3.0)


def select(fw, iw, step, i, at, n):
    def cap(j):
        return fw[CAPS + j, i, :, pl.ds(at, n), :]

    def p_at(plane, row):
        return fw[STATE + step, plane, :, pl.ds(row, n), :]

    p = p_at(i, at)
    near = jnp.maximum(jnp.minimum(x_next(p), cap(0)), jnp.minimum(x_prev(p), cap(1)))
    near = jnp.maximum(near, jnp.minimum(p_at(i, at + 1), cap(2)))
    near = jnp.maximum(near, jnp.minimum(p_at(i, at - 1), cap(3)))
    near = jnp.maximum(near, jnp.minimum(p_at(i + 1, at), cap(4)))
    near = jnp.maximum(near, jnp.minimum(p_at(i - 1, at), cap(5)))
    new = (p >= 0) & (p > near)
    iw[NEW + 1 + step, i, :, pl.ds(at, n), :] = jnp.where(new, 63, 0)


def hits(fw, iw, step, i, at, n):
    def n_at(plane, row):
        return iw[NEW + 1 + step, plane, :, pl.ds(row, n), :]

    new = n_at(i, at)
    hit = (x_next(new) & 1) | (x_prev(new) & 2)
    hit |= (n_at(i, at + 1) & 4) | (n_at(i, at - 1) & 8)
    hit |= (n_at(i + 1, at) & 16) | (n_at(i - 1, at) & 32)
    hit &= iw[PATTERN, i, :, pl.ds(at, n), :]
    return new != 0, hit != 0, fw[STATE + step, i, :, pl.ds(at, n), :]


def update(fw, iw, step, i, at, n):
    new, hit, p = hits(fw, iw, step, i, at, n)
    p = jnp.where(new, -2.0, jnp.where((p >= 0) & hit, -1.0, p))
    fw[STATE + step + 1, i, :, pl.ds(at, n), :] = p


def inner_kernel(d_ext, m_ext, fw, iw):
    planes, rows, _ = m_ext.shape
    depth = planes - 2 * H

    @pl.loop(0, planes)
    def _(i):
        iw[PATTERN, i, :, pl.ds(T, rows), :] = blocks(d_ext[i])
        fw[STATE, i, :, pl.ds(T, rows), :] = blocks(m_ext[i])

    for stage in range(2 * ROUNDS - 1):
        step, reach = stage // 2, H - 1 - stage

        @pl.loop(H - reach, H + depth + reach)
        def _(i):
            for at in range(T, T + rows, T):
                if stage == 0:
                    set_caps(fw, iw, i, at, T)
                if stage % 2 == 0:
                    select(fw, iw, step, i, at, T)
                else:
                    update(fw, iw, step, i, at, T)


def outer_kernel(re, ro, fw_in, iw_in, state_out, count_out, fw, iw):
    del fw_in, iw_in
    depth, rows, width = state_out.shape
    planes = depth + 2 * H
    ylo, yhi = neighbours("gy")
    even = lax.axis_index("gy") % 2 == 0
    patterns, measures, _ = y_layout(depth)
    for z, n, at in patterns:
        e, o = re[pl.ds(at, n), :], ro[pl.ds(at, n), :]
        above = jnp.where(yhi, jnp.where(even, e, o), 0.0).astype(I32)
        below = jnp.where(ylo, jnp.where(even, o, e), 0.0).astype(I32)
        iw[PATTERN, z + H, :, pl.ds(T - n, n), :] = blocks(below)
        iw[PATTERN, z + H, :, pl.ds(T + rows, n), :] = blocks(above)
    for z, n, at in measures:
        e, o = re[pl.ds(at, n), :], ro[pl.ds(at, n), :]
        fw[STATE, z + H, :, pl.ds(T - n, n), :] = blocks(jnp.where(even, o, e))
        fw[STATE, z + H, :, pl.ds(T + rows, n), :] = blocks(jnp.where(even, e, o))

    def low(stage):
        return T - H + stage

    def high(stage):
        return T + rows + H - T - stage

    shape = (width // L, T, L)
    row = lax.broadcasted_iota(I32, shape, 1)

    @pl.loop(0, planes)
    def _(i):
        for at, one, two in ((low(0), H - 1, H), (high(0), T - H - 1, T - H)):
            d_next = iw[PATTERN, i, :, pl.ds(at + 1, T), :]
            d_prev = iw[PATTERN, i, :, pl.ds(at - 1, T), :]
            bit = jnp.where(row == one, d_next & 8, jnp.where(row == two, d_prev & 4, 0))
            here = pl.ds(at, T)
            fw[STATE, i, :, here, :] = scaled(fw[STATE, i, :, here, :], bit)

    for stage in range(2 * ROUNDS - 1):
        step, reach = stage // 2, H - 1 - stage

        @pl.loop(H - reach, H + depth + reach)
        def _(i):
            for at in (low(stage), high(stage)):
                if stage == 0:
                    set_caps(fw, iw, i, at, T)
                if stage % 2 == 0:
                    select(fw, iw, step, i, at, T)
                else:
                    update(fw, iw, step, i, at, T)

    def finish(z, totals):
        totals = list(totals)
        for at in range(0, rows, T):
            new, hit, p = hits(fw, iw, ROUNDS - 1, z + H, T + at, T)
            old = jnp.where(p >= 0, jnp.where(hit, 1, 0), jnp.where(p == -2.0, 2, 1))
            state = jnp.where(new, 2, old)
            for j in range(width // L):
                state_out[z, pl.ds(at, T), pl.ds(j * L, L)] = state[j]
            totals[-1] = totals[-1] + jnp.where(state == 0, 1, 0)
            for step in range(ROUNDS - 1):
                p = fw[STATE + step + 1, z + H, :, pl.ds(T + at, T), :]
                totals[step] = totals[step] + jnp.where(p >= 0, 1, 0)
        return tuple(totals)

    totals = lax.fori_loop(0, depth, finish, (jnp.zeros(shape, I32),) * ROUNDS)
    lane = lax.broadcasted_iota(I32, count_out.shape, 2)
    counts = jnp.zeros(count_out.shape, I32)
    for step in range(ROUNDS):
        counts = jnp.where(lane == step, jnp.sum(totals[step]), counts)
    count_out[...] = counts


def shift(value, axis, step):
    count = lax.axis_size(axis)
    return lax.ppermute(value, axis, [(i, (i + step) % count) for i in range(count)])


def swap(value, axis, odd):
    count = lax.axis_size(axis)
    pairs = [(i, i) for i in range(count)]
    for i in range(odd, count - 1, 2):
        pairs[i], pairs[i + 1] = (i, i + 1), (i + 1, i)
    return lax.ppermute(value, axis, pairs)


def call(kernel, outs, args, limit, cost, **more):
    specs = more.pop("in_specs", [vmem()] * len(args))
    return pl.pallas_call(
        kernel,
        out_shape=outs,
        in_specs=specs,
        out_specs=[vmem()] * len(outs),
        compiler_params=pltpu.CompilerParams(vmem_limit_bytes=limit * 2**20),
        cost_estimate=pl.CostEstimate(flops=cost, bytes_accessed=cost, transcendentals=0),
        **more,
    )(*args)


def per_device(ranks, seeds, flags):
    depth, rows, width = ranks.shape
    assert depth >= H and rows >= 2 * T and T == H + 2 and width % L == 0
    planes = depth + 2 * H
    devices = lax.axis_size("gz") * lax.axis_size("gy")
    of = jax.ShapeDtypeStruct
    own = [of(ranks.shape, F32)]
    sz_top, sy_last, twice, rm = call(
        edge_kernel,
        [of((rows, width), F32), of((depth, width), F32), of(seeds.shape, F32)] + own,
        (seeds,),
        8,
        4000000,
    )
    sz_low = shift(sz_top, "gz", 1)
    sy_low = shift(sy_last, "gy", 1)
    (packed,) = call(packed_kernel, own, (ranks, flags), 8, 4000000)
    message = of((2 * H * rows, width), F32)
    up, dn, d_own, m_own = call(
        strength_kernel,
        [message, message, of(ranks.shape, I32)] + own,
        (twice, rm, packed, sz_low, sy_low),
        8,
        4000000,
    )
    zb = shift(up, "gz", 1)
    za = shift(dn, "gz", -1)
    message = of((y_layout(depth)[2], width), F32)
    ext = (planes, rows, width)
    ye, yo, d_ext, m_ext = call(
        planes_kernel, [message, message, of(ext, I32), of(ext, F32)], (zb, za, d_own, m_own), 8, 4000000
    )
    re = swap(ye, "gy", 0)
    ro = swap(yo, "gy", 1)
    cells = (planes, width // L, rows + 2 * T, L)
    works = [of((STATE + ROUNDS,) + cells, F32), of((NEW + 1 + ROUNDS,) + cells, I32)]
    fw, iw = call(inner_kernel, works, (d_ext, m_ext), 8, 20000000)
    state, counts, _, _ = call(
        outer_kernel,
        [of(ranks.shape, I32), of((devices, 1, L), I32)] + works,
        (re, ro, fw, iw),
        8,
        20000000,
        input_output_aliases={2: 2, 3: 3},
    )
    everyone = lax.all_to_all(counts, ("gz", "gy"), 0, 0, tiled=True)
    undecided = jnp.sum(everyone, axis=(0, 1))[:ROUNDS]
    return (state, undecided)


def solution(mesh):
    return jax.shard_map(
        per_device,
        mesh=mesh,
        in_specs=(P("gz", "gy", None), P(None, "gz", "gy", None), P("gz", "gy", None)),
        out_specs=(P("gz", "gy", None), P()),
        check_vma=False,
    )
```

time: 159 us -> 60.4 us (0.38)
  starting transfers between devices: 64.6 us -> 8.54 us
  other arithmetic: 29.5 us -> 0.56 us
  blocking collectives: 41.4 us -> 12.5 us
  Pallas kernels: 0 us -> 17.1 us
  waiting for transfers between devices: 21.8 us -> 17.7 us
  local copies, waits for them, and re-layouts: 0.1 us -> 3.03 us
    ppermute x22 -> x6, starting transfers between devices: 64.6 us -> 8.54 us  [the longest x4 7.79 us: shift(): lax.ppermute(value, axis, [(i, (i + step) % count) for i in range(count)])]
    psum x1 -> x0, blocking collectives: 41.4 us -> none  [per_device(): totals.append(lax.psum(local, ('gz', 'gy')))]
    pallas_call x0 -> x6, Pallas kernels: none -> 17.1 us  [call(): pl.pallas_call(kernel, out_shape=outs, in_specs=specs, out_specs=[vmem()]...]
    convert_element_type x3 -> x0, other arithmetic: 16.5 us -> none  [select(): return ((center >= 0) & (center > nearest)).astype(jnp.int32)]
    all_to_all x0 -> x1, blocking collectives: none -> 12.5 us  [per_device(): everyone = lax.all_to_all(counts, ('gz', 'gy'), 0, 0, tiled=True)]
    reduce_sum x3 -> x1, other arithmetic: 6.73 us -> 0.56 us  [per_device(): undecided = jnp.sum(everyone, axis=(0, 1))[:ROUNDS]]
    ppermute x22 -> x6, waiting for transfers between devices: 21.8 us -> 17.7 us  [the longest x4 17.6 us: shift(): lax.ppermute(value, axis, [(i, (i + step) % count) for i in range(count)])]
    unnamed x4 -> x6, local copies, waits for them, and re-layouts: 0.01 us -> 3.03 us
  transfers between devices with their start and end apart: 22 -> 6, of which waited for: 10 -> 4; matrix products, arithmetic and copies ran while one was open for 0% -> 0% of each run, Pallas kernels for 0% -> 12%
where the time goes in v2:
time: 60.4 us; the launch traced here: 60.1 us
  waiting for transfers between devices  17.7 us (29%)
  Pallas kernels  17.1 us (28%)
  blocking collectives  12.5 us (21%)
  starting transfers between devices  8.54 us (14%)
  local copies, waits for them, and re-layouts  3.03 us (5%)
  between operations  0.71 us (1%)
    ppermute x4, waiting for transfers between devices, shift(): lax.ppermute(value, axis, [(i, (i + step) % count) for i in range(count)])  17.6 us
    pallas_call x6, Pallas kernels, call(): pl.pallas_call(kernel, out_shape=outs, in_specs=specs, out_specs=[vmem()]...  17.1 us
    all_to_all x1, blocking collectives, per_device(): everyone = lax.all_to_all(counts, ('gz', 'gy'), 0, 0, tiled=True)  12.5 us
    ppermute x4, starting transfers between devices, shift(): lax.ppermute(value, axis, [(i, (i + step) % count) for i in range(count)])  7.79 us
    unnamed x6, local copies, waits for them, and re-layouts  3.03 us
  transfers between devices with their start and end apart: 6, of which 4 were waited for; matrix products, arithmetic and copies ran while one was open for 0% of the time, Pallas kernels for 12%

profile of v2, /device:TPU:0, one launch (start us, length us, event | category | flops | bytes accessed | tf_op | source)
XLA Modules:
  0.0 60.1 jit_solution(488934363798744185)
XLA Ops:
  0.6 0.0 copy-start
  0.6 1.1 %copy-done = f32[3,8,16,512]{3,2,1,0:T(8,128)S(1)} copy-done((f32[3,8,16,512]{3,2,1,0:T(8,128)S(1)}, f32[3,8,16,512]{3,2,1,0:T(8,128)}, u32[]{:S(2)}) %copy-start) | copy-done | bytes 786456
  1.8 0.2 shard_map.50
  1.9 3.0 %collective-permute-start = (f32[16,512]{1,0:T(8,128)S(1)}, f32[16,512]{1,0:T(8,128)S(1)}, u32[]{:S(2)}, u32[]{:S(2)}) collective-permute-start(f32[16,512]{1,0:T(8,128)S(1)} %get-tuple-element.20), channel_id=1, source_target_pairs={{0,4},{4,8},{8,12},{12,16},{16,20},{20,24},{24,28},{28,0},{1,5},{5... | collective-permute-start | bytes 98312 | tf_op jit(solution)/shard_map/ppermute | solution.py:314
  5.0 0.0 collective-permute-start.1
  5.0 0.0 copy-start.1
  5.0 0.9 %copy-done.1 = f32[8,16,512]{2,1,0:T(8,128)S(1)} copy-done((f32[8,16,512]{2,1,0:T(8,128)S(1)}, f32[8,16,512]{2,1,0:T(8,128)}, u32[]{:S(2)}) %copy-start.1) | copy-done | bytes 262168
  5.9 0.9 %copy-done.2 = s32[8,16,512]{2,1,0:T(8,128)S(1)} copy-done((s32[8,16,512]{2,1,0:T(8,128)S(1)}, s32[8,16,512]{2,1,0:T(8,128)}, u32[]{:S(2)}) %copy-start.2) | copy-done | bytes 262168
  6.9 1.2 %collective-permute-done.1.sy_low = f32[8,512]{1,0:T(8,128)S(1)} collective-permute-done((f32[8,512]{1,0:T(8,128)S(1)}, f32[8,512]{1,0:T(8,128)S(1)}, u32[]{:S(2)}, u32[]{:S(2)}) %collective-permute-start.1) | collective-permute-done | bytes 16416 | tf_op jit(solution)/shard_map/ppermute | solution.py:314
  8.1 1.8 %collective-permute-done.sz_low = f32[16,512]{1,0:T(8,128)S(1)} collective-permute-done((f32[16,512]{1,0:T(8,128)S(1)}, f32[16,512]{1,0:T(8,128)S(1)}, u32[]{:S(2)}, u32[]{:S(2)}) %collective-permute-start) | collective-permute-done | bytes 32800 | tf_op jit(solution)/shard_map/ppermute | solution.py:314
  9.9 0.5 shard_map.52
  10.4 0.1 collective-permute-start.2
  10.5 4.7 %collective-permute-start.3 = (f32[192,512]{1,0:T(8,128)S(1)}, f32[192,512]{1,0:T(8,128)S(1)}, u32[]{:S(2)}, u32[]{:S(2)}) collective-permute-start(f32[192,512]{1,0:T(8,128)S(1)} %get-tuple-element.23), channel_id=1, source_target_pairs={{0,28},{4,0},{8,4},{12,8},{16,12},{20,16},{24,20},{28,24},{1,29},{... | collective-permute-start | bytes 1179656 | tf_op jit(solution)/shard_map/ppermute | solution.py:314
  15.2 12.5 %collective-permute-done.2.zb = f32[192,512]{1,0:T(8,128)S(1)} collective-permute-done((f32[192,512]{1,0:T(8,128)S(1)}, f32[192,512]{1,0:T(8,128)S(1)}, u32[]{:S(2)}, u32[]{:S(2)}) %collective-permute-start.2) | collective-permute-done | bytes 393248 | tf_op jit(solution)/shard_map/ppermute | solution.py:314
  27.7 2.2 %collective-permute-done.3.za = f32[192,512]{1,0:T(8,128)S(1)} collective-permute-done((f32[192,512]{1,0:T(8,128)S(1)}, f32[192,512]{1,0:T(8,128)S(1)}, u32[]{:S(2)}, u32[]{:S(2)}) %collective-permute-start.3) | collective-permute-done | bytes 393248 | tf_op jit(solution)/shard_map/ppermute | solution.py:314
  29.9 0.2 shard_map.53
  30.1 0.1 collective-permute-start.4
  30.2 0.7 %collective-permute-start.5 = (f32[160,512]{1,0:T(8,128)S(1)}, f32[160,512]{1,0:T(8,128)S(1)}, u32[]{:S(2)}, u32[]{:S(2)}) collective-permute-start(f32[160,512]{1,0:T(8,128)S(1)} %get-tuple-element.27), channel_id=1, source_target_pairs={{0,0},{1,2},{2,1},{3,3},{4,4},{5,6},{6,5},{7,7},{8,8},{9,10},{10,9... | collective-permute-start | bytes 983048 | tf_op jit(solution)/shard_map/ppermute | solution.py:322
  30.9 7.2 %shard_map.54 = (f32[9,20,4,32,128]{4,3,2,1,0:T(8,128)S(1)}, s32[4,20,4,32,128]{4,3,2,1,0:T(8,128)S(1)}) custom-call(s32[20,16,512]{2,1,0:T(8,128)S(1)} %get-tuple-element.28.d_ext, f32[20,16,512]{2,1,0:T(8,128)S(1)} %get-tuple-element.29.m_ext), custom_call_target="tpu_custom_call" | custom-call | flops 20000000 | bytes 20000000 | tf_op jit(solution)/shard_map/pallas_call | solution.py:327
  38.1 0.0 collective-permute-done.4.re
  38.1 0.0 collective-permute-done.5.ro
  38.1 9.0 %shard_map.55 = (s32[8,16,512]{2,1,0:T(8,128)}, s32[32,1,128]{2,1,0:T(1,128)S(1)}, f32[9,20,4,32,128]{4,3,2,1,0:T(8,128)S(1)}, s32[4,20,4,32,128]{4,3,2,1,0:T(8,128)S(1)}) custom-call(f32[160,512]{1,0:T(8,128)S(1)} %collective-permute-done.4.re, f32[160,512]{1,0:T(8,128)S(1)} %collective-permute-done.5.ro, ...), custom_call_target="tpu_custom_call", output_to_operand_aliasing={{2}: (2, {}), {3}: (3, {})} | custom-call | flops 20000000 | bytes 20000000 | tf_op jit(solution)/shard_map/pallas_call | solution.py:327
  47.1 12.5 %all_to_all.5 = s32[32,1,128]{2,1,0:T(1,128)S(1)} all-to-all(s32[32,1,128]{2,1,0:T(1,128)S(1)} %get-tuple-element.33), channel_id=1, replica_groups=mesh['gz'=8,'gy'=4] {'gz','gy'}, dimensions={0} | all-to-all | bytes 32768 | tf_op jit(solution)/shard_map/all_to_all | solution.py:383
  59.6 0.6 reduce_sum.9
  (2 shorter events, 0.0 us)
Async XLA Ops:
  0.6 1.1 %copy-start = (f32[3,8,16,512]{3,2,1,0:T(8,128)S(1)}, f32[3,8,16,512]{3,2,1,0:T(8,128)}, u32[]{:S(2)}) copy-start(f32[3,8,16,512]{3,2,1,0:T(8,128)} %seeds.1) | copy-start | bytes 2359300
  1.9 8.0 %collective-permute-start = (f32[16,512]{1,0:T(8,128)S(1)}, f32[16,512]{1,0:T(8,128)S(1)}, u32[]{:S(2)}, u32[]{:S(2)}) collective-permute-start(f32[16,512]{1,0:T(8,128)S(1)} %get-tuple-element.20), channel_id=1, source_target_pairs={{0,4},{4,8},{8,12},{12,16},{16,20},{20,24},{24,28},{28,0},{1,5},{5... | collective-permute-start | bytes 98312 | tf_op jit(solution)/shard_map/ppermute | solution.py:314
  5.0 3.2 %collective-permute-start.1 = (f32[8,512]{1,0:T(8,128)S(1)}, f32[8,512]{1,0:T(8,128)S(1)}, u32[]{:S(2)}, u32[]{:S(2)}) collective-permute-start(f32[8,512]{1,0:T(8,128)S(1)} %get-tuple-element.21), channel_id=1, source_target_pairs={{0,1},{1,2},{2,3},{3,0},{4,5},{5,6},{6,7},{7,4},{8,9},{9,10},{10,1... | collective-permute-start | bytes 49160 | tf_op jit(solution)/shard_map/ppermute | solution.py:314
  5.0 1.0 %copy-start.1 = (f32[8,16,512]{2,1,0:T(8,128)S(1)}, f32[8,16,512]{2,1,0:T(8,128)}, u32[]{:S(2)}) copy-start(f32[8,16,512]{2,1,0:T(8,128)} %ranks.1) | copy-start | bytes 786436
  5.9 0.9 %copy-start.2 = (s32[8,16,512]{2,1,0:T(8,128)S(1)}, s32[8,16,512]{2,1,0:T(8,128)}, u32[]{:S(2)}) copy-start(s32[8,16,512]{2,1,0:T(8,128)} %flags.1) | copy-start | bytes 786436
  10.4 17.2 %collective-permute-start.2 = (f32[192,512]{1,0:T(8,128)S(1)}, f32[192,512]{1,0:T(8,128)S(1)}, u32[]{:S(2)}, u32[]{:S(2)}) collective-permute-start(f32[192,512]{1,0:T(8,128)S(1)} %get-tuple-element.22), channel_id=1, source_target_pairs={{0,4},{4,8},{8,12},{12,16},{16,20},{20,24},{24,28},{28,0},{1,5},{5... | collective-permute-start | bytes 1179656 | tf_op jit(solution)/shard_map/ppermute | solution.py:314
  10.5 19.4 %collective-permute-start.3 = (f32[192,512]{1,0:T(8,128)S(1)}, f32[192,512]{1,0:T(8,128)S(1)}, u32[]{:S(2)}, u32[]{:S(2)}) collective-permute-start(f32[192,512]{1,0:T(8,128)S(1)} %get-tuple-element.23), channel_id=1, source_target_pairs={{0,28},{4,0},{8,4},{12,8},{16,12},{20,16},{24,20},{28,24},{1,29},{... | collective-permute-start | bytes 1179656 | tf_op jit(solution)/shard_map/ppermute | solution.py:314
  30.1 8.0 %collective-permute-start.4 = (f32[160,512]{1,0:T(8,128)S(1)}, f32[160,512]{1,0:T(8,128)S(1)}, u32[]{:S(2)}, u32[]{:S(2)}) collective-permute-start(f32[160,512]{1,0:T(8,128)S(1)} %get-tuple-element.26), channel_id=1, source_target_pairs={{0,1},{1,0},{2,3},{3,2},{4,5},{5,4},{6,7},{7,6},{8,9},{9,8},{10,11... | collective-permute-start | bytes 983048 | tf_op jit(solution)/shard_map/ppermute | solution.py:322
  30.2 7.9 %collective-permute-start.5 = (f32[160,512]{1,0:T(8,128)S(1)}, f32[160,512]{1,0:T(8,128)S(1)}, u32[]{:S(2)}, u32[]{:S(2)}) collective-permute-start(f32[160,512]{1,0:T(8,128)S(1)} %get-tuple-element.27), channel_id=1, source_target_pairs={{0,0},{1,2},{2,1},{3,3},{4,4},{5,6},{6,5},{7,7},{8,8},{9,10},{10,9... | collective-permute-start | bytes 983048 | tf_op jit(solution)/shard_map/ppermute | solution.py:322

commit v3 on v2

--- a/solution.py
+++ b/solution.py
@@ -114,7 +114,7 @@
     return patterns, measures, -(-at // T) * T
 
 
-def planes_kernel(zb, za, d_own, m_own, ye, yo, d_ext, m_ext):
+def planes_kernel(zb, za, d_own, m_own, yo, ye, d_ext, m_ext):
     depth, rows, _ = m_own.shape
     zlo, zhi = neighbours("gz")
     even = lax.axis_index("gy") % 2 == 0
@@ -169,50 +169,77 @@
     return jnp.where(lane == 0, jnp.concatenate([r[-1:], r[:-1]], 0), r)
 
 
-def set_caps(fw, iw, i, at, n):
-    def d_at(plane, row):
-        return iw[PATTERN, plane, :, pl.ds(row, n), :]
-
-    d = d_at(i, at)
-    others = (x_next(d), x_prev(d), d_at(i, at + 1), d_at(i, at - 1), d_at(i + 1, at), d_at(i - 1, at))
-    for j, other in enumerate(others):
-        linked = (d & (1 << j)) | (other & (1 << (j ^ 1)))
-        fw[CAPS + j, i, :, pl.ds(at, n), :] = jnp.where(linked != 0, BIG, -3.0)
-
-
-def select(fw, iw, step, i, at, n):
-    def cap(j):
-        return fw[CAPS + j, i, :, pl.ds(at, n), :]
-
-    def p_at(plane, row):
-        return fw[STATE + step, plane, :, pl.ds(row, n), :]
-
-    p = p_at(i, at)
-    near = jnp.maximum(jnp.minimum(x_next(p), cap(0)), jnp.minimum(x_prev(p), cap(1)))
-    near = jnp.maximum(near, jnp.minimum(p_at(i, at + 1), cap(2)))
-    near = jnp.maximum(near, jnp.minimum(p_at(i, at - 1), cap(3)))
-    near = jnp.maximum(near, jnp.minimum(p_at(i + 1, at), cap(4)))
-    near = jnp.maximum(near, jnp.minimum(p_at(i - 1, at), cap(5)))
-    new = (p >= 0) & (p > near)
-    iw[NEW + 1 + step, i, :, pl.ds(at, n), :] = jnp.where(new, 63, 0)
-
-
-def hits(fw, iw, step, i, at, n):
+def set_caps(fw, iw, sites):
+    found = []
+    for i, at in sites:
+
+        def d_at(plane, row):
+            return iw[PATTERN, plane, :, pl.ds(row, T), :]
+
+        d = d_at(i, at)
+        others = (x_next(d), x_prev(d), d_at(i, at + 1), d_at(i, at - 1), d_at(i + 1, at), d_at(i - 1, at))
+        found.append([(d & (1 << j)) | (other & (1 << (j ^ 1))) for j, other in enumerate(others)])
+    caps = [[jnp.where(linked != 0, BIG, -3.0) for linked in some] for some in found]
+    for (i, at), some in zip(sites, caps):
+        for j, cap in enumerate(some):
+            fw[CAPS + j, i, :, pl.ds(at, T), :] = cap
+    return caps
+
+
+def caps_of(fw, sites):
+    return [[fw[CAPS + j, i, :, pl.ds(at, T), :] for j in range(6)] for i, at in sites]
+
+
+def select(fw, iw, step, sites, caps):
+    found = []
+    for (i, at), cap in zip(sites, caps):
+
+        def p_at(plane, row):
+            return fw[STATE + step, plane, :, pl.ds(row, T), :]
+
+        p = p_at(i, at)
+        y = jnp.maximum(jnp.minimum(p_at(i, at + 1), cap[2]), jnp.minimum(p_at(i, at - 1), cap[3]))
+        z = jnp.maximum(jnp.minimum(p_at(i + 1, at), cap[4]), jnp.minimum(p_at(i - 1, at), cap[5]))
+        x = jnp.maximum(jnp.minimum(x_next(p), cap[0]), jnp.minimum(x_prev(p), cap[1]))
+        found.append((p >= 0) & (p > jnp.maximum(jnp.maximum(y, z), x)))
+    for (i, at), new in zip(sites, found):
+        iw[NEW + 1 + step, i, :, pl.ds(at, T), :] = jnp.where(new, 63, 0)
+
+
+def hits(fw, iw, step, i, at):
     def n_at(plane, row):
-        return iw[NEW + 1 + step, plane, :, pl.ds(row, n), :]
+        return iw[NEW + 1 + step, plane, :, pl.ds(row, T), :]
 
     new = n_at(i, at)
-    hit = (x_next(new) & 1) | (x_prev(new) & 2)
-    hit |= (n_at(i, at + 1) & 4) | (n_at(i, at - 1) & 8)
-    hit |= (n_at(i + 1, at) & 16) | (n_at(i - 1, at) & 32)
-    hit &= iw[PATTERN, i, :, pl.ds(at, n), :]
-    return new != 0, hit != 0, fw[STATE + step, i, :, pl.ds(at, n), :]
-
-
-def update(fw, iw, step, i, at, n):
-    new, hit, p = hits(fw, iw, step, i, at, n)
-    p = jnp.where(new, -2.0, jnp.where((p >= 0) & hit, -1.0, p))
-    fw[STATE + step + 1, i, :, pl.ds(at, n), :] = p
+    hit = ((n_at(i, at + 1) & 4) | (n_at(i, at - 1) & 8)) | ((n_at(i + 1, at) & 16) | (n_at(i - 1, at) & 32))
+    hit |= (x_next(new) & 1) | (x_prev(new) & 2)
+    hit &= iw[PATTERN, i, :, pl.ds(at, T), :]
+    return new != 0, hit != 0, fw[STATE + step, i, :, pl.ds(at, T), :]
+
+
+def update(fw, iw, step, sites):
+    found = []
+    for i, at in sites:
+        new, hit, p = hits(fw, iw, step, i, at)
+        found.append(jnp.where(new, -2.0, jnp.where((p >= 0) & hit, -1.0, p)))
+    for (i, at), p in zip(sites, found):
+        fw[STATE + step + 1, i, :, pl.ds(at, T), :] = p
+
+
+def stages(fw, iw, depth, rows_of):
+    for stage in range(2 * ROUNDS - 1):
+        step, reach = stage // 2, H - 1 - stage
+        each = max(n for n in (1, 2, 3, 4) if (depth + 2 * reach) % n == 0)
+
+        @pl.loop(H - reach, H + depth + reach, step=each)
+        def _(i):
+            sites = [(i + j, at) for j in range(each) for at in rows_of(stage)]
+            if stage == 0:
+                select(fw, iw, step, sites, set_caps(fw, iw, sites))
+            elif stage % 2 == 0:
+                select(fw, iw, step, sites, caps_of(fw, sites))
+            else:
+                update(fw, iw, step, sites)
 
 
 def inner_kernel(d_ext, m_ext, fw, iw):
@@ -224,21 +251,10 @@
         iw[PATTERN, i, :, pl.ds(T, rows), :] = blocks(d_ext[i])
         fw[STATE, i, :, pl.ds(T, rows), :] = blocks(m_ext[i])
 
-    for stage in range(2 * ROUNDS - 1):
-        step, reach = stage // 2, H - 1 - stage
-
-        @pl.loop(H - reach, H + depth + reach)
-        def _(i):
-            for at in range(T, T + rows, T):
-                if stage == 0:
-                    set_caps(fw, iw, i, at, T)
-                if stage % 2 == 0:
-                    select(fw, iw, step, i, at, T)
-                else:
-                    update(fw, iw, step, i, at, T)
-
-
-def outer_kernel(re, ro, fw_in, iw_in, state_out, count_out, fw, iw):
+    stages(fw, iw, depth, lambda stage: range(T, T + rows, T))
+
+
+def outer_kernel(ro, re, fw_in, iw_in, state_out, count_out, fw, iw):
     del fw_in, iw_in
     depth, rows, width = state_out.shape
     planes = depth + 2 * H
@@ -274,23 +290,12 @@
             here = pl.ds(at, T)
             fw[STATE, i, :, here, :] = scaled(fw[STATE, i, :, here, :], bit)
 
-    for stage in range(2 * ROUNDS - 1):
-        step, reach = stage // 2, H - 1 - stage
-
-        @pl.loop(H - reach, H + depth + reach)
-        def _(i):
-            for at in (low(stage), high(stage)):
-                if stage == 0:
-                    set_caps(fw, iw, i, at, T)
-                if stage % 2 == 0:
-                    select(fw, iw, step, i, at, T)
-                else:
-                    update(fw, iw, step, i, at, T)
+    stages(fw, iw, depth, lambda stage: (low(stage), high(stage)))
 
     def finish(z, totals):
         totals = list(totals)
         for at in range(0, rows, T):
-            new, hit, p = hits(fw, iw, ROUNDS - 1, z + H, T + at, T)
+            new, hit, p = hits(fw, iw, ROUNDS - 1, z + H, T + at)
             old = jnp.where(p >= 0, jnp.where(hit, 1, 0), jnp.where(p == -2.0, 2, 1))
             state = jnp.where(new, 2, old)
             for j in range(width // L):
@@ -364,18 +369,18 @@
     za = shift(dn, "gz", -1)
     message = of((y_layout(depth)[2], width), F32)
     ext = (planes, rows, width)
-    ye, yo, d_ext, m_ext = call(
+    yo, ye, d_ext, m_ext = call(
         planes_kernel, [message, message, of(ext, I32), of(ext, F32)], (zb, za, d_own, m_own), 8, 4000000
     )
+    ro = swap(yo, "gy", 1)
     re = swap(ye, "gy", 0)
-    ro = swap(yo, "gy", 1)
     cells = (planes, width // L, rows + 2 * T, L)
     works = [of((STATE + ROUNDS,) + cells, F32), of((NEW + 1 + ROUNDS,) + cells, I32)]
     fw, iw = call(inner_kernel, works, (d_ext, m_ext), 8, 20000000)
     state, counts, _, _ = call(
         outer_kernel,
         [of(ranks.shape, I32), of((devices, 1, L), I32)] + works,
-        (re, ro, fw, iw),
+        (ro, re, fw, iw),
         8,
         20000000,
         input_output_aliases={2: 2, 3: 3},

time: 60.4 us -> 55.3 us (0.916)
  Pallas kernels: 17.1 us -> 10.2 us
  starting transfers between devices: 8.54 us -> 10.5 us
    pallas_call x6, Pallas kernels: 17.1 us -> 10.2 us  [call(): pl.pallas_call(kernel, out_shape=outs, in_specs=specs, out_specs=[vmem()]...]
    ppermute x2, starting transfers between devices: 0.75 us -> 2.7 us  [swap(): return lax.ppermute(value, axis, pairs)]
  transfers between devices with their start and end apart: 6 -> 6, of which waited for: 4 -> 4; matrix products, arithmetic and copies ran while one was open for 0% -> 0% of each run, Pallas kernels for 12% -> 7%
where the time goes in v3:
time: 55.3 us; the launch traced here: 55.1 us
  waiting for transfers between devices  17.7 us (32%)
  blocking collectives  12.5 us (23%)
  starting transfers between devices  10.5 us (19%)
  Pallas kernels  10.2 us (18%)
  local copies, waits for them, and re-layouts  3.03 us (5%)
  between operations  0.7 us (1%)
  other arithmetic  0.56 us (1%)
    ppermute x4, waiting for transfers between devices, shift(): lax.ppermute(value, axis, [(i, (i + step) % count) for i in range(count)])  17.6 us
    all_to_all x1, blocking collectives, per_device(): everyone = lax.all_to_all(counts, ('gz', 'gy'), 0, 0, tiled=True)  12.5 us
    pallas_call x6, Pallas kernels, call(): pl.pallas_call(kernel, out_shape=outs, in_specs=specs, out_specs=[vmem()]...  10.2 us
    ppermute x4, starting transfers between devices, shift(): lax.ppermute(value, axis, [(i, (i + step) % count) for i in range(count)])  7.79 us
    unnamed x6, local copies, waits for them, and re-layouts  3.03 us
    ppermute x2, starting transfers between devices, swap(): return lax.ppermute(value, axis, pairs)  2.7 us
  transfers between devices with their start and end apart: 6, of which 4 were waited for; matrix products, arithmetic and copies ran while one was open for 0% of the time, Pallas kernels for 7%

profile of v3, /device:TPU:0, one launch (start us, length us, event | category | flops | bytes accessed | tf_op | source)
XLA Modules:
  0.0 55.1 jit_solution(18204328034112399762)
XLA Ops:
  0.6 0.0 copy-start
  0.6 1.1 %copy-done = f32[3,8,16,512]{3,2,1,0:T(8,128)S(1)} copy-done((f32[3,8,16,512]{3,2,1,0:T(8,128)S(1)}, f32[3,8,16,512]{3,2,1,0:T(8,128)}, u32[]{:S(2)}) %copy-start) | copy-done | bytes 786456
  1.8 0.2 shard_map.50
  1.9 3.0 %collective-permute-start = (f32[16,512]{1,0:T(8,128)S(1)}, f32[16,512]{1,0:T(8,128)S(1)}, u32[]{:S(2)}, u32[]{:S(2)}) collective-permute-start(f32[16,512]{1,0:T(8,128)S(1)} %get-tuple-element.20), channel_id=1, source_target_pairs={{0,4},{4,8},{8,12},{12,16},{16,20},{20,24},{24,28},{28,0},{1,5},{5... | collective-permute-start | bytes 98312 | tf_op jit(solution)/shard_map/ppermute | solution.py:319
  5.0 0.0 collective-permute-start.1
  5.0 0.0 copy-start.1
  5.0 0.9 %copy-done.1 = f32[8,16,512]{2,1,0:T(8,128)S(1)} copy-done((f32[8,16,512]{2,1,0:T(8,128)S(1)}, f32[8,16,512]{2,1,0:T(8,128)}, u32[]{:S(2)}) %copy-start.1) | copy-done | bytes 262168
  5.9 0.9 %copy-done.2 = s32[8,16,512]{2,1,0:T(8,128)S(1)} copy-done((s32[8,16,512]{2,1,0:T(8,128)S(1)}, s32[8,16,512]{2,1,0:T(8,128)}, u32[]{:S(2)}) %copy-start.2) | copy-done | bytes 262168
  6.9 1.2 %collective-permute-done.1.sy_low = f32[8,512]{1,0:T(8,128)S(1)} collective-permute-done((f32[8,512]{1,0:T(8,128)S(1)}, f32[8,512]{1,0:T(8,128)S(1)}, u32[]{:S(2)}, u32[]{:S(2)}) %collective-permute-start.1) | collective-permute-done | bytes 16416 | tf_op jit(solution)/shard_map/ppermute | solution.py:319
  8.1 1.8 %collective-permute-done.sz_low = f32[16,512]{1,0:T(8,128)S(1)} collective-permute-done((f32[16,512]{1,0:T(8,128)S(1)}, f32[16,512]{1,0:T(8,128)S(1)}, u32[]{:S(2)}, u32[]{:S(2)}) %collective-permute-start) | collective-permute-done | bytes 32800 | tf_op jit(solution)/shard_map/ppermute | solution.py:319
  9.9 0.5 shard_map.52
  10.4 0.1 collective-permute-start.2
  10.5 4.7 %collective-permute-start.3 = (f32[192,512]{1,0:T(8,128)S(1)}, f32[192,512]{1,0:T(8,128)S(1)}, u32[]{:S(2)}, u32[]{:S(2)}) collective-permute-start(f32[192,512]{1,0:T(8,128)S(1)} %get-tuple-element.23), channel_id=1, source_target_pairs={{0,28},{4,0},{8,4},{12,8},{16,12},{20,16},{24,20},{28,24},{1,29},{... | collective-permute-start | bytes 1179656 | tf_op jit(solution)/shard_map/ppermute | solution.py:319
  15.2 12.5 %collective-permute-done.2.zb = f32[192,512]{1,0:T(8,128)S(1)} collective-permute-done((f32[192,512]{1,0:T(8,128)S(1)}, f32[192,512]{1,0:T(8,128)S(1)}, u32[]{:S(2)}, u32[]{:S(2)}) %collective-permute-start.2) | collective-permute-done | bytes 393248 | tf_op jit(solution)/shard_map/ppermute | solution.py:319
  27.7 2.2 %collective-permute-done.3.za = f32[192,512]{1,0:T(8,128)S(1)} collective-permute-done((f32[192,512]{1,0:T(8,128)S(1)}, f32[192,512]{1,0:T(8,128)S(1)}, u32[]{:S(2)}, u32[]{:S(2)}) %collective-permute-start.3) | collective-permute-done | bytes 393248 | tf_op jit(solution)/shard_map/ppermute | solution.py:319
  29.9 0.2 shard_map.53
  30.1 0.7 %collective-permute-start.4 = (f32[160,512]{1,0:T(8,128)S(1)}, f32[160,512]{1,0:T(8,128)S(1)}, u32[]{:S(2)}, u32[]{:S(2)}) collective-permute-start(f32[160,512]{1,0:T(8,128)S(1)} %get-tuple-element.26), channel_id=1, source_target_pairs={{0,0},{1,2},{2,1},{3,3},{4,4},{5,6},{6,5},{7,7},{8,8},{9,10},{10,9... | collective-permute-start | bytes 983048 | tf_op jit(solution)/shard_map/ppermute | solution.py:327
  30.8 2.0 %collective-permute-start.5 = (f32[160,512]{1,0:T(8,128)S(1)}, f32[160,512]{1,0:T(8,128)S(1)}, u32[]{:S(2)}, u32[]{:S(2)}) collective-permute-start(f32[160,512]{1,0:T(8,128)S(1)} %get-tuple-element.27), channel_id=1, source_target_pairs={{0,1},{1,0},{2,3},{3,2},{4,5},{5,4},{6,7},{7,6},{8,9},{9,8},{10,11... | collective-permute-start | bytes 983048 | tf_op jit(solution)/shard_map/ppermute | solution.py:327
  32.8 3.7 %shard_map.54 = (f32[9,20,4,32,128]{4,3,2,1,0:T(8,128)S(1)}, s32[4,20,4,32,128]{4,3,2,1,0:T(8,128)S(1)}) custom-call(s32[20,16,512]{2,1,0:T(8,128)S(1)} %get-tuple-element.28.d_ext, f32[20,16,512]{2,1,0:T(8,128)S(1)} %get-tuple-element.29.m_ext), custom_call_target="tpu_custom_call" | custom-call | flops 20000000 | bytes 20000000 | tf_op jit(solution)/shard_map/pallas_call | solution.py:332
  36.5 0.0 collective-permute-done.4.ro
  36.5 0.0 collective-permute-done.5.re
  36.6 5.5 %shard_map.55 = (s32[8,16,512]{2,1,0:T(8,128)}, s32[32,1,128]{2,1,0:T(1,128)S(1)}, f32[9,20,4,32,128]{4,3,2,1,0:T(8,128)S(1)}, s32[4,20,4,32,128]{4,3,2,1,0:T(8,128)S(1)}) custom-call(f32[160,512]{1,0:T(8,128)S(1)} %collective-permute-done.4.ro, f32[160,512]{1,0:T(8,128)S(1)} %collective-permute-done.5.re, ...), custom_call_target="tpu_custom_call", output_to_operand_aliasing={{2}: (2, {}), {3}: (3, {})} | custom-call | flops 20000000 | bytes 20000000 | tf_op jit(solution)/shard_map/pallas_call | solution.py:332
  42.1 12.5 %all_to_all.5 = s32[32,1,128]{2,1,0:T(1,128)S(1)} all-to-all(s32[32,1,128]{2,1,0:T(1,128)S(1)} %get-tuple-element.33), channel_id=1, replica_groups=mesh['gz'=8,'gy'=4] {'gz','gy'}, dimensions={0} | all-to-all | bytes 32768 | tf_op jit(solution)/shard_map/all_to_all | solution.py:388
  54.5 0.6 %reduce_sum.9 = s32[128]{0:T(128)} reduce(s32[32,1,128]{2,1,0:T(1,128)S(1)} %all_to_all.5, s32[]{:T(128)} %constant.0.clone.1), dimensions={0,1}, to_apply=%region_0.0 | reduce | flops 3968 | bytes 16900 | tf_op jit(solution)/shard_map/reduce_sum | solution.py:389
  (2 shorter events, 0.0 us)
Async XLA Ops:
  0.6 1.1 %copy-start = (f32[3,8,16,512]{3,2,1,0:T(8,128)S(1)}, f32[3,8,16,512]{3,2,1,0:T(8,128)}, u32[]{:S(2)}) copy-start(f32[3,8,16,512]{3,2,1,0:T(8,128)} %seeds.1) | copy-start | bytes 2359300
  1.9 8.0 %collective-permute-start = (f32[16,512]{1,0:T(8,128)S(1)}, f32[16,512]{1,0:T(8,128)S(1)}, u32[]{:S(2)}, u32[]{:S(2)}) collective-permute-start(f32[16,512]{1,0:T(8,128)S(1)} %get-tuple-element.20), channel_id=1, source_target_pairs={{0,4},{4,8},{8,12},{12,16},{16,20},{20,24},{24,28},{28,0},{1,5},{5... | collective-permute-start | bytes 98312 | tf_op jit(solution)/shard_map/ppermute | solution.py:319
  5.0 3.2 %collective-permute-start.1 = (f32[8,512]{1,0:T(8,128)S(1)}, f32[8,512]{1,0:T(8,128)S(1)}, u32[]{:S(2)}, u32[]{:S(2)}) collective-permute-start(f32[8,512]{1,0:T(8,128)S(1)} %get-tuple-element.21), channel_id=1, source_target_pairs={{0,1},{1,2},{2,3},{3,0},{4,5},{5,6},{6,7},{7,4},{8,9},{9,10},{10,1... | collective-permute-start | bytes 49160 | tf_op jit(solution)/shard_map/ppermute | solution.py:319
  5.0 1.0 %copy-start.1 = (f32[8,16,512]{2,1,0:T(8,128)S(1)}, f32[8,16,512]{2,1,0:T(8,128)}, u32[]{:S(2)}) copy-start(f32[8,16,512]{2,1,0:T(8,128)} %ranks.1) | copy-start | bytes 786436
  5.9 0.9 %copy-start.2 = (s32[8,16,512]{2,1,0:T(8,128)S(1)}, s32[8,16,512]{2,1,0:T(8,128)}, u32[]{:S(2)}) copy-start(s32[8,16,512]{2,1,0:T(8,128)} %flags.1) | copy-start | bytes 786436
  10.4 17.2 %collective-permute-start.2 = (f32[192,512]{1,0:T(8,128)S(1)}, f32[192,512]{1,0:T(8,128)S(1)}, u32[]{:S(2)}, u32[]{:S(2)}) collective-permute-start(f32[192,512]{1,0:T(8,128)S(1)} %get-tuple-element.22), channel_id=1, source_target_pairs={{0,4},{4,8},{8,12},{12,16},{16,20},{20,24},{24,28},{28,0},{1,5},{5... | collective-permute-start | bytes 1179656 | tf_op jit(solution)/shard_map/ppermute | solution.py:319
  10.5 19.4 %collective-permute-start.3 = (f32[192,512]{1,0:T(8,128)S(1)}, f32[192,512]{1,0:T(8,128)S(1)}, u32[]{:S(2)}, u32[]{:S(2)}) collective-permute-start(f32[192,512]{1,0:T(8,128)S(1)} %get-tuple-element.23), channel_id=1, source_target_pairs={{0,28},{4,0},{8,4},{12,8},{16,12},{20,16},{24,20},{28,24},{1,29},{... | collective-permute-start | bytes 1179656 | tf_op jit(solution)/shard_map/ppermute | solution.py:319
  30.1 6.4 %collective-permute-start.4 = (f32[160,512]{1,0:T(8,128)S(1)}, f32[160,512]{1,0:T(8,128)S(1)}, u32[]{:S(2)}, u32[]{:S(2)}) collective-permute-start(f32[160,512]{1,0:T(8,128)S(1)} %get-tuple-element.26), channel_id=1, source_target_pairs={{0,0},{1,2},{2,1},{3,3},{4,4},{5,6},{6,5},{7,7},{8,8},{9,10},{10,9... | collective-permute-start | bytes 983048 | tf_op jit(solution)/shard_map/ppermute | solution.py:327
  30.8 5.8 %collective-permute-start.5 = (f32[160,512]{1,0:T(8,128)S(1)}, f32[160,512]{1,0:T(8,128)S(1)}, u32[]{:S(2)}, u32[]{:S(2)}) collective-permute-start(f32[160,512]{1,0:T(8,128)S(1)} %get-tuple-element.27), channel_id=1, source_target_pairs={{0,1},{1,0},{2,3},{3,2},{4,5},{5,4},{6,7},{7,6},{8,9},{9,8},{10,11... | collective-permute-start | bytes 983048 | tf_op jit(solution)/shard_map/ppermute | solution.py:327

commit v4 on v3

--- a/solution.py
+++ b/solution.py
@@ -8,6 +8,7 @@
 ROUNDS = 3
 H = 2 * ROUNDS
 T = 8
+RELAYED = 2
 L = 128
 BIG = 3.0e38
 F32, I32 = jnp.float32, jnp.int32
@@ -61,7 +62,14 @@
     packed[...] = jnp.where(f == 0, ranks[...], jnp.where(f == 2, -2.0, -1.0))
 
 
-def strength_kernel(twice, rm, packed, sz_low, sy_low, up, dn, d_out, m_out):
+def plane_lists(depth):
+    both = list(range(H - RELAYED, H))
+    partner = [z for z in range(depth - H, depth) if z not in both]
+    other = list(range(H - RELAYED))
+    return both, partner, other
+
+
+def strength_kernel(twice, rm, packed, sz_low, sy_low, both, partner, other, d_out, m_out):
     depth, rows, width = packed.shape
     zlo, _ = neighbours("gz")
     ylo, _ = neighbours("gy")
@@ -93,13 +101,21 @@
         p = packed[z]
         m = jnp.where(p >= 0, p * (1 << many).astype(F32), p)
         m_out[z] = m
-        k = depth - z
-        if k <= H:
-            up[pl.ds((k - 1) * rows, rows), :] = d.astype(F32)
-            up[pl.ds((H + k - 1) * rows, rows), :] = m
-        if z < H:
-            dn[pl.ds(z * rows, rows), :] = d.astype(F32)
-            dn[pl.ds((H + z) * rows, rows), :] = m
+    even = lax.axis_index("gz") % 2 == 0
+
+    def send(place):
+        for ref, zs in zip((both, partner, other), plane_lists(depth)):
+            for j, z in enumerate(zs):
+                ref[pl.ds(j * rows, rows), :] = d_out[place(z)].astype(F32)
+                ref[pl.ds((len(zs) + j) * rows, rows), :] = m_out[place(z)]
+
+    @pl.when(even)
+    def _():
+        send(lambda z: z)
+
+    @pl.when(jnp.logical_not(even))
+    def _():
+        send(lambda z: depth - 1 - z)
 
 
 def y_layout(depth):
@@ -114,16 +130,25 @@
     return patterns, measures, -(-at // T) * T
 
 
-def planes_kernel(zb, za, d_own, m_own, yo, ye, d_ext, m_ext):
+def planes_kernel(both, partner, other, relayed, d_own, m_own, yo, ye, d_ext, m_ext):
     depth, rows, _ = m_own.shape
     zlo, zhi = neighbours("gz")
+    above = lax.axis_index("gz") % 2 == 0
     even = lax.axis_index("gy") % 2 == 0
-    for k in range(1, H + 1):
-        at, am = pl.ds((k - 1) * rows, rows), pl.ds((H + k - 1) * rows, rows)
-        d_ext[H - k] = jnp.where(zlo, zb[at, :], 0.0).astype(I32)
-        d_ext[H + depth + k - 1] = jnp.where(zhi, za[at, :], 0.0).astype(I32)
-        m_ext[H - k] = zb[am, :]
-        m_ext[H + depth + k - 1] = za[am, :]
+
+    def put(ref, zs, above, distance):
+        for j, z in enumerate(zs):
+            k = distance(z)
+            i = jnp.where(above, H + depth + k - 1, H - k)
+            d = ref[pl.ds(j * rows, rows), :]
+            d_ext[i] = jnp.where((above & zhi) | (jnp.logical_not(above) & zlo), d, 0.0).astype(I32)
+            m_ext[i] = ref[pl.ds((len(zs) + j) * rows, rows), :]
+
+    for_both, for_partner, for_other = plane_lists(depth)
+    put(both, for_both, above, lambda z: depth - z)
+    put(partner, for_partner, above, lambda z: depth - z)
+    put(other, for_other, jnp.logical_not(above), lambda z: z + 1)
+    put(relayed, for_both, jnp.logical_not(above), lambda z: z + 1)
     for z in range(depth):
         d_ext[H + z] = d_own[z]
         m_ext[H + z] = m_own[z]
@@ -327,6 +352,12 @@
     return lax.ppermute(value, axis, pairs)
 
 
+def relay(value, axis):
+    last = lax.axis_size(axis) - 1
+    pairs = [(i, min(i + 2, last) if i % 2 == 0 else max(i - 2, 0)) for i in range(last + 1)]
+    return lax.ppermute(value, axis, pairs)
+
+
 def call(kernel, outs, args, limit, cost, **more):
     specs = more.pop("in_specs", [vmem()] * len(args))
     return pl.pallas_call(
@@ -342,7 +373,7 @@
 
 def per_device(ranks, seeds, flags):
     depth, rows, width = ranks.shape
-    assert depth >= H and rows >= 2 * T and T == H + 2 and width % L == 0
+    assert H + RELAYED <= depth + 1 <= 2 * H and lax.axis_size("gz") % 2 == 0 and rows >= 2 * T and T == H + 2 and width % L == 0
     planes = depth + 2 * H
     devices = lax.axis_size("gz") * lax.axis_size("gy")
     of = jax.ShapeDtypeStruct
@@ -357,20 +388,23 @@
     sz_low = shift(sz_top, "gz", 1)
     sy_low = shift(sy_last, "gy", 1)
     (packed,) = call(packed_kernel, own, (ranks, flags), 8, 4000000)
-    message = of((2 * H * rows, width), F32)
-    up, dn, d_own, m_own = call(
+    messages = [of((2 * len(zs) * rows, width), F32) for zs in plane_lists(depth)]
+    both, partner, other, d_own, m_own = call(
         strength_kernel,
-        [message, message, of(ranks.shape, I32)] + own,
+        messages + [of(ranks.shape, I32)] + own,
         (twice, rm, packed, sz_low, sy_low),
         8,
         4000000,
     )
-    zb = shift(up, "gz", 1)
-    za = shift(dn, "gz", -1)
+    both = swap(both, "gz", 0)
+    partner = swap(partner, "gz", 0)
+    other, both = lax.optimization_barrier((other, both))
+    relayed = relay(both, "gz")
+    other = swap(other, "gz", 1)
     message = of((y_layout(depth)[2], width), F32)
     ext = (planes, rows, width)
     yo, ye, d_ext, m_ext = call(
-        planes_kernel, [message, message, of(ext, I32), of(ext, F32)], (zb, za, d_own, m_own), 8, 4000000
+        planes_kernel, [message, message, of(ext, I32), of(ext, F32)], (both, partner, other, relayed, d_own, m_own), 8, 4000000
     )
     ro = swap(yo, "gy", 1)
     re = swap(ye, "gy", 0)

time: 55.3 us -> 51.7 us (0.935)
  waiting for transfers between devices: 17.7 us -> 11.9 us
  blocking collectives: 12.5 us -> 14.4 us
    ppermute x4 -> x2, waiting for transfers between devices: 17.6 us -> 2.99 us  [shift(): lax.ppermute(value, axis, [(i, (i + step) % count) for i in range(count)])]
    ppermute x2 -> x5, waiting for transfers between devices: 0.01 us -> 5.94 us  [swap(): return lax.ppermute(value, axis, pairs)]
    ppermute x4 -> x2, starting transfers between devices: 7.79 us -> 3.02 us  [shift(): lax.ppermute(value, axis, [(i, (i + step) % count) for i in range(count)])]
    ppermute x0 -> x1, waiting for transfers between devices: none -> 3 us  [relay(): return lax.ppermute(value, axis, pairs)]
    ppermute x0 -> x1, starting transfers between devices: none -> 2.75 us  [relay(): return lax.ppermute(value, axis, pairs)]
    ppermute x2 -> x5, starting transfers between devices: 2.7 us -> 4.79 us  [swap(): return lax.ppermute(value, axis, pairs)]
    all_to_all x1, blocking collectives: 12.5 us -> 14.4 us  [per_device(): everyone = lax.all_to_all(counts, ('gz', 'gy'), 0, 0, tiled=True)]
  transfers between devices with their start and end apart: 6 -> 8, of which waited for: 4 -> 5; matrix products, arithmetic and copies ran while one was open for 0% -> 0% of each run, Pallas kernels for 7% -> 7%
where the time goes in v4:
time: 51.7 us; the launch traced here: 51.4 us
  blocking collectives  14.4 us (28%)
  waiting for transfers between devices  11.9 us (23%)
  starting transfers between devices  10.6 us (21%)
  Pallas kernels  10.2 us (20%)
  local copies, waits for them, and re-layouts  3.03 us (6%)
  between operations  0.72 us (1%)
  other arithmetic  0.56 us (1%)
    all_to_all x1, blocking collectives, per_device(): everyone = lax.all_to_all(counts, ('gz', 'gy'), 0, 0, tiled=True)  14.4 us
    pallas_call x6, Pallas kernels, call(): pl.pallas_call(kernel, out_shape=outs, in_specs=specs, out_specs=[vmem()]...  10.2 us
    ppermute x5, waiting for transfers between devices, swap(): return lax.ppermute(value, axis, pairs)  5.94 us
    ppermute x5, starting transfers between devices, swap(): return lax.ppermute(value, axis, pairs)  4.79 us
    unnamed x6, local copies, waits for them, and re-layouts  3.03 us
    ppermute x2, starting transfers between devices, shift(): lax.ppermute(value, axis, [(i, (i + step) % count) for i in range(count)])  3.02 us
    ppermute x1, waiting for transfers between devices, relay(): return lax.ppermute(value, axis, pairs)  3 us
    ppermute x2, waiting for transfers between devices, shift(): lax.ppermute(value, axis, [(i, (i + step) % count) for i in range(count)])  2.99 us
  transfers between devices with their start and end apart: 8, of which 5 were waited for; matrix products, arithmetic and copies ran while one was open for 0% of the time, Pallas kernels for 7%

profile of v4, /device:TPU:0, one launch (start us, length us, event | category | flops | bytes accessed | tf_op | source)
XLA Modules:
  0.0 51.4 jit_solution(9491049153684021246)
XLA Ops:
  0.6 1.1 %copy-done = f32[3,8,16,512]{3,2,1,0:T(8,128)S(1)} copy-done((f32[3,8,16,512]{3,2,1,0:T(8,128)S(1)}, f32[3,8,16,512]{3,2,1,0:T(8,128)}, u32[]{:S(2)}) %copy-start) | copy-done | bytes 786456
  1.8 0.2 shard_map.50
  1.9 3.0 %collective-permute-start = (f32[16,512]{1,0:T(8,128)S(1)}, f32[16,512]{1,0:T(8,128)S(1)}, u32[]{:S(2)}, u32[]{:S(2)}) collective-permute-start(f32[16,512]{1,0:T(8,128)S(1)} %get-tuple-element.23), channel_id=1, source_target_pairs={{0,4},{4,8},{8,12},{12,16},{16,20},{20,24},{24,28},{28,0},{1,5},{5... | collective-permute-start | bytes 98312 | tf_op jit(solution)/shard_map/ppermute | solution.py:344
  5.0 0.0 collective-permute-start.1
  5.0 0.9 %copy-done.1 = f32[8,16,512]{2,1,0:T(8,128)S(1)} copy-done((f32[8,16,512]{2,1,0:T(8,128)S(1)}, f32[8,16,512]{2,1,0:T(8,128)}, u32[]{:S(2)}) %copy-start.1) | copy-done | bytes 262168
  5.9 0.9 %copy-done.2 = s32[8,16,512]{2,1,0:T(8,128)S(1)} copy-done((s32[8,16,512]{2,1,0:T(8,128)S(1)}, s32[8,16,512]{2,1,0:T(8,128)}, u32[]{:S(2)}) %copy-start.2) | copy-done | bytes 262168
  6.9 1.2 %collective-permute-done.1.sy_low = f32[8,512]{1,0:T(8,128)S(1)} collective-permute-done((f32[8,512]{1,0:T(8,128)S(1)}, f32[8,512]{1,0:T(8,128)S(1)}, u32[]{:S(2)}, u32[]{:S(2)}) %collective-permute-start.1) | collective-permute-done | bytes 16416 | tf_op jit(solution)/shard_map/ppermute | solution.py:344
  8.1 1.8 %collective-permute-done.sz_low = f32[16,512]{1,0:T(8,128)S(1)} collective-permute-done((f32[16,512]{1,0:T(8,128)S(1)}, f32[16,512]{1,0:T(8,128)S(1)}, u32[]{:S(2)}, u32[]{:S(2)}) %collective-permute-start) | collective-permute-done | bytes 32800 | tf_op jit(solution)/shard_map/ppermute | solution.py:344
  9.9 0.6 %shard_map.52 = (f32[64,512]{1,0:T(8,128)S(1)}, f32[128,512]{1,0:T(8,128)S(1)}, f32[128,512]{1,0:T(8,128)S(1)}, s32[8,16,512]{2,1,0:T(8,128)S(1)}, f32[8,16,512]{2,1,0:T(8,128)S(1)}) custom-call(f32[3,8,16,512]{3,2,1,0:T(8,128)S(1)} %get-tuple-element.21.twice, f32[8,16,512]{2,1,0:T(8,128)S(1)} %get-tuple-element.22.rm, f32[8,16,512]{2,1,0:T(8,128)S(1)} %shard_map.51.packed, ...), custom_call_target="tpu_custom_call" | custom-call | flops 4000000 | bytes 4000000 | tf_op jit(solution)/shard_map/pallas_call | solution.py:363
  10.5 0.1 collective-permute-start.2
  10.5 2.0 %collective-permute-start.3 = (f32[128,512]{1,0:T(8,128)S(1)}, f32[128,512]{1,0:T(8,128)S(1)}, u32[]{:S(2)}, u32[]{:S(2)}) collective-permute-start(f32[128,512]{1,0:T(8,128)S(1)} %get-tuple-element.28), channel_id=1, source_target_pairs={{0,4},{4,0},{8,12},{12,8},{16,20},{20,16},{24,28},{28,24},{1,5},{5... | collective-permute-start | bytes 786440 | tf_op jit(solution)/shard_map/ppermute | solution.py:352
  12.6 4.3 %collective-permute-done.2.both = f32[64,512]{1,0:T(8,128)S(1)} collective-permute-done((f32[64,512]{1,0:T(8,128)S(1)}, f32[64,512]{1,0:T(8,128)S(1)}, u32[]{:S(2)}, u32[]{:S(2)}) %collective-permute-start.2) | collective-permute-done | bytes 131104 | tf_op jit(solution)/shard_map/ppermute | solution.py:352
  16.9 0.7 %collective-permute-start.4 = (f32[128,512]{1,0:T(8,128)S(1)}, f32[128,512]{1,0:T(8,128)S(1)}, u32[]{:S(2)}, u32[]{:S(2)}) collective-permute-start(f32[128,512]{1,0:T(8,128)S(1)} %get-tuple-element.29), channel_id=1, source_target_pairs={{0,0},{4,8},{8,4},{12,16},{16,12},{20,24},{24,20},{28,28},{1,1},{5... | collective-permute-start | bytes 786440 | tf_op jit(solution)/shard_map/ppermute | solution.py:352
  17.6 2.8 %collective-permute-start.5 = (f32[64,512]{1,0:T(8,128)S(1)}, f32[64,512]{1,0:T(8,128)S(1)}, u32[]{:S(2)}, u32[]{:S(2)}) collective-permute-start(f32[64,512]{1,0:T(8,128)S(1)} %collective-permute-done.2.both), channel_id=1, source_target_pairs={{0,8},{4,0},{8,16},{12,4},{16,24},{20,12},{24,28},{28,20},{1,9},{5... | collective-permute-start | bytes 393224 | tf_op jit(solution)/shard_map/ppermute | solution.py:358
  20.3 3.0 %collective-permute-done.5.relayed = f32[64,512]{1,0:T(8,128)S(1)} collective-permute-done((f32[64,512]{1,0:T(8,128)S(1)}, f32[64,512]{1,0:T(8,128)S(1)}, u32[]{:S(2)}, u32[]{:S(2)}) %collective-permute-start.5) | collective-permute-done | bytes 131104 | tf_op jit(solution)/shard_map/ppermute | solution.py:358
  23.3 1.6 %collective-permute-done.3.partner = f32[128,512]{1,0:T(8,128)S(1)} collective-permute-done((f32[128,512]{1,0:T(8,128)S(1)}, f32[128,512]{1,0:T(8,128)S(1)}, u32[]{:S(2)}, u32[]{:S(2)}) %collective-permute-start.3) | collective-permute-done | bytes 262176 | tf_op jit(solution)/shard_map/ppermute | solution.py:352
  24.9 0.2 shard_map.53
  25.1 0.7 %collective-permute-start.6 = (f32[160,512]{1,0:T(8,128)S(1)}, f32[160,512]{1,0:T(8,128)S(1)}, u32[]{:S(2)}, u32[]{:S(2)}) collective-permute-start(f32[160,512]{1,0:T(8,128)S(1)} %get-tuple-element.32), channel_id=1, source_target_pairs={{0,0},{1,2},{2,1},{3,3},{4,4},{5,6},{6,5},{7,7},{8,8},{9,10},{10,9... | collective-permute-start | bytes 983048 | tf_op jit(solution)/shard_map/ppermute | solution.py:352
  25.8 1.4 %collective-permute-start.7 = (f32[160,512]{1,0:T(8,128)S(1)}, f32[160,512]{1,0:T(8,128)S(1)}, u32[]{:S(2)}, u32[]{:S(2)}) collective-permute-start(f32[160,512]{1,0:T(8,128)S(1)} %get-tuple-element.33), channel_id=1, source_target_pairs={{0,1},{1,0},{2,3},{3,2},{4,5},{5,4},{6,7},{7,6},{8,9},{9,8},{10,11... | collective-permute-start | bytes 983048 | tf_op jit(solution)/shard_map/ppermute | solution.py:352
  27.2 3.7 %shard_map.54 = (f32[9,20,4,32,128]{4,3,2,1,0:T(8,128)S(1)}, s32[4,20,4,32,128]{4,3,2,1,0:T(8,128)S(1)}) custom-call(s32[20,16,512]{2,1,0:T(8,128)S(1)} %get-tuple-element.34.d_ext, f32[20,16,512]{2,1,0:T(8,128)S(1)} %get-tuple-element.35.m_ext), custom_call_target="tpu_custom_call" | custom-call | flops 20000000 | bytes 20000000 | tf_op jit(solution)/shard_map/pallas_call | solution.py:363
  30.9 0.0 collective-permute-done.7.re
  30.9 5.5 %shard_map.55 = (s32[8,16,512]{2,1,0:T(8,128)}, s32[32,1,128]{2,1,0:T(1,128)S(1)}, f32[9,20,4,32,128]{4,3,2,1,0:T(8,128)S(1)}, s32[4,20,4,32,128]{4,3,2,1,0:T(8,128)S(1)}) custom-call(f32[160,512]{1,0:T(8,128)S(1)} %collective-permute-done.6.ro, f32[160,512]{1,0:T(8,128)S(1)} %collective-permute-done.7.re, ...), custom_call_target="tpu_custom_call", output_to_operand_aliasing={{2}: (2, {}), {3}: (3, {})} | custom-call | flops 20000000 | bytes 20000000 | tf_op jit(solution)/shard_map/pallas_call | solution.py:363
  36.4 14.4 %all_to_all.5 = s32[32,1,128]{2,1,0:T(1,128)S(1)} all-to-all(s32[32,1,128]{2,1,0:T(1,128)S(1)} %get-tuple-element.39), channel_id=1, replica_groups=mesh['gz'=8,'gy'=4] {'gz','gy'}, dimensions={0} | all-to-all | bytes 32768 | tf_op jit(solution)/shard_map/all_to_all | solution.py:422
  50.9 0.6 %reduce_sum.9 = s32[128]{0:T(128)} reduce(s32[32,1,128]{2,1,0:T(1,128)S(1)} %all_to_all.5, s32[]{:T(128)} %constant.0.clone.1), dimensions={0,1}, to_apply=%region_0.0 | reduce | flops 3968 | bytes 16900 | tf_op jit(solution)/shard_map/reduce_sum | solution.py:423
  (6 shorter events, 0.0 us)
Async XLA Ops:
  0.6 1.1 %copy-start = (f32[3,8,16,512]{3,2,1,0:T(8,128)S(1)}, f32[3,8,16,512]{3,2,1,0:T(8,128)}, u32[]{:S(2)}) copy-start(f32[3,8,16,512]{3,2,1,0:T(8,128)} %seeds.1) | copy-start | bytes 2359300
  1.9 8.0 %collective-permute-start = (f32[16,512]{1,0:T(8,128)S(1)}, f32[16,512]{1,0:T(8,128)S(1)}, u32[]{:S(2)}, u32[]{:S(2)}) collective-permute-start(f32[16,512]{1,0:T(8,128)S(1)} %get-tuple-element.23), channel_id=1, source_target_pairs={{0,4},{4,8},{8,12},{12,16},{16,20},{20,24},{24,28},{28,0},{1,5},{5... | collective-permute-start | bytes 98312 | tf_op jit(solution)/shard_map/ppermute | solution.py:344
  5.0 3.2 %collective-permute-start.1 = (f32[8,512]{1,0:T(8,128)S(1)}, f32[8,512]{1,0:T(8,128)S(1)}, u32[]{:S(2)}, u32[]{:S(2)}) collective-permute-start(f32[8,512]{1,0:T(8,128)S(1)} %get-tuple-element.24), channel_id=1, source_target_pairs={{0,1},{1,2},{2,3},{3,0},{4,5},{5,6},{6,7},{7,4},{8,9},{9,10},{10,1... | collective-permute-start | bytes 49160 | tf_op jit(solution)/shard_map/ppermute | solution.py:344
  5.0 1.0 %copy-start.1 = (f32[8,16,512]{2,1,0:T(8,128)S(1)}, f32[8,16,512]{2,1,0:T(8,128)}, u32[]{:S(2)}) copy-start(f32[8,16,512]{2,1,0:T(8,128)} %ranks.1) | copy-start | bytes 786436
  5.9 0.9 %copy-start.2 = (s32[8,16,512]{2,1,0:T(8,128)S(1)}, s32[8,16,512]{2,1,0:T(8,128)}, u32[]{:S(2)}) copy-start(s32[8,16,512]{2,1,0:T(8,128)} %flags.1) | copy-start | bytes 786436
  10.5 6.4 %collective-permute-start.2 = (f32[64,512]{1,0:T(8,128)S(1)}, f32[64,512]{1,0:T(8,128)S(1)}, u32[]{:S(2)}, u32[]{:S(2)}) collective-permute-start(f32[64,512]{1,0:T(8,128)S(1)} %get-tuple-element.26), channel_id=1, source_target_pairs={{0,4},{4,0},{8,12},{12,8},{16,20},{20,16},{24,28},{28,24},{1,5},{5... | collective-permute-start | bytes 393224 | tf_op jit(solution)/shard_map/ppermute | solution.py:352
  10.5 14.4 %collective-permute-start.3 = (f32[128,512]{1,0:T(8,128)S(1)}, f32[128,512]{1,0:T(8,128)S(1)}, u32[]{:S(2)}, u32[]{:S(2)}) collective-permute-start(f32[128,512]{1,0:T(8,128)S(1)} %get-tuple-element.28), channel_id=1, source_target_pairs={{0,4},{4,0},{8,12},{12,8},{16,20},{20,16},{24,28},{28,24},{1,5},{5... | collective-permute-start | bytes 786440 | tf_op jit(solution)/shard_map/ppermute | solution.py:352
  16.9 8.0 %collective-permute-start.4 = (f32[128,512]{1,0:T(8,128)S(1)}, f32[128,512]{1,0:T(8,128)S(1)}, u32[]{:S(2)}, u32[]{:S(2)}) collective-permute-start(f32[128,512]{1,0:T(8,128)S(1)} %get-tuple-element.29), channel_id=1, source_target_pairs={{0,0},{4,8},{8,4},{12,16},{16,12},{20,24},{24,20},{28,28},{1,1},{5... | collective-permute-start | bytes 786440 | tf_op jit(solution)/shard_map/ppermute | solution.py:352
  17.6 5.8 %collective-permute-start.5 = (f32[64,512]{1,0:T(8,128)S(1)}, f32[64,512]{1,0:T(8,128)S(1)}, u32[]{:S(2)}, u32[]{:S(2)}) collective-permute-start(f32[64,512]{1,0:T(8,128)S(1)} %collective-permute-done.2.both), channel_id=1, source_target_pairs={{0,8},{4,0},{8,16},{12,4},{16,24},{20,12},{24,28},{28,20},{1,9},{5... | collective-permute-start | bytes 393224 | tf_op jit(solution)/shard_map/ppermute | solution.py:358
  25.1 5.8 %collective-permute-start.6 = (f32[160,512]{1,0:T(8,128)S(1)}, f32[160,512]{1,0:T(8,128)S(1)}, u32[]{:S(2)}, u32[]{:S(2)}) collective-permute-start(f32[160,512]{1,0:T(8,128)S(1)} %get-tuple-element.32), channel_id=1, source_target_pairs={{0,0},{1,2},{2,1},{3,3},{4,4},{5,6},{6,5},{7,7},{8,8},{9,10},{10,9... | collective-permute-start | bytes 983048 | tf_op jit(solution)/shard_map/ppermute | solution.py:352
  25.8 5.1 %collective-permute-start.7 = (f32[160,512]{1,0:T(8,128)S(1)}, f32[160,512]{1,0:T(8,128)S(1)}, u32[]{:S(2)}, u32[]{:S(2)}) collective-permute-start(f32[160,512]{1,0:T(8,128)S(1)} %get-tuple-element.33), channel_id=1, source_target_pairs={{0,1},{1,0},{2,3},{3,2},{4,5},{5,4},{6,7},{7,6},{8,9},{9,8},{10,11... | collective-permute-start | bytes 983048 | tf_op jit(solution)/shard_map/ppermute | solution.py:352

commit v5 on v4

--- a/solution.py
+++ b/solution.py
@@ -4,6 +4,7 @@
 from jax.experimental import pallas as pl
 from jax.experimental.pallas import tpu as pltpu
 from jax.sharding import PartitionSpec as P
+
 
 ROUNDS = 3
 H = 2 * ROUNDS
@@ -118,23 +119,50 @@
         send(lambda z: depth - 1 - z)
 
 
-def y_layout(depth):
+def y_layout(depth, early):
     patterns, measures, at = [], [], 0
     for out, least in ((patterns, 1), (measures, 0)):
         for z in range(-H, depth + H):
             k = max(-z, z - depth + 1, 0)
             n = max(H - k, least)
-            if n:
+            ready = 0 <= z < depth and (least or 0 < z < depth - 1)
+            if n and ready == early:
                 out.append((z, n, at))
                 at += n
     return patterns, measures, -(-at // T) * T
+
+
+def send_rows(layout, pattern, measure, yo, ye):
+    patterns, measures, _ = layout
+    even = lax.axis_index("gy") % 2 == 0
+
+    def send(upward, downward):
+        for z, n, at in patterns:
+            e = pattern(z).astype(F32)
+            upward[pl.ds(at, n), :] = e[e.shape[0] - n :]
+            downward[pl.ds(at, n), :] = e[:n]
+        for z, n, at in measures:
+            e = measure(z)
+            upward[pl.ds(at, n), :] = e[e.shape[0] - n :]
+            downward[pl.ds(at, n), :] = e[:n]
+
+    @pl.when(even)
+    def _():
+        send(ye, yo)
+
+    @pl.when(jnp.logical_not(even))
+    def _():
+        send(yo, ye)
+
+
+def early_kernel(d_own, m_own, yo, ye):
+    send_rows(y_layout(m_own.shape[0], True), lambda z: d_own[z], lambda z: m_own[z], yo, ye)
 
 
 def planes_kernel(both, partner, other, relayed, d_own, m_own, yo, ye, d_ext, m_ext):
     depth, rows, _ = m_own.shape
     zlo, zhi = neighbours("gz")
     above = lax.axis_index("gz") % 2 == 0
-    even = lax.axis_index("gy") % 2 == 0
 
     def put(ref, zs, above, distance):
         for j, z in enumerate(zs):
@@ -157,25 +185,7 @@
     m_ext[first] = scaled(m_ext[first], d_ext[first - 1] & 16)
     m_ext[last] = scaled(m_ext[last], d_ext[last + 1] & 32)
     m_ext[last + 1] = scaled(m_ext[last + 1], d_ext[last] & 16)
-    patterns, measures, _ = y_layout(depth)
-
-    def send(upward, downward):
-        for z, n, at in patterns:
-            e = d_ext[z + H].astype(F32)
-            upward[pl.ds(at, n), :] = e[rows - n :]
-            downward[pl.ds(at, n), :] = e[:n]
-        for z, n, at in measures:
-            e = m_ext[z + H]
-            upward[pl.ds(at, n), :] = e[rows - n :]
-            downward[pl.ds(at, n), :] = e[:n]
-
-    @pl.when(even)
-    def _():
-        send(ye, yo)
-
-    @pl.when(jnp.logical_not(even))
-    def _():
-        send(yo, ye)
+    send_rows(y_layout(depth, False), lambda z: d_ext[z + H], lambda z: m_ext[z + H], yo, ye)
 
 
 def blocks(v):
@@ -279,23 +289,24 @@
     stages(fw, iw, depth, lambda stage: range(T, T + rows, T))
 
 
-def outer_kernel(ro, re, fw_in, iw_in, state_out, count_out, fw, iw):
+def outer_kernel(ro1, re1, ro2, re2, fw_in, iw_in, state_out, count_out, fw, iw, state_ref, sems):
     del fw_in, iw_in
-    depth, rows, width = state_out.shape
+    depth, rows, width = state_ref.shape
     planes = depth + 2 * H
     ylo, yhi = neighbours("gy")
     even = lax.axis_index("gy") % 2 == 0
-    patterns, measures, _ = y_layout(depth)
-    for z, n, at in patterns:
-        e, o = re[pl.ds(at, n), :], ro[pl.ds(at, n), :]
-        above = jnp.where(yhi, jnp.where(even, e, o), 0.0).astype(I32)
-        below = jnp.where(ylo, jnp.where(even, o, e), 0.0).astype(I32)
-        iw[PATTERN, z + H, :, pl.ds(T - n, n), :] = blocks(below)
-        iw[PATTERN, z + H, :, pl.ds(T + rows, n), :] = blocks(above)
-    for z, n, at in measures:
-        e, o = re[pl.ds(at, n), :], ro[pl.ds(at, n), :]
-        fw[STATE, z + H, :, pl.ds(T - n, n), :] = blocks(jnp.where(even, o, e))
-        fw[STATE, z + H, :, pl.ds(T + rows, n), :] = blocks(jnp.where(even, e, o))
+    for ro, re, early in ((ro1, re1, True), (ro2, re2, False)):
+        patterns, measures, _ = y_layout(depth, early)
+        for z, n, at in patterns:
+            e, o = re[pl.ds(at, n), :], ro[pl.ds(at, n), :]
+            above = jnp.where(yhi, jnp.where(even, e, o), 0.0).astype(I32)
+            below = jnp.where(ylo, jnp.where(even, o, e), 0.0).astype(I32)
+            iw[PATTERN, z + H, :, pl.ds(T - n, n), :] = blocks(below)
+            iw[PATTERN, z + H, :, pl.ds(T + rows, n), :] = blocks(above)
+        for z, n, at in measures:
+            e, o = re[pl.ds(at, n), :], ro[pl.ds(at, n), :]
+            fw[STATE, z + H, :, pl.ds(T - n, n), :] = blocks(jnp.where(even, o, e))
+            fw[STATE, z + H, :, pl.ds(T + rows, n), :] = blocks(jnp.where(even, e, o))
 
     def low(stage):
         return T - H + stage
@@ -306,14 +317,19 @@
     shape = (width // L, T, L)
     row = lax.broadcasted_iota(I32, shape, 1)
 
-    @pl.loop(0, planes)
+    each = max(n for n in (1, 2, 4) if planes % n == 0)
+
+    @pl.loop(0, planes, step=each)
     def _(i):
-        for at, one, two in ((low(0), H - 1, H), (high(0), T - H - 1, T - H)):
+        sites = [(i + j, *edge) for j in range(each) for edge in ((low(0), H - 1, H), (high(0), T - H - 1, T - H))]
+        found = []
+        for i, at, one, two in sites:
             d_next = iw[PATTERN, i, :, pl.ds(at + 1, T), :]
             d_prev = iw[PATTERN, i, :, pl.ds(at - 1, T), :]
             bit = jnp.where(row == one, d_next & 8, jnp.where(row == two, d_prev & 4, 0))
-            here = pl.ds(at, T)
-            fw[STATE, i, :, here, :] = scaled(fw[STATE, i, :, here, :], bit)
+            found.append(scaled(fw[STATE, i, :, pl.ds(at, T), :], bit))
+        for (i, at, _, _), p in zip(sites, found):
+            fw[STATE, i, :, pl.ds(at, T), :] = p
 
     stages(fw, iw, depth, lambda stage: (low(stage), high(stage)))
 
@@ -324,11 +340,12 @@
             old = jnp.where(p >= 0, jnp.where(hit, 1, 0), jnp.where(p == -2.0, 2, 1))
             state = jnp.where(new, 2, old)
             for j in range(width // L):
-                state_out[z, pl.ds(at, T), pl.ds(j * L, L)] = state[j]
+                state_ref[z, pl.ds(at, T), pl.ds(j * L, L)] = state[j]
             totals[-1] = totals[-1] + jnp.where(state == 0, 1, 0)
             for step in range(ROUNDS - 1):
                 p = fw[STATE + step + 1, z + H, :, pl.ds(T + at, T), :]
                 totals[step] = totals[step] + jnp.where(p >= 0, 1, 0)
+        pltpu.make_async_copy(state_ref.at[z], state_out.at[z], sems.at[z]).start()
         return tuple(totals)
 
     totals = lax.fori_loop(0, depth, finish, (jnp.zeros(shape, I32),) * ROUNDS)
@@ -337,6 +354,8 @@
     for step in range(ROUNDS):
         counts = jnp.where(lane == step, jnp.sum(totals[step]), counts)
     count_out[...] = counts
+    for z in range(depth):
+        pltpu.make_async_copy(state_ref.at[z], state_out.at[z], sems.at[z]).wait()
 
 
 def shift(value, axis, step):
@@ -359,12 +378,11 @@
 
 
 def call(kernel, outs, args, limit, cost, **more):
-    specs = more.pop("in_specs", [vmem()] * len(args))
     return pl.pallas_call(
         kernel,
         out_shape=outs,
-        in_specs=specs,
-        out_specs=[vmem()] * len(outs),
+        in_specs=[vmem()] * len(args),
+        out_specs=more.pop("out_specs", [vmem()] * len(outs)),
         compiler_params=pltpu.CompilerParams(vmem_limit_bytes=limit * 2**20),
         cost_estimate=pl.CostEstimate(flops=cost, bytes_accessed=cost, transcendentals=0),
         **more,
@@ -401,23 +419,29 @@
     other, both = lax.optimization_barrier((other, both))
     relayed = relay(both, "gz")
     other = swap(other, "gz", 1)
-    message = of((y_layout(depth)[2], width), F32)
+    message = of((y_layout(depth, True)[2], width), F32)
+    yo, ye = call(early_kernel, [message, message], (d_own, m_own), 8, 1000000)
+    ro1 = swap(yo, "gy", 1)
+    re1 = swap(ye, "gy", 0)
+    message = of((y_layout(depth, False)[2], width), F32)
     ext = (planes, rows, width)
     yo, ye, d_ext, m_ext = call(
         planes_kernel, [message, message, of(ext, I32), of(ext, F32)], (both, partner, other, relayed, d_own, m_own), 8, 4000000
     )
-    ro = swap(yo, "gy", 1)
-    re = swap(ye, "gy", 0)
+    ro2 = swap(yo, "gy", 1)
+    re2 = swap(ye, "gy", 0)
     cells = (planes, width // L, rows + 2 * T, L)
     works = [of((STATE + ROUNDS,) + cells, F32), of((NEW + 1 + ROUNDS,) + cells, I32)]
     fw, iw = call(inner_kernel, works, (d_ext, m_ext), 8, 20000000)
     state, counts, _, _ = call(
         outer_kernel,
         [of(ranks.shape, I32), of((devices, 1, L), I32)] + works,
-        (ro, re, fw, iw),
+        (ro1, re1, ro2, re2, fw, iw),
         8,
         20000000,
-        input_output_aliases={2: 2, 3: 3},
+        input_output_aliases={4: 2, 5: 3},
+        out_specs=[pl.BlockSpec(memory_space=pl.ANY), vmem(), vmem(), vmem()],
+        scratch_shapes=[pltpu.VMEM(ranks.shape, I32), pltpu.SemaphoreType.DMA((depth,))],
     )
     everyone = lax.all_to_all(counts, ("gz", "gy"), 0, 0, tiled=True)
     undecided = jnp.sum(everyone, axis=(0, 1))[:ROUNDS]

time: 51.7 us -> 49.8 us (0.963)
  waiting for transfers between devices: 11.9 us -> 8.07 us
  starting transfers between devices: 10.6 us -> 14.4 us
  blocking collectives: 14.4 us -> 12.7 us
    ppermute x5 -> x7, starting transfers between devices: 4.79 us -> 8.58 us  [swap(): return lax.ppermute(value, axis, pairs)]
    ppermute x1, waiting for transfers between devices: 3 us -> 0.01 us  [relay(): return lax.ppermute(value, axis, pairs)]
    all_to_all x1, blocking collectives: 14.4 us -> 12.7 us  [per_device(): everyone = lax.all_to_all(counts, ('gz', 'gy'), 0, 0, tiled=True)]
    ppermute x5 -> x7, waiting for transfers between devices: 5.94 us -> 5.08 us  [swap(): return lax.ppermute(value, axis, pairs)]
    pallas_call x6 -> x7, Pallas kernels: 10.2 us -> 10.1 us  [call(): pl.pallas_call(kernel, out_shape=outs, in_specs=[vmem()] * len(args), out...]
  transfers between devices with their start and end apart: 8 -> 10, of which waited for: 5 -> 4; matrix products, arithmetic and copies ran while one was open for 0% -> 0% of each run, Pallas kernels for 7% -> 8%
where the time goes in v5:
time: 49.8 us; the launch traced here: 49.5 us
  starting transfers between devices  14.4 us (29%)
  blocking collectives  12.7 us (26%)
  Pallas kernels  10.1 us (20%)
  waiting for transfers between devices  8.07 us (16%)
  local copies, waits for them, and re-layouts  3.03 us (6%)
  between operations  0.76 us (2%)
  other arithmetic  0.56 us (1%)
    all_to_all x1, blocking collectives, per_device(): everyone = lax.all_to_all(counts, ('gz', 'gy'), 0, 0, tiled=True)  12.7 us
    pallas_call x7, Pallas kernels, call(): pl.pallas_call(kernel, out_shape=outs, in_specs=[vmem()] * len(args), out...  10.1 us
    ppermute x7, starting transfers between devices, swap(): return lax.ppermute(value, axis, pairs)  8.58 us
    ppermute x7, waiting for transfers between devices, swap(): return lax.ppermute(value, axis, pairs)  5.08 us
    unnamed x6, local copies, waits for them, and re-layouts  3.03 us
    ppermute x2, starting transfers between devices, shift(): lax.ppermute(value, axis, [(i, (i + step) % count) for i in range(count)])  3.02 us
    ppermute x2, waiting for transfers between devices, shift(): lax.ppermute(value, axis, [(i, (i + step) % count) for i in range(count)])  2.99 us
    ppermute x1, starting transfers between devices, relay(): return lax.ppermute(value, axis, pairs)  2.75 us
  transfers between devices with their start and end apart: 10, of which 4 were waited for; matrix products, arithmetic and copies ran while one was open for 0% of the time, Pallas kernels for 8%

profile of v5, /device:TPU:0, one launch (start us, length us, event | category | flops | bytes accessed | tf_op | source)
XLA Modules:
  0.0 49.5 jit_solution(14485422337660554053)
XLA Ops:
  0.6 1.1 %copy-done = f32[3,8,16,512]{3,2,1,0:T(8,128)S(1)} copy-done((f32[3,8,16,512]{3,2,1,0:T(8,128)S(1)}, f32[3,8,16,512]{3,2,1,0:T(8,128)}, u32[]{:S(2)}) %copy-start) | copy-done | bytes 786456
  1.8 0.2 shard_map.50
  1.9 3.0 %collective-permute-start = (f32[16,512]{1,0:T(8,128)S(1)}, f32[16,512]{1,0:T(8,128)S(1)}, u32[]{:S(2)}, u32[]{:S(2)}) collective-permute-start(f32[16,512]{1,0:T(8,128)S(1)} %get-tuple-element.25), channel_id=1, source_target_pairs={{0,4},{4,8},{8,12},{12,16},{16,20},{20,24},{24,28},{28,0},{1,5},{5... | collective-permute-start | bytes 98312 | tf_op jit(solution)/shard_map/ppermute | solution.py:363
  5.0 0.0 collective-permute-start.1
  5.0 0.9 %copy-done.1 = f32[8,16,512]{2,1,0:T(8,128)S(1)} copy-done((f32[8,16,512]{2,1,0:T(8,128)S(1)}, f32[8,16,512]{2,1,0:T(8,128)}, u32[]{:S(2)}) %copy-start.1) | copy-done | bytes 262168
  5.9 0.9 %copy-done.2 = s32[8,16,512]{2,1,0:T(8,128)S(1)} copy-done((s32[8,16,512]{2,1,0:T(8,128)S(1)}, s32[8,16,512]{2,1,0:T(8,128)}, u32[]{:S(2)}) %copy-start.2) | copy-done | bytes 262168
  6.9 1.2 %collective-permute-done.1.sy_low = f32[8,512]{1,0:T(8,128)S(1)} collective-permute-done((f32[8,512]{1,0:T(8,128)S(1)}, f32[8,512]{1,0:T(8,128)S(1)}, u32[]{:S(2)}, u32[]{:S(2)}) %collective-permute-start.1) | collective-permute-done | bytes 16416 | tf_op jit(solution)/shard_map/ppermute | solution.py:363
  8.1 1.8 %collective-permute-done.sz_low = f32[16,512]{1,0:T(8,128)S(1)} collective-permute-done((f32[16,512]{1,0:T(8,128)S(1)}, f32[16,512]{1,0:T(8,128)S(1)}, u32[]{:S(2)}, u32[]{:S(2)}) %collective-permute-start) | collective-permute-done | bytes 32800 | tf_op jit(solution)/shard_map/ppermute | solution.py:363
  9.9 0.6 %shard_map.52 = (f32[64,512]{1,0:T(8,128)S(1)}, f32[128,512]{1,0:T(8,128)S(1)}, f32[128,512]{1,0:T(8,128)S(1)}, s32[8,16,512]{2,1,0:T(8,128)S(1)}, f32[8,16,512]{2,1,0:T(8,128)S(1)}) custom-call(f32[3,8,16,512]{3,2,1,0:T(8,128)S(1)} %get-tuple-element.23.twice, f32[8,16,512]{2,1,0:T(8,128)S(1)} %get-tuple-element.24.rm, f32[8,16,512]{2,1,0:T(8,128)S(1)} %shard_map.51.packed, ...), custom_call_target="tpu_custom_call" | custom-call | flops 4000000 | bytes 4000000 | tf_op jit(solution)/shard_map/pallas_call | solution.py:381
  10.5 0.1 collective-permute-start.4
  10.5 2.0 %collective-permute-start.5 = (f32[128,512]{1,0:T(8,128)S(1)}, f32[128,512]{1,0:T(8,128)S(1)}, u32[]{:S(2)}, u32[]{:S(2)}) collective-permute-start(f32[128,512]{1,0:T(8,128)S(1)} %get-tuple-element.34), channel_id=1, source_target_pairs={{0,4},{4,0},{8,12},{12,8},{16,20},{20,16},{24,28},{28,24},{1,5},{5... | collective-permute-start | bytes 786440 | tf_op jit(solution)/shard_map/ppermute | solution.py:371
  12.6 4.3 %collective-permute-done.4.both = f32[64,512]{1,0:T(8,128)S(1)} collective-permute-done((f32[64,512]{1,0:T(8,128)S(1)}, f32[64,512]{1,0:T(8,128)S(1)}, u32[]{:S(2)}, u32[]{:S(2)}) %collective-permute-start.4) | collective-permute-done | bytes 131104 | tf_op jit(solution)/shard_map/ppermute | solution.py:371
  16.9 0.7 %collective-permute-start.6 = (f32[128,512]{1,0:T(8,128)S(1)}, f32[128,512]{1,0:T(8,128)S(1)}, u32[]{:S(2)}, u32[]{:S(2)}) collective-permute-start(f32[128,512]{1,0:T(8,128)S(1)} %get-tuple-element.35), channel_id=1, source_target_pairs={{0,0},{4,8},{8,4},{12,16},{16,12},{20,24},{24,20},{28,28},{1,1},{5... | collective-permute-start | bytes 786440 | tf_op jit(solution)/shard_map/ppermute | solution.py:371
  17.6 2.8 %collective-permute-start.7 = (f32[64,512]{1,0:T(8,128)S(1)}, f32[64,512]{1,0:T(8,128)S(1)}, u32[]{:S(2)}, u32[]{:S(2)}) collective-permute-start(f32[64,512]{1,0:T(8,128)S(1)} %collective-permute-done.4.both), channel_id=1, source_target_pairs={{0,8},{4,0},{8,16},{12,4},{16,24},{20,12},{24,28},{28,20},{1,9},{5... | collective-permute-start | bytes 393224 | tf_op jit(solution)/shard_map/ppermute | solution.py:377
  20.4 0.7 %collective-permute-start.2 = (f32[88,512]{1,0:T(8,128)S(1)}, f32[88,512]{1,0:T(8,128)S(1)}, u32[]{:S(2)}, u32[]{:S(2)}) collective-permute-start(f32[88,512]{1,0:T(8,128)S(1)} %get-tuple-element.29), channel_id=1, source_target_pairs={{0,0},{1,2},{2,1},{3,3},{4,4},{5,6},{6,5},{7,7},{8,8},{9,10},{10,9... | collective-permute-start | bytes 540680 | tf_op jit(solution)/shard_map/ppermute | solution.py:371
  21.1 3.1 %collective-permute-start.3 = (f32[88,512]{1,0:T(8,128)S(1)}, f32[88,512]{1,0:T(8,128)S(1)}, u32[]{:S(2)}, u32[]{:S(2)}) collective-permute-start(f32[88,512]{1,0:T(8,128)S(1)} %get-tuple-element.30), channel_id=1, source_target_pairs={{0,1},{1,0},{2,3},{3,2},{4,5},{5,4},{6,7},{7,6},{8,9},{9,8},{10,11... | collective-permute-start | bytes 540680 | tf_op jit(solution)/shard_map/ppermute | solution.py:371
  24.2 0.7 %collective-permute-done.5.partner = f32[128,512]{1,0:T(8,128)S(1)} collective-permute-done((f32[128,512]{1,0:T(8,128)S(1)}, f32[128,512]{1,0:T(8,128)S(1)}, u32[]{:S(2)}, u32[]{:S(2)}) %collective-permute-start.5) | collective-permute-done | bytes 262176 | tf_op jit(solution)/shard_map/ppermute | solution.py:371
  24.9 0.2 shard_map.54
  25.1 0.7 %collective-permute-start.8 = (f32[80,512]{1,0:T(8,128)S(1)}, f32[80,512]{1,0:T(8,128)S(1)}, u32[]{:S(2)}, u32[]{:S(2)}) collective-permute-start(f32[80,512]{1,0:T(8,128)S(1)} %get-tuple-element.36), channel_id=1, source_target_pairs={{0,0},{1,2},{2,1},{3,3},{4,4},{5,6},{6,5},{7,7},{8,8},{9,10},{10,9... | collective-permute-start | bytes 491528 | tf_op jit(solution)/shard_map/ppermute | solution.py:371
  25.8 1.4 %collective-permute-start.9 = (f32[80,512]{1,0:T(8,128)S(1)}, f32[80,512]{1,0:T(8,128)S(1)}, u32[]{:S(2)}, u32[]{:S(2)}) collective-permute-start(f32[80,512]{1,0:T(8,128)S(1)} %get-tuple-element.37), channel_id=1, source_target_pairs={{0,1},{1,0},{2,3},{3,2},{4,5},{5,4},{6,7},{7,6},{8,9},{9,8},{10,11... | collective-permute-start | bytes 491528 | tf_op jit(solution)/shard_map/ppermute | solution.py:371
  27.1 3.7 %shard_map.55 = (f32[9,20,4,32,128]{4,3,2,1,0:T(8,128)S(1)}, s32[4,20,4,32,128]{4,3,2,1,0:T(8,128)S(1)}) custom-call(s32[20,16,512]{2,1,0:T(8,128)S(1)} %get-tuple-element.38.d_ext, f32[20,16,512]{2,1,0:T(8,128)S(1)} %get-tuple-element.39.m_ext), custom_call_target="tpu_custom_call" | custom-call | flops 20000000 | bytes 20000000 | tf_op jit(solution)/shard_map/pallas_call | solution.py:381
  30.9 5.4 %shard_map.56 = (s32[8,16,512]{2,1,0:T(8,128)}, s32[32,1,128]{2,1,0:T(1,128)S(1)}, f32[9,20,4,32,128]{4,3,2,1,0:T(8,128)S(1)}, s32[4,20,4,32,128]{4,3,2,1,0:T(8,128)S(1)}) custom-call(f32[88,512]{1,0:T(8,128)S(1)} %collective-permute-done.2.ro1, f32[88,512]{1,0:T(8,128)S(1)} %collective-permute-done.3.re1, ...), custom_call_target="tpu_custom_call", output_to_operand_aliasing={{2}: (4, {}), {3}: (5, {})} | custom-call | flops 20000000 | bytes 20000000 | tf_op jit(solution)/shard_map/pallas_call | solution.py:381
  36.3 12.7 %all_to_all.5 = s32[32,1,128]{2,1,0:T(1,128)S(1)} all-to-all(s32[32,1,128]{2,1,0:T(1,128)S(1)} %get-tuple-element.43), channel_id=1, replica_groups=mesh['gz'=8,'gy'=4] {'gz','gy'}, dimensions={0} | all-to-all | bytes 32768 | tf_op jit(solution)/shard_map/all_to_all | solution.py:446
  49.0 0.6 %reduce_sum.9 = s32[128]{0:T(128)} reduce(s32[32,1,128]{2,1,0:T(1,128)S(1)} %all_to_all.5, s32[]{:T(128)} %constant.0.clone.1), dimensions={0,1}, to_apply=%region_0.0 | reduce | flops 3968 | bytes 16900 | tf_op jit(solution)/shard_map/reduce_sum | solution.py:447
  (11 shorter events, 0.1 us)
Async XLA Ops:
  0.6 1.1 %copy-start = (f32[3,8,16,512]{3,2,1,0:T(8,128)S(1)}, f32[3,8,16,512]{3,2,1,0:T(8,128)}, u32[]{:S(2)}) copy-start(f32[3,8,16,512]{3,2,1,0:T(8,128)} %seeds.1) | copy-start | bytes 2359300
  1.9 8.0 %collective-permute-start = (f32[16,512]{1,0:T(8,128)S(1)}, f32[16,512]{1,0:T(8,128)S(1)}, u32[]{:S(2)}, u32[]{:S(2)}) collective-permute-start(f32[16,512]{1,0:T(8,128)S(1)} %get-tuple-element.25), channel_id=1, source_target_pairs={{0,4},{4,8},{8,12},{12,16},{16,20},{20,24},{24,28},{28,0},{1,5},{5... | collective-permute-start | bytes 98312 | tf_op jit(solution)/shard_map/ppermute | solution.py:363
  5.0 3.2 %collective-permute-start.1 = (f32[8,512]{1,0:T(8,128)S(1)}, f32[8,512]{1,0:T(8,128)S(1)}, u32[]{:S(2)}, u32[]{:S(2)}) collective-permute-start(f32[8,512]{1,0:T(8,128)S(1)} %get-tuple-element.26), channel_id=1, source_target_pairs={{0,1},{1,2},{2,3},{3,0},{4,5},{5,6},{6,7},{7,4},{8,9},{9,10},{10,1... | collective-permute-start | bytes 49160 | tf_op jit(solution)/shard_map/ppermute | solution.py:363
  5.0 1.0 %copy-start.1 = (f32[8,16,512]{2,1,0:T(8,128)S(1)}, f32[8,16,512]{2,1,0:T(8,128)}, u32[]{:S(2)}) copy-start(f32[8,16,512]{2,1,0:T(8,128)} %ranks.1) | copy-start | bytes 786436
  5.9 0.9 %copy-start.2 = (s32[8,16,512]{2,1,0:T(8,128)S(1)}, s32[8,16,512]{2,1,0:T(8,128)}, u32[]{:S(2)}) copy-start(s32[8,16,512]{2,1,0:T(8,128)} %flags.1) | copy-start | bytes 786436
  10.5 6.4 %collective-permute-start.4 = (f32[64,512]{1,0:T(8,128)S(1)}, f32[64,512]{1,0:T(8,128)S(1)}, u32[]{:S(2)}, u32[]{:S(2)}) collective-permute-start(f32[64,512]{1,0:T(8,128)S(1)} %get-tuple-element.32), channel_id=1, source_target_pairs={{0,4},{4,0},{8,12},{12,8},{16,20},{20,16},{24,28},{28,24},{1,5},{5... | collective-permute-start | bytes 393224 | tf_op jit(solution)/shard_map/ppermute | solution.py:371
  10.5 14.4 %collective-permute-start.5 = (f32[128,512]{1,0:T(8,128)S(1)}, f32[128,512]{1,0:T(8,128)S(1)}, u32[]{:S(2)}, u32[]{:S(2)}) collective-permute-start(f32[128,512]{1,0:T(8,128)S(1)} %get-tuple-element.34), channel_id=1, source_target_pairs={{0,4},{4,0},{8,12},{12,8},{16,20},{20,16},{24,28},{28,24},{1,5},{5... | collective-permute-start | bytes 786440 | tf_op jit(solution)/shard_map/ppermute | solution.py:371
  16.9 8.0 %collective-permute-start.6 = (f32[128,512]{1,0:T(8,128)S(1)}, f32[128,512]{1,0:T(8,128)S(1)}, u32[]{:S(2)}, u32[]{:S(2)}) collective-permute-start(f32[128,512]{1,0:T(8,128)S(1)} %get-tuple-element.35), channel_id=1, source_target_pairs={{0,0},{4,8},{8,4},{12,16},{16,12},{20,24},{24,20},{28,28},{1,1},{5... | collective-permute-start | bytes 786440 | tf_op jit(solution)/shard_map/ppermute | solution.py:371
  17.6 6.6 %collective-permute-start.7 = (f32[64,512]{1,0:T(8,128)S(1)}, f32[64,512]{1,0:T(8,128)S(1)}, u32[]{:S(2)}, u32[]{:S(2)}) collective-permute-start(f32[64,512]{1,0:T(8,128)S(1)} %collective-permute-done.4.both), channel_id=1, source_target_pairs={{0,8},{4,0},{8,16},{12,4},{16,24},{20,12},{24,28},{28,20},{1,9},{5... | collective-permute-start | bytes 393224 | tf_op jit(solution)/shard_map/ppermute | solution.py:377
  20.4 10.5 %collective-permute-start.2 = (f32[88,512]{1,0:T(8,128)S(1)}, f32[88,512]{1,0:T(8,128)S(1)}, u32[]{:S(2)}, u32[]{:S(2)}) collective-permute-start(f32[88,512]{1,0:T(8,128)S(1)} %get-tuple-element.29), channel_id=1, source_target_pairs={{0,0},{1,2},{2,1},{3,3},{4,4},{5,6},{6,5},{7,7},{8,8},{9,10},{10,9... | collective-permute-start | bytes 540680 | tf_op jit(solution)/shard_map/ppermute | solution.py:371
  21.1 9.8 %collective-permute-start.3 = (f32[88,512]{1,0:T(8,128)S(1)}, f32[88,512]{1,0:T(8,128)S(1)}, u32[]{:S(2)}, u32[]{:S(2)}) collective-permute-start(f32[88,512]{1,0:T(8,128)S(1)} %get-tuple-element.30), channel_id=1, source_target_pairs={{0,1},{1,0},{2,3},{3,2},{4,5},{5,4},{6,7},{7,6},{8,9},{9,8},{10,11... | collective-permute-start | bytes 540680 | tf_op jit(solution)/shard_map/ppermute | solution.py:371
  25.1 5.8 %collective-permute-start.8 = (f32[80,512]{1,0:T(8,128)S(1)}, f32[80,512]{1,0:T(8,128)S(1)}, u32[]{:S(2)}, u32[]{:S(2)}) collective-permute-start(f32[80,512]{1,0:T(8,128)S(1)} %get-tuple-element.36), channel_id=1, source_target_pairs={{0,0},{1,2},{2,1},{3,3},{4,4},{5,6},{6,5},{7,7},{8,8},{9,10},{10,9... | collective-permute-start | bytes 491528 | tf_op jit(solution)/shard_map/ppermute | solution.py:371
  25.8 5.1 %collective-permute-start.9 = (f32[80,512]{1,0:T(8,128)S(1)}, f32[80,512]{1,0:T(8,128)S(1)}, u32[]{:S(2)}, u32[]{:S(2)}) collective-permute-start(f32[80,512]{1,0:T(8,128)S(1)} %get-tuple-element.37), channel_id=1, source_target_pairs={{0,1},{1,0},{2,3},{3,2},{4,5},{5,4},{6,7},{7,6},{8,9},{9,8},{10,11... | collective-permute-start | bytes 491528 | tf_op jit(solution)/shard_map/ppermute | solution.py:371

commit v6 on v5

--- a/solution.py
+++ b/solution.py
@@ -9,7 +9,7 @@
 ROUNDS = 3
 H = 2 * ROUNDS
 T = 8
-RELAYED = 2
+RELAYED = 3
 L = 128
 BIG = 3.0e38
 F32, I32 = jnp.float32, jnp.int32
@@ -391,7 +391,7 @@
 
 def per_device(ranks, seeds, flags):
     depth, rows, width = ranks.shape
-    assert H + RELAYED <= depth + 1 <= 2 * H and lax.axis_size("gz") % 2 == 0 and rows >= 2 * T and T == H + 2 and width % L == 0
+    assert RELAYED <= 2 * H - depth and H < depth and lax.axis_size("gz") % 2 == 0 and rows >= 2 * T and T == H + 2 and width % L == 0
     planes = depth + 2 * H
     devices = lax.axis_size("gz") * lax.axis_size("gy")
     of = jax.ShapeDtypeStruct
@@ -416,7 +416,6 @@
     )
     both = swap(both, "gz", 0)
     partner = swap(partner, "gz", 0)
-    other, both = lax.optimization_barrier((other, both))
     relayed = relay(both, "gz")
     other = swap(other, "gz", 1)
     message = of((y_layout(depth, True)[2], width), F32)

time: 49.8 us -> 51.6 us (1.036)
  waiting for transfers between devices: 8.07 us -> 9.69 us
  blocking collectives: 12.7 us -> 11.4 us
  starting transfers between devices: 14.4 us -> 15.7 us
    ppermute x7, waiting for transfers between devices: 5.08 us -> 6.69 us  [swap(): return lax.ppermute(value, axis, pairs)]
    ppermute x7, starting transfers between devices: 8.58 us -> 10.1 us  [swap(): return lax.ppermute(value, axis, pairs)]
    all_to_all x1, blocking collectives: 12.7 us -> 11.4 us  [per_device(): everyone = lax.all_to_all(counts, ('gz', 'gy'), 0, 0, tiled=True)]
  transfers between devices with their start and end apart: 10 -> 10, of which waited for: 4 -> 3; matrix products, arithmetic and copies ran while one was open for 0% -> 0% of each run, Pallas kernels for 8% -> 8%
where the time goes in v6:
time: 51.6 us; the launch traced here: 51.3 us
  starting transfers between devices  15.7 us (30%)
  blocking collectives  11.4 us (22%)
  Pallas kernels  10.1 us (20%)
  waiting for transfers between devices  9.69 us (19%)
  local copies, waits for them, and re-layouts  3.03 us (6%)
  between operations  0.76 us (1%)
  other arithmetic  0.56 us (1%)
    all_to_all x1, blocking collectives, per_device(): everyone = lax.all_to_all(counts, ('gz', 'gy'), 0, 0, tiled=True)  11.4 us
    ppermute x7, starting transfers between devices, swap(): return lax.ppermute(value, axis, pairs)  10.1 us
    pallas_call x7, Pallas kernels, call(): pl.pallas_call(kernel, out_shape=outs, in_specs=[vmem()] * len(args), out...  10.1 us
    ppermute x7, waiting for transfers between devices, swap(): return lax.ppermute(value, axis, pairs)  6.69 us
    unnamed x6, local copies, waits for them, and re-layouts  3.03 us
    ppermute x2, starting transfers between devices, shift(): lax.ppermute(value, axis, [(i, (i + step) % count) for i in range(count)])  3.02 us
    ppermute x2, waiting for transfers between devices, shift(): lax.ppermute(value, axis, [(i, (i + step) % count) for i in range(count)])  2.99 us
    ppermute x1, starting transfers between devices, relay(): return lax.ppermute(value, axis, pairs)  2.58 us
  transfers between devices with their start and end apart: 10, of which 3 were waited for; matrix products, arithmetic and copies ran while one was open for 0% of the time, Pallas kernels for 8%

profile of v6, /device:TPU:0, one launch (start us, length us, event | category | flops | bytes accessed | tf_op | source)
XLA Modules:
  0.0 51.3 jit_solution(16750706305762411009)
XLA Ops:
  0.6 1.1 %copy-done = f32[3,8,16,512]{3,2,1,0:T(8,128)S(1)} copy-done((f32[3,8,16,512]{3,2,1,0:T(8,128)S(1)}, f32[3,8,16,512]{3,2,1,0:T(8,128)}, u32[]{:S(2)}) %copy-start) | copy-done | bytes 786456
  1.8 0.2 shard_map.50
  1.9 3.0 %collective-permute-start = (f32[16,512]{1,0:T(8,128)S(1)}, f32[16,512]{1,0:T(8,128)S(1)}, u32[]{:S(2)}, u32[]{:S(2)}) collective-permute-start(f32[16,512]{1,0:T(8,128)S(1)} %get-tuple-element.23), channel_id=1, source_target_pairs={{0,4},{4,8},{8,12},{12,16},{16,20},{20,24},{24,28},{28,0},{1,5},{5... | collective-permute-start | bytes 98312 | tf_op jit(solution)/shard_map/ppermute | solution.py:363
  5.0 0.0 collective-permute-start.1
  5.0 0.9 %copy-done.1 = f32[8,16,512]{2,1,0:T(8,128)S(1)} copy-done((f32[8,16,512]{2,1,0:T(8,128)S(1)}, f32[8,16,512]{2,1,0:T(8,128)}, u32[]{:S(2)}) %copy-start.1) | copy-done | bytes 262168
  5.9 0.9 %copy-done.2 = s32[8,16,512]{2,1,0:T(8,128)S(1)} copy-done((s32[8,16,512]{2,1,0:T(8,128)S(1)}, s32[8,16,512]{2,1,0:T(8,128)}, u32[]{:S(2)}) %copy-start.2) | copy-done | bytes 262168
  6.9 1.2 %collective-permute-done.1.sy_low = f32[8,512]{1,0:T(8,128)S(1)} collective-permute-done((f32[8,512]{1,0:T(8,128)S(1)}, f32[8,512]{1,0:T(8,128)S(1)}, u32[]{:S(2)}, u32[]{:S(2)}) %collective-permute-start.1) | collective-permute-done | bytes 16416 | tf_op jit(solution)/shard_map/ppermute | solution.py:363
  8.1 1.8 %collective-permute-done.sz_low = f32[16,512]{1,0:T(8,128)S(1)} collective-permute-done((f32[16,512]{1,0:T(8,128)S(1)}, f32[16,512]{1,0:T(8,128)S(1)}, u32[]{:S(2)}, u32[]{:S(2)}) %collective-permute-start) | collective-permute-done | bytes 32800 | tf_op jit(solution)/shard_map/ppermute | solution.py:363
  9.9 0.6 %shard_map.52 = (f32[96,512]{1,0:T(8,128)S(1)}, f32[96,512]{1,0:T(8,128)S(1)}, f32[96,512]{1,0:T(8,128)S(1)}, s32[8,16,512]{2,1,0:T(8,128)S(1)}, f32[8,16,512]{2,1,0:T(8,128)S(1)}) custom-call(f32[3,8,16,512]{3,2,1,0:T(8,128)S(1)} %get-tuple-element.21.twice, f32[8,16,512]{2,1,0:T(8,128)S(1)} %get-tuple-element.22.rm, f32[8,16,512]{2,1,0:T(8,128)S(1)} %shard_map.51.packed, ...), custom_call_target="tpu_custom_call" | custom-call | flops 4000000 | bytes 4000000 | tf_op jit(solution)/shard_map/pallas_call | solution.py:381
  10.5 0.1 collective-permute-start.4
  10.5 2.0 %collective-permute-start.5 = (f32[96,512]{1,0:T(8,128)S(1)}, f32[96,512]{1,0:T(8,128)S(1)}, u32[]{:S(2)}, u32[]{:S(2)}) collective-permute-start(f32[96,512]{1,0:T(8,128)S(1)} %get-tuple-element.30), channel_id=1, source_target_pairs={{0,4},{4,0},{8,12},{12,8},{16,20},{20,16},{24,28},{28,24},{1,5},{5... | collective-permute-start | bytes 589832 | tf_op jit(solution)/shard_map/ppermute | solution.py:371
  12.5 0.7 %collective-permute-start.6 = (f32[96,512]{1,0:T(8,128)S(1)}, f32[96,512]{1,0:T(8,128)S(1)}, u32[]{:S(2)}, u32[]{:S(2)}) collective-permute-start(f32[96,512]{1,0:T(8,128)S(1)} %get-tuple-element.31), channel_id=1, source_target_pairs={{0,0},{4,8},{8,4},{12,16},{16,12},{20,24},{24,20},{28,28},{1,1},{5... | collective-permute-start | bytes 589832 | tf_op jit(solution)/shard_map/ppermute | solution.py:371
  13.2 6.7 %collective-permute-done.4.both = f32[96,512]{1,0:T(8,128)S(1)} collective-permute-done((f32[96,512]{1,0:T(8,128)S(1)}, f32[96,512]{1,0:T(8,128)S(1)}, u32[]{:S(2)}, u32[]{:S(2)}) %collective-permute-start.4) | collective-permute-done | bytes 196640 | tf_op jit(solution)/shard_map/ppermute | solution.py:371
  19.9 2.6 %collective-permute-start.7 = (f32[96,512]{1,0:T(8,128)S(1)}, f32[96,512]{1,0:T(8,128)S(1)}, u32[]{:S(2)}, u32[]{:S(2)}) collective-permute-start(f32[96,512]{1,0:T(8,128)S(1)} %collective-permute-done.4.both), channel_id=1, source_target_pairs={{0,8},{4,0},{8,16},{12,4},{16,24},{20,12},{24,28},{28,20},{1,9},{5... | collective-permute-start | bytes 589832 | tf_op jit(solution)/shard_map/ppermute | solution.py:377
  22.5 0.7 %collective-permute-start.2 = (f32[88,512]{1,0:T(8,128)S(1)}, f32[88,512]{1,0:T(8,128)S(1)}, u32[]{:S(2)}, u32[]{:S(2)}) collective-permute-start(f32[88,512]{1,0:T(8,128)S(1)} %get-tuple-element.27), channel_id=1, source_target_pairs={{0,0},{1,2},{2,1},{3,3},{4,4},{5,6},{6,5},{7,7},{8,8},{9,10},{10,9... | collective-permute-start | bytes 540680 | tf_op jit(solution)/shard_map/ppermute | solution.py:371
  23.2 2.9 %collective-permute-start.3 = (f32[88,512]{1,0:T(8,128)S(1)}, f32[88,512]{1,0:T(8,128)S(1)}, u32[]{:S(2)}, u32[]{:S(2)}) collective-permute-start(f32[88,512]{1,0:T(8,128)S(1)} %get-tuple-element.28), channel_id=1, source_target_pairs={{0,1},{1,0},{2,3},{3,2},{4,5},{5,4},{6,7},{7,6},{8,9},{9,8},{10,11... | collective-permute-start | bytes 540680 | tf_op jit(solution)/shard_map/ppermute | solution.py:371
  26.1 0.0 collective-permute-done.7.relayed
  26.2 0.2 shard_map.54
  26.4 0.7 %collective-permute-start.8 = (f32[80,512]{1,0:T(8,128)S(1)}, f32[80,512]{1,0:T(8,128)S(1)}, u32[]{:S(2)}, u32[]{:S(2)}) collective-permute-start(f32[80,512]{1,0:T(8,128)S(1)} %get-tuple-element.32), channel_id=1, source_target_pairs={{0,0},{1,2},{2,1},{3,3},{4,4},{5,6},{6,5},{7,7},{8,8},{9,10},{10,9... | collective-permute-start | bytes 491528 | tf_op jit(solution)/shard_map/ppermute | solution.py:371
  27.0 3.1 %collective-permute-start.9 = (f32[80,512]{1,0:T(8,128)S(1)}, f32[80,512]{1,0:T(8,128)S(1)}, u32[]{:S(2)}, u32[]{:S(2)}) collective-permute-start(f32[80,512]{1,0:T(8,128)S(1)} %get-tuple-element.33), channel_id=1, source_target_pairs={{0,1},{1,0},{2,3},{3,2},{4,5},{5,4},{6,7},{7,6},{8,9},{9,8},{10,11... | collective-permute-start | bytes 491528 | tf_op jit(solution)/shard_map/ppermute | solution.py:371
  30.2 3.7 %shard_map.55 = (f32[9,20,4,32,128]{4,3,2,1,0:T(8,128)S(1)}, s32[4,20,4,32,128]{4,3,2,1,0:T(8,128)S(1)}) custom-call(s32[20,16,512]{2,1,0:T(8,128)S(1)} %get-tuple-element.34.d_ext, f32[20,16,512]{2,1,0:T(8,128)S(1)} %get-tuple-element.35.m_ext), custom_call_target="tpu_custom_call" | custom-call | flops 20000000 | bytes 20000000 | tf_op jit(solution)/shard_map/pallas_call | solution.py:381
  33.9 5.4 %shard_map.56 = (s32[8,16,512]{2,1,0:T(8,128)}, s32[32,1,128]{2,1,0:T(1,128)S(1)}, f32[9,20,4,32,128]{4,3,2,1,0:T(8,128)S(1)}, s32[4,20,4,32,128]{4,3,2,1,0:T(8,128)S(1)}) custom-call(f32[88,512]{1,0:T(8,128)S(1)} %collective-permute-done.2.ro1, f32[88,512]{1,0:T(8,128)S(1)} %collective-permute-done.3.re1, ...), custom_call_target="tpu_custom_call", output_to_operand_aliasing={{2}: (4, {}), {3}: (5, {})} | custom-call | flops 20000000 | bytes 20000000 | tf_op jit(solution)/shard_map/pallas_call | solution.py:381
  39.3 11.4 %all_to_all.5 = s32[32,1,128]{2,1,0:T(1,128)S(1)} all-to-all(s32[32,1,128]{2,1,0:T(1,128)S(1)} %get-tuple-element.39), channel_id=1, replica_groups=mesh['gz'=8,'gy'=4] {'gz','gy'}, dimensions={0} | all-to-all | bytes 32768 | tf_op jit(solution)/shard_map/all_to_all | solution.py:445
  50.7 0.6 %reduce_sum.9 = s32[128]{0:T(128)} reduce(s32[32,1,128]{2,1,0:T(1,128)S(1)} %all_to_all.5, s32[]{:T(128)} %constant.0.clone.1), dimensions={0,1}, to_apply=%region_0.0 | reduce | flops 3968 | bytes 16900 | tf_op jit(solution)/shard_map/reduce_sum | solution.py:446
  (11 shorter events, 0.1 us)
Async XLA Ops:
  0.6 1.1 %copy-start = (f32[3,8,16,512]{3,2,1,0:T(8,128)S(1)}, f32[3,8,16,512]{3,2,1,0:T(8,128)}, u32[]{:S(2)}) copy-start(f32[3,8,16,512]{3,2,1,0:T(8,128)} %seeds.1) | copy-start | bytes 2359300
  1.9 8.0 %collective-permute-start = (f32[16,512]{1,0:T(8,128)S(1)}, f32[16,512]{1,0:T(8,128)S(1)}, u32[]{:S(2)}, u32[]{:S(2)}) collective-permute-start(f32[16,512]{1,0:T(8,128)S(1)} %get-tuple-element.23), channel_id=1, source_target_pairs={{0,4},{4,8},{8,12},{12,16},{16,20},{20,24},{24,28},{28,0},{1,5},{5... | collective-permute-start | bytes 98312 | tf_op jit(solution)/shard_map/ppermute | solution.py:363
  5.0 3.2 %collective-permute-start.1 = (f32[8,512]{1,0:T(8,128)S(1)}, f32[8,512]{1,0:T(8,128)S(1)}, u32[]{:S(2)}, u32[]{:S(2)}) collective-permute-start(f32[8,512]{1,0:T(8,128)S(1)} %get-tuple-element.24), channel_id=1, source_target_pairs={{0,1},{1,2},{2,3},{3,0},{4,5},{5,6},{6,7},{7,4},{8,9},{9,10},{10,1... | collective-permute-start | bytes 49160 | tf_op jit(solution)/shard_map/ppermute | solution.py:363
  5.0 1.0 %copy-start.1 = (f32[8,16,512]{2,1,0:T(8,128)S(1)}, f32[8,16,512]{2,1,0:T(8,128)}, u32[]{:S(2)}) copy-start(f32[8,16,512]{2,1,0:T(8,128)} %ranks.1) | copy-start | bytes 786436
  5.9 0.9 %copy-start.2 = (s32[8,16,512]{2,1,0:T(8,128)S(1)}, s32[8,16,512]{2,1,0:T(8,128)}, u32[]{:S(2)}) copy-start(s32[8,16,512]{2,1,0:T(8,128)} %flags.1) | copy-start | bytes 786436
  10.5 9.4 %collective-permute-start.4 = (f32[96,512]{1,0:T(8,128)S(1)}, f32[96,512]{1,0:T(8,128)S(1)}, u32[]{:S(2)}, u32[]{:S(2)}) collective-permute-start(f32[96,512]{1,0:T(8,128)S(1)} %get-tuple-element.29), channel_id=1, source_target_pairs={{0,4},{4,0},{8,12},{12,8},{16,20},{20,16},{24,28},{28,24},{1,5},{5... | collective-permute-start | bytes 589832 | tf_op jit(solution)/shard_map/ppermute | solution.py:371
  10.5 15.6 %collective-permute-start.5 = (f32[96,512]{1,0:T(8,128)S(1)}, f32[96,512]{1,0:T(8,128)S(1)}, u32[]{:S(2)}, u32[]{:S(2)}) collective-permute-start(f32[96,512]{1,0:T(8,128)S(1)} %get-tuple-element.30), channel_id=1, source_target_pairs={{0,4},{4,0},{8,12},{12,8},{16,20},{20,16},{24,28},{28,24},{1,5},{5... | collective-permute-start | bytes 589832 | tf_op jit(solution)/shard_map/ppermute | solution.py:371
  12.5 13.6 %collective-permute-start.6 = (f32[96,512]{1,0:T(8,128)S(1)}, f32[96,512]{1,0:T(8,128)S(1)}, u32[]{:S(2)}, u32[]{:S(2)}) collective-permute-start(f32[96,512]{1,0:T(8,128)S(1)} %get-tuple-element.31), channel_id=1, source_target_pairs={{0,0},{4,8},{8,4},{12,16},{16,12},{20,24},{24,20},{28,28},{1,1},{5... | collective-permute-start | bytes 589832 | tf_op jit(solution)/shard_map/ppermute | solution.py:371
  19.9 6.3 %collective-permute-start.7 = (f32[96,512]{1,0:T(8,128)S(1)}, f32[96,512]{1,0:T(8,128)S(1)}, u32[]{:S(2)}, u32[]{:S(2)}) collective-permute-start(f32[96,512]{1,0:T(8,128)S(1)} %collective-permute-done.4.both), channel_id=1, source_target_pairs={{0,8},{4,0},{8,16},{12,4},{16,24},{20,12},{24,28},{28,20},{1,9},{5... | collective-permute-start | bytes 589832 | tf_op jit(solution)/shard_map/ppermute | solution.py:377
  22.5 11.3 %collective-permute-start.2 = (f32[88,512]{1,0:T(8,128)S(1)}, f32[88,512]{1,0:T(8,128)S(1)}, u32[]{:S(2)}, u32[]{:S(2)}) collective-permute-start(f32[88,512]{1,0:T(8,128)S(1)} %get-tuple-element.27), channel_id=1, source_target_pairs={{0,0},{1,2},{2,1},{3,3},{4,4},{5,6},{6,5},{7,7},{8,8},{9,10},{10,9... | collective-permute-start | bytes 540680 | tf_op jit(solution)/shard_map/ppermute | solution.py:371
  23.2 10.7 %collective-permute-start.3 = (f32[88,512]{1,0:T(8,128)S(1)}, f32[88,512]{1,0:T(8,128)S(1)}, u32[]{:S(2)}, u32[]{:S(2)}) collective-permute-start(f32[88,512]{1,0:T(8,128)S(1)} %get-tuple-element.28), channel_id=1, source_target_pairs={{0,1},{1,0},{2,3},{3,2},{4,5},{5,4},{6,7},{7,6},{8,9},{9,8},{10,11... | collective-permute-start | bytes 540680 | tf_op jit(solution)/shard_map/ppermute | solution.py:371
  26.4 7.5 %collective-permute-start.8 = (f32[80,512]{1,0:T(8,128)S(1)}, f32[80,512]{1,0:T(8,128)S(1)}, u32[]{:S(2)}, u32[]{:S(2)}) collective-permute-start(f32[80,512]{1,0:T(8,128)S(1)} %get-tuple-element.32), channel_id=1, source_target_pairs={{0,0},{1,2},{2,1},{3,3},{4,4},{5,6},{6,5},{7,7},{8,8},{9,10},{10,9... | collective-permute-start | bytes 491528 | tf_op jit(solution)/shard_map/ppermute | solution.py:371
  27.0 6.9 %collective-permute-start.9 = (f32[80,512]{1,0:T(8,128)S(1)}, f32[80,512]{1,0:T(8,128)S(1)}, u32[]{:S(2)}, u32[]{:S(2)}) collective-permute-start(f32[80,512]{1,0:T(8,128)S(1)} %get-tuple-element.33), channel_id=1, source_target_pairs={{0,1},{1,0},{2,3},{3,2},{4,5},{5,4},{6,7},{7,6},{8,9},{9,8},{10,11... | collective-permute-start | bytes 491528 | tf_op jit(solution)/shard_map/ppermute | solution.py:371

commit v7 on v6

--- a/solution.py
+++ b/solution.py
@@ -58,11 +58,6 @@
             twice[d, z] = doubled(s)
 
 
-def packed_kernel(ranks, flags, packed):
-    f = flags[...]
-    packed[...] = jnp.where(f == 0, ranks[...], jnp.where(f == 2, -2.0, -1.0))
-
-
 def plane_lists(depth):
     both = list(range(H - RELAYED, H))
     partner = [z for z in range(depth - H, depth) if z not in both]
@@ -70,17 +65,26 @@
     return both, partner, other
 
 
-def strength_kernel(twice, rm, packed, sz_low, sy_low, both, partner, other, d_out, m_out):
+def shared_kernel(twice, rm, packed, sy_low, both, d_out, m_out):
+    strength(twice, rm, packed, None, sy_low, (both,), d_out, m_out)
+
+
+def strength_kernel(twice, rm, packed, sz_low, sy_low, partner, other, d_out, m_out):
+    strength(twice, rm, packed, sz_low, sy_low, (None, partner, other), d_out, m_out)
+
+
+def strength(twice, rm, packed, sz_low, sy_low, messages, d_out, m_out):
     depth, rows, width = packed.shape
     zlo, _ = neighbours("gz")
     ylo, _ = neighbours("gy")
+    from_below = jnp.where(zlo, sz_low[...], 0.0) if sz_low is not None else jnp.zeros((rows, width), F32)
     row = lax.broadcasted_iota(I32, (rows, width), 0)
-    tz_prev = doubled(jnp.where(zlo, sz_low[...], 0.0))
+    tz_prev = doubled(from_below)
     for z in range(depth):
         sy_prev = jnp.where(ylo, sy_low[pl.ds(z, 1), :], 0.0)
         r = jnp.maximum(rm[z], jnp.where(row == 0, sy_prev, 0.0))
         if z == 0:
-            r = jnp.maximum(r, jnp.where(zlo, sz_low[...], 0.0))
+            r = jnp.maximum(r, from_below)
         tx, ty, tz = twice[0, z], twice[1, z], twice[2, z]
         ty_prev = jnp.where(row == 0, doubled(sy_prev), pltpu.roll(ty, 1, 0))
         d = jnp.where(tx >= r, 1, 0) + jnp.where(pltpu.roll(tx, 1, 1) >= r, 2, 0)
@@ -105,8 +109,8 @@
     even = lax.axis_index("gz") % 2 == 0
 
     def send(place):
-        for ref, zs in zip((both, partner, other), plane_lists(depth)):
-            for j, z in enumerate(zs):
+        for ref, zs in zip(messages, plane_lists(depth)):
+            for j, z in enumerate(zs if ref is not None else ()):
                 ref[pl.ds(j * rows, rows), :] = d_out[place(z)].astype(F32)
                 ref[pl.ds((len(zs) + j) * rows, rows), :] = m_out[place(z)]
 
@@ -403,18 +407,17 @@
         8,
         4000000,
     )
+    sy_low = shift(sy_last, "gy", 1)
     sz_low = shift(sz_top, "gz", 1)
-    sy_low = shift(sy_last, "gy", 1)
-    (packed,) = call(packed_kernel, own, (ranks, flags), 8, 4000000)
+    packed = jnp.where(flags == 0, ranks, jnp.where(flags == 2, -2.0, -1.0))
     messages = [of((2 * len(zs) * rows, width), F32) for zs in plane_lists(depth)]
-    both, partner, other, d_own, m_own = call(
-        strength_kernel,
-        messages + [of(ranks.shape, I32)] + own,
-        (twice, rm, packed, sz_low, sy_low),
-        8,
-        4000000,
+    cells = [of(ranks.shape, I32)] + own
+    scratch = [pltpu.VMEM(ranks.shape, I32), pltpu.VMEM(ranks.shape, F32)]
+    (both,) = call(shared_kernel, messages[:1], (twice, rm, packed, sy_low), 8, 4000000, scratch_shapes=scratch)
+    both = swap(both, "gz", 0)
+    partner, other, d_own, m_own = call(
+        strength_kernel, messages[1:] + cells, (twice, rm, packed, sz_low, sy_low), 8, 4000000
     )
-    both = swap(both, "gz", 0)
     partner = swap(partner, "gz", 0)
     relayed = relay(both, "gz")
     other = swap(other, "gz", 1)

time: 51.6 us -> 49.4 us (0.957)
  local copies, waits for them, and re-layouts: 3.03 us -> 1.13 us
  starting transfers between devices: 15.7 us -> 14.6 us
  other arithmetic: 0.56 us -> 1.63 us
    ppermute x7, waiting for transfers between devices: 6.69 us -> 0.02 us  [swap(): return lax.ppermute(value, axis, pairs)]
    ppermute x2, waiting for transfers between devices: 2.99 us -> 8.83 us  [shift(): lax.ppermute(value, axis, [(i, (i + step) % count) for i in range(count)])]
    ppermute x2, starting transfers between devices: 3.02 us -> 0.61 us  [shift(): lax.ppermute(value, axis, [(i, (i + step) % count) for i in range(count)])]
    unnamed x6 -> x2, local copies, waits for them, and re-layouts: 3.03 us -> 1.13 us
    ppermute x1, starting transfers between devices: 2.58 us -> 4.31 us  [relay(): return lax.ppermute(value, axis, pairs)]
    select_n x0 -> x1, other arithmetic: none -> 1.07 us  [per_device(): packed = jnp.where(flags == 0, ranks, jnp.where(flags == 2, -2.0, -1.0))]
    ppermute x1, waiting for transfers between devices: 0.02 us -> 0.75 us  [relay(): return lax.ppermute(value, axis, pairs)]
  transfers between devices with their start and end apart: 10 -> 10, of which waited for: 3 -> 3; matrix products, arithmetic and copies ran while one was open for 0% -> 2% of each run, Pallas kernels for 8% -> 9%
where the time goes in v7:
time: 49.4 us; the launch traced here: 49.1 us
  starting transfers between devices  14.6 us (30%)
  blocking collectives  11 us (22%)
  Pallas kernels  10.5 us (21%)
  waiting for transfers between devices  9.6 us (19%)
  other arithmetic  1.63 us (3%)
  local copies, waits for them, and re-layouts  1.13 us (2%)
  between operations  0.76 us (2%)
    all_to_all x1, blocking collectives, per_device(): everyone = lax.all_to_all(counts, ('gz', 'gy'), 0, 0, tiled=True)  11 us
    pallas_call x7, Pallas kernels, call(): pl.pallas_call(kernel, out_shape=outs, in_specs=[vmem()] * len(args), out...  10.5 us
    ppermute x7, starting transfers between devices, swap(): return lax.ppermute(value, axis, pairs)  9.63 us
    ppermute x2, waiting for transfers between devices, shift(): lax.ppermute(value, axis, [(i, (i + step) % count) for i in range(count)])  8.83 us
    ppermute x1, starting transfers between devices, relay(): return lax.ppermute(value, axis, pairs)  4.31 us
    unnamed x2, local copies, waits for them, and re-layouts  1.13 us
    select_n x1, other arithmetic, per_device(): packed = jnp.where(flags == 0, ranks, jnp.where(flags == 2, -2.0, -1.0))  1.07 us
  transfers between devices with their start and end apart: 10, of which 3 were waited for; matrix products, arithmetic and copies ran while one was open for 2% of the time, Pallas kernels for 9%

profile of v7, /device:TPU:0, one launch (start us, length us, event | category | flops | bytes accessed | tf_op | source)
XLA Modules:
  0.0 49.1 jit_solution(11475484891213748459)
XLA Ops:
  0.6 1.1 %copy-done = f32[3,8,16,512]{3,2,1,0:T(8,128)S(1)} copy-done((f32[3,8,16,512]{3,2,1,0:T(8,128)S(1)}, f32[3,8,16,512]{3,2,1,0:T(8,128)}, u32[]{:S(2)}) %copy-start) | copy-done | bytes 786456
  1.8 0.2 shard_map.50
  1.9 0.5 %collective-permute-start.1 = (f32[8,512]{1,0:T(8,128)S(1)}, f32[8,512]{1,0:T(8,128)S(1)}, u32[]{:S(2)}, u32[]{:S(2)}) collective-permute-start(f32[8,512]{1,0:T(8,128)S(1)} %get-tuple-element.23), channel_id=1, source_target_pairs={{0,1},{1,2},{2,3},{3,0},{4,5},{5,6},{6,7},{7,4},{8,9},{9,10},{10,1... | collective-permute-start | bytes 49160 | tf_op jit(solution)/shard_map/ppermute | solution.py:367
  2.5 1.1 %select_select_fusion.packed = f32[8,16,512]{2,1,0:T(8,128)S(1)} fusion(f32[8,16,512]{2,1,0:T(8,128)} %param.3, s32[8,16,512]{2,1,0:T(8,128)} %param.5), kind=kLoop, calls=%fused_computation | loop fusion | flops 262144 | bytes 786432 | tf_op jit(solution)/shard_map/jit(_where)/select_n | solution.py:412
  3.6 2.3 %collective-permute-done.1.sy_low = f32[8,512]{1,0:T(8,128)S(1)} collective-permute-done((f32[8,512]{1,0:T(8,128)S(1)}, f32[8,512]{1,0:T(8,128)S(1)}, u32[]{:S(2)}, u32[]{:S(2)}) %collective-permute-start.1) | collective-permute-done | bytes 16416 | tf_op jit(solution)/shard_map/ppermute | solution.py:367
  5.9 0.4 shard_map.53
  6.3 2.3 %collective-permute-start.4 = (f32[96,512]{1,0:T(8,128)S(1)}, f32[96,512]{1,0:T(8,128)S(1)}, u32[]{:S(2)}, u32[]{:S(2)}) collective-permute-start(f32[96,512]{1,0:T(8,128)S(1)} %shard_map.53), channel_id=1, source_target_pairs={{0,4},{4,0},{8,12},{12,8},{16,20},{20,16},{24,28},{28,24},{1,5},{5... | collective-permute-start | bytes 589832 | tf_op jit(solution)/shard_map/ppermute | solution.py:375
  8.6 0.1 collective-permute-start
  8.7 6.5 %collective-permute-done.sz_low = f32[16,512]{1,0:T(8,128)S(1)} collective-permute-done((f32[16,512]{1,0:T(8,128)S(1)}, f32[16,512]{1,0:T(8,128)S(1)}, u32[]{:S(2)}, u32[]{:S(2)}) %collective-permute-start) | collective-permute-done | bytes 32800 | tf_op jit(solution)/shard_map/ppermute | solution.py:367
  15.2 0.6 %shard_map.51 = (f32[96,512]{1,0:T(8,128)S(1)}, f32[96,512]{1,0:T(8,128)S(1)}, s32[8,16,512]{2,1,0:T(8,128)S(1)}, f32[8,16,512]{2,1,0:T(8,128)S(1)}) custom-call(f32[3,8,16,512]{3,2,1,0:T(8,128)S(1)} %get-tuple-element.20.twice, f32[8,16,512]{2,1,0:T(8,128)S(1)} %get-tuple-element.21.rm, f32[8,16,512]{2,1,0:T(8,128)S(1)} %select_select_fusion.packed, ...), custom_call_target="tpu_custom_call" | custom-call | flops 4000000 | bytes 4000000 | tf_op jit(solution)/shard_map/pallas_call | solution.py:385
  15.8 0.5 %collective-permute-start.5 = (f32[96,512]{1,0:T(8,128)S(1)}, f32[96,512]{1,0:T(8,128)S(1)}, u32[]{:S(2)}, u32[]{:S(2)}) collective-permute-start(f32[96,512]{1,0:T(8,128)S(1)} %get-tuple-element.28), channel_id=1, source_target_pairs={{0,4},{4,0},{8,12},{12,8},{16,20},{20,16},{24,28},{28,24},{1,5},{5... | collective-permute-start | bytes 589832 | tf_op jit(solution)/shard_map/ppermute | solution.py:375
  16.3 0.7 %collective-permute-start.6 = (f32[96,512]{1,0:T(8,128)S(1)}, f32[96,512]{1,0:T(8,128)S(1)}, u32[]{:S(2)}, u32[]{:S(2)}) collective-permute-start(f32[96,512]{1,0:T(8,128)S(1)} %get-tuple-element.29), channel_id=1, source_target_pairs={{0,0},{4,8},{8,4},{12,16},{16,12},{20,24},{24,20},{28,28},{1,1},{5... | collective-permute-start | bytes 589832 | tf_op jit(solution)/shard_map/ppermute | solution.py:375
  17.0 0.0 collective-permute-done.4.both
  17.0 4.3 %collective-permute-start.7 = (f32[96,512]{1,0:T(8,128)S(1)}, f32[96,512]{1,0:T(8,128)S(1)}, u32[]{:S(2)}, u32[]{:S(2)}) collective-permute-start(f32[96,512]{1,0:T(8,128)S(1)} %collective-permute-done.4.both), channel_id=1, source_target_pairs={{0,8},{4,0},{8,16},{12,4},{16,24},{20,12},{24,28},{28,20},{1,9},{5... | collective-permute-start | bytes 589832 | tf_op jit(solution)/shard_map/ppermute | solution.py:381
  21.4 0.7 %collective-permute-start.2 = (f32[88,512]{1,0:T(8,128)S(1)}, f32[88,512]{1,0:T(8,128)S(1)}, u32[]{:S(2)}, u32[]{:S(2)}) collective-permute-start(f32[88,512]{1,0:T(8,128)S(1)} %get-tuple-element.26), channel_id=1, source_target_pairs={{0,0},{1,2},{2,1},{3,3},{4,4},{5,6},{6,5},{7,7},{8,8},{9,10},{10,9... | collective-permute-start | bytes 540680 | tf_op jit(solution)/shard_map/ppermute | solution.py:375
  22.1 2.9 %collective-permute-start.3 = (f32[88,512]{1,0:T(8,128)S(1)}, f32[88,512]{1,0:T(8,128)S(1)}, u32[]{:S(2)}, u32[]{:S(2)}) collective-permute-start(f32[88,512]{1,0:T(8,128)S(1)} %get-tuple-element.27), channel_id=1, source_target_pairs={{0,1},{1,0},{2,3},{3,2},{4,5},{5,4},{6,7},{7,6},{8,9},{9,8},{10,11... | collective-permute-start | bytes 540680 | tf_op jit(solution)/shard_map/ppermute | solution.py:375
  25.0 0.8 %collective-permute-done.7.relayed = f32[96,512]{1,0:T(8,128)S(1)} collective-permute-done((f32[96,512]{1,0:T(8,128)S(1)}, f32[96,512]{1,0:T(8,128)S(1)}, u32[]{:S(2)}, u32[]{:S(2)}) %collective-permute-start.7) | collective-permute-done | bytes 196640 | tf_op jit(solution)/shard_map/ppermute | solution.py:381
  25.7 0.2 shard_map.54
  25.9 0.7 %collective-permute-start.8 = (f32[80,512]{1,0:T(8,128)S(1)}, f32[80,512]{1,0:T(8,128)S(1)}, u32[]{:S(2)}, u32[]{:S(2)}) collective-permute-start(f32[80,512]{1,0:T(8,128)S(1)} %get-tuple-element.30), channel_id=1, source_target_pairs={{0,0},{1,2},{2,1},{3,3},{4,4},{5,6},{6,5},{7,7},{8,8},{9,10},{10,9... | collective-permute-start | bytes 491528 | tf_op jit(solution)/shard_map/ppermute | solution.py:375
  26.6 1.8 %collective-permute-start.9 = (f32[80,512]{1,0:T(8,128)S(1)}, f32[80,512]{1,0:T(8,128)S(1)}, u32[]{:S(2)}, u32[]{:S(2)}) collective-permute-start(f32[80,512]{1,0:T(8,128)S(1)} %get-tuple-element.31), channel_id=1, source_target_pairs={{0,1},{1,0},{2,3},{3,2},{4,5},{5,4},{6,7},{7,6},{8,9},{9,8},{10,11... | collective-permute-start | bytes 491528 | tf_op jit(solution)/shard_map/ppermute | solution.py:375
  28.4 3.7 %shard_map.55 = (f32[9,20,4,32,128]{4,3,2,1,0:T(8,128)S(1)}, s32[4,20,4,32,128]{4,3,2,1,0:T(8,128)S(1)}) custom-call(s32[20,16,512]{2,1,0:T(8,128)S(1)} %get-tuple-element.32.d_ext, f32[20,16,512]{2,1,0:T(8,128)S(1)} %get-tuple-element.33.m_ext), custom_call_target="tpu_custom_call" | custom-call | flops 20000000 | bytes 20000000 | tf_op jit(solution)/shard_map/pallas_call | solution.py:385
  32.2 5.4 %shard_map.56 = (s32[8,16,512]{2,1,0:T(8,128)}, s32[32,1,128]{2,1,0:T(1,128)S(1)}, f32[9,20,4,32,128]{4,3,2,1,0:T(8,128)S(1)}, s32[4,20,4,32,128]{4,3,2,1,0:T(8,128)S(1)}) custom-call(f32[88,512]{1,0:T(8,128)S(1)} %collective-permute-done.2.ro1, f32[88,512]{1,0:T(8,128)S(1)} %collective-permute-done.3.re1, ...), custom_call_target="tpu_custom_call", output_to_operand_aliasing={{2}: (4, {}), {3}: (5, {})} | custom-call | flops 20000000 | bytes 20000000 | tf_op jit(solution)/shard_map/pallas_call | solution.py:385
  37.6 11.0 %all_to_all.5 = s32[32,1,128]{2,1,0:T(1,128)S(1)} all-to-all(s32[32,1,128]{2,1,0:T(1,128)S(1)} %get-tuple-element.37), channel_id=1, replica_groups=mesh['gz'=8,'gy'=4] {'gz','gy'}, dimensions={0} | all-to-all | bytes 32768 | tf_op jit(solution)/shard_map/all_to_all | solution.py:448
  48.6 0.6 %reduce_sum.9 = s32[128]{0:T(128)} reduce(s32[32,1,128]{2,1,0:T(1,128)S(1)} %all_to_all.5, s32[]{:T(128)} %constant.4.clone.1), dimensions={0,1}, to_apply=%region_0.1 | reduce | flops 3968 | bytes 16900 | tf_op jit(solution)/shard_map/reduce_sum | solution.py:449
  (8 shorter events, 0.1 us)
Async XLA Ops:
  0.6 1.1 %copy-start = (f32[3,8,16,512]{3,2,1,0:T(8,128)S(1)}, f32[3,8,16,512]{3,2,1,0:T(8,128)}, u32[]{:S(2)}) copy-start(f32[3,8,16,512]{3,2,1,0:T(8,128)} %seeds.1) | copy-start | bytes 2359300
  1.9 3.9 %collective-permute-start.1 = (f32[8,512]{1,0:T(8,128)S(1)}, f32[8,512]{1,0:T(8,128)S(1)}, u32[]{:S(2)}, u32[]{:S(2)}) collective-permute-start(f32[8,512]{1,0:T(8,128)S(1)} %get-tuple-element.23), channel_id=1, source_target_pairs={{0,1},{1,2},{2,3},{3,0},{4,5},{5,6},{6,7},{7,4},{8,9},{9,10},{10,1... | collective-permute-start | bytes 49160 | tf_op jit(solution)/shard_map/ppermute | solution.py:367
  6.3 10.7 %collective-permute-start.4 = (f32[96,512]{1,0:T(8,128)S(1)}, f32[96,512]{1,0:T(8,128)S(1)}, u32[]{:S(2)}, u32[]{:S(2)}) collective-permute-start(f32[96,512]{1,0:T(8,128)S(1)} %shard_map.53), channel_id=1, source_target_pairs={{0,4},{4,0},{8,12},{12,8},{16,20},{20,16},{24,28},{28,24},{1,5},{5... | collective-permute-start | bytes 589832 | tf_op jit(solution)/shard_map/ppermute | solution.py:375
  8.6 6.6 %collective-permute-start = (f32[16,512]{1,0:T(8,128)S(1)}, f32[16,512]{1,0:T(8,128)S(1)}, u32[]{:S(2)}, u32[]{:S(2)}) collective-permute-start(f32[16,512]{1,0:T(8,128)S(1)} %get-tuple-element.22), channel_id=1, source_target_pairs={{0,4},{4,8},{8,12},{12,16},{16,20},{20,24},{24,28},{28,0},{1,5},{5... | collective-permute-start | bytes 98312 | tf_op jit(solution)/shard_map/ppermute | solution.py:367
  15.8 9.2 %collective-permute-start.5 = (f32[96,512]{1,0:T(8,128)S(1)}, f32[96,512]{1,0:T(8,128)S(1)}, u32[]{:S(2)}, u32[]{:S(2)}) collective-permute-start(f32[96,512]{1,0:T(8,128)S(1)} %get-tuple-element.28), channel_id=1, source_target_pairs={{0,4},{4,0},{8,12},{12,8},{16,20},{20,16},{24,28},{28,24},{1,5},{5... | collective-permute-start | bytes 589832 | tf_op jit(solution)/shard_map/ppermute | solution.py:375
  16.3 8.7 %collective-permute-start.6 = (f32[96,512]{1,0:T(8,128)S(1)}, f32[96,512]{1,0:T(8,128)S(1)}, u32[]{:S(2)}, u32[]{:S(2)}) collective-permute-start(f32[96,512]{1,0:T(8,128)S(1)} %get-tuple-element.29), channel_id=1, source_target_pairs={{0,0},{4,8},{8,4},{12,16},{16,12},{20,24},{24,20},{28,28},{1,1},{5... | collective-permute-start | bytes 589832 | tf_op jit(solution)/shard_map/ppermute | solution.py:375
  17.0 8.7 %collective-permute-start.7 = (f32[96,512]{1,0:T(8,128)S(1)}, f32[96,512]{1,0:T(8,128)S(1)}, u32[]{:S(2)}, u32[]{:S(2)}) collective-permute-start(f32[96,512]{1,0:T(8,128)S(1)} %collective-permute-done.4.both), channel_id=1, source_target_pairs={{0,8},{4,0},{8,16},{12,4},{16,24},{20,12},{24,28},{28,20},{1,9},{5... | collective-permute-start | bytes 589832 | tf_op jit(solution)/shard_map/ppermute | solution.py:381
  21.4 10.8 %collective-permute-start.2 = (f32[88,512]{1,0:T(8,128)S(1)}, f32[88,512]{1,0:T(8,128)S(1)}, u32[]{:S(2)}, u32[]{:S(2)}) collective-permute-start(f32[88,512]{1,0:T(8,128)S(1)} %get-tuple-element.26), channel_id=1, source_target_pairs={{0,0},{1,2},{2,1},{3,3},{4,4},{5,6},{6,5},{7,7},{8,8},{9,10},{10,9... | collective-permute-start | bytes 540680 | tf_op jit(solution)/shard_map/ppermute | solution.py:375
  22.1 10.1 %collective-permute-start.3 = (f32[88,512]{1,0:T(8,128)S(1)}, f32[88,512]{1,0:T(8,128)S(1)}, u32[]{:S(2)}, u32[]{:S(2)}) collective-permute-start(f32[88,512]{1,0:T(8,128)S(1)} %get-tuple-element.27), channel_id=1, source_target_pairs={{0,1},{1,0},{2,3},{3,2},{4,5},{5,4},{6,7},{7,6},{8,9},{9,8},{10,11... | collective-permute-start | bytes 540680 | tf_op jit(solution)/shard_map/ppermute | solution.py:375
  25.9 6.2 %collective-permute-start.8 = (f32[80,512]{1,0:T(8,128)S(1)}, f32[80,512]{1,0:T(8,128)S(1)}, u32[]{:S(2)}, u32[]{:S(2)}) collective-permute-start(f32[80,512]{1,0:T(8,128)S(1)} %get-tuple-element.30), channel_id=1, source_target_pairs={{0,0},{1,2},{2,1},{3,3},{4,4},{5,6},{6,5},{7,7},{8,8},{9,10},{10,9... | collective-permute-start | bytes 491528 | tf_op jit(solution)/shard_map/ppermute | solution.py:375
  26.6 5.6 %collective-permute-start.9 = (f32[80,512]{1,0:T(8,128)S(1)}, f32[80,512]{1,0:T(8,128)S(1)}, u32[]{:S(2)}, u32[]{:S(2)}) collective-permute-start(f32[80,512]{1,0:T(8,128)S(1)} %get-tuple-element.31), channel_id=1, source_target_pairs={{0,1},{1,0},{2,3},{3,2},{4,5},{5,4},{6,7},{7,6},{8,9},{9,8},{10,11... | collective-permute-start | bytes 491528 | tf_op jit(solution)/shard_map/ppermute | solution.py:375

commit v8 on v7

--- a/solution.py
+++ b/solution.py
@@ -268,10 +268,8 @@
 def stages(fw, iw, depth, rows_of):
     for stage in range(2 * ROUNDS - 1):
         step, reach = stage // 2, H - 1 - stage
-        each = max(n for n in (1, 2, 3, 4) if (depth + 2 * reach) % n == 0)
-
-        @pl.loop(H - reach, H + depth + reach, step=each)
-        def _(i):
+
+        def planes(i, each):
             sites = [(i + j, at) for j in range(each) for at in rows_of(stage)]
             if stage == 0:
                 select(fw, iw, step, sites, set_caps(fw, iw, sites))
@@ -280,6 +278,17 @@
             else:
                 update(fw, iw, step, sites)
 
+        first, count = H - reach, depth + 2 * reach
+        each = 3 if stage == 0 and count % 3 == 0 else 4
+        whole_steps = count // each * each
+
+        @pl.loop(first, first + whole_steps, step=each)
+        def _(i):
+            planes(i, each)
+
+        if count > whole_steps:
+            planes(first + whole_steps, count - whole_steps)
+
 
 def inner_kernel(d_ext, m_ext, fw, iw):
     planes, rows, _ = m_ext.shape
@@ -299,18 +308,27 @@
     planes = depth + 2 * H
     ylo, yhi = neighbours("gy")
     even = lax.axis_index("gy") % 2 == 0
-    for ro, re, early in ((ro1, re1, True), (ro2, re2, False)):
+
+    def unpack(above, below, early):
         patterns, measures, _ = y_layout(depth, early)
         for z, n, at in patterns:
-            e, o = re[pl.ds(at, n), :], ro[pl.ds(at, n), :]
-            above = jnp.where(yhi, jnp.where(even, e, o), 0.0).astype(I32)
-            below = jnp.where(ylo, jnp.where(even, o, e), 0.0).astype(I32)
-            iw[PATTERN, z + H, :, pl.ds(T - n, n), :] = blocks(below)
-            iw[PATTERN, z + H, :, pl.ds(T + rows, n), :] = blocks(above)
+            d = jnp.where(yhi, above[pl.ds(at, n), :], 0.0).astype(I32)
+            iw[PATTERN, z + H, :, pl.ds(T + rows, n), :] = blocks(d)
+            d = jnp.where(ylo, below[pl.ds(at, n), :], 0.0).astype(I32)
+            iw[PATTERN, z + H, :, pl.ds(T - n, n), :] = blocks(d)
         for z, n, at in measures:
-            e, o = re[pl.ds(at, n), :], ro[pl.ds(at, n), :]
-            fw[STATE, z + H, :, pl.ds(T - n, n), :] = blocks(jnp.where(even, o, e))
-            fw[STATE, z + H, :, pl.ds(T + rows, n), :] = blocks(jnp.where(even, e, o))
+            fw[STATE, z + H, :, pl.ds(T + rows, n), :] = blocks(above[pl.ds(at, n), :])
+            fw[STATE, z + H, :, pl.ds(T - n, n), :] = blocks(below[pl.ds(at, n), :])
+
+    @pl.when(even)
+    def _():
+        unpack(re1, ro1, True)
+        unpack(re2, ro2, False)
+
+    @pl.when(jnp.logical_not(even))
+    def _():
+        unpack(ro1, re1, True)
+        unpack(ro2, re2, False)
 
     def low(stage):
         return T - H + stage
@@ -352,12 +370,15 @@
         pltpu.make_async_copy(state_ref.at[z], state_out.at[z], sems.at[z]).start()
         return tuple(totals)
 
-    totals = lax.fori_loop(0, depth, finish, (jnp.zeros(shape, I32),) * ROUNDS)
-    lane = lax.broadcasted_iota(I32, count_out.shape, 2)
-    counts = jnp.zeros(count_out.shape, I32)
+    totals = lax.fori_loop(0, depth, finish, (jnp.zeros(shape, I32),) * ROUNDS, unroll=2 - depth % 2)
+    row = lax.broadcasted_iota(I32, (T, L), 0)
+    lane = lax.broadcasted_iota(I32, (T, L), 1)
+    partial = jnp.zeros((T, L), I32)
     for step in range(ROUNDS):
-        counts = jnp.where(lane == step, jnp.sum(totals[step]), counts)
-    count_out[...] = counts
+        partial = jnp.where(row == step, jnp.sum(jnp.sum(totals[step], axis=0), axis=0, keepdims=True), partial)
+    counts = jnp.where(lane == row, jnp.sum(partial, axis=1, keepdims=True), 0)
+    counts = jnp.sum(counts, axis=0, keepdims=True)
+    count_out[...] = jnp.broadcast_to(counts[None], count_out.shape)
     for z in range(depth):
         pltpu.make_async_copy(state_ref.at[z], state_out.at[z], sems.at[z]).wait()
 

time: 49.4 us -> 48.7 us (0.986)
  Pallas kernels: 10.5 us -> 9.5 us
    pallas_call x7, Pallas kernels: 10.5 us -> 9.5 us  [call(): pl.pallas_call(kernel, out_shape=outs, in_specs=[vmem()] * len(args), out...]
where the time goes in v8:
time: 48.7 us; the launch traced here: 48.5 us
  starting transfers between devices  14.6 us (30%)
  blocking collectives  11.3 us (23%)
  waiting for transfers between devices  9.6 us (20%)
  Pallas kernels  9.5 us (20%)
  other arithmetic  1.63 us (3%)
  local copies, waits for them, and re-layouts  1.13 us (2%)
  between operations  0.76 us (2%)
    all_to_all x1, blocking collectives, per_device(): everyone = lax.all_to_all(counts, ('gz', 'gy'), 0, 0, tiled=True)  11.3 us
    ppermute x7, starting transfers between devices, swap(): return lax.ppermute(value, axis, pairs)  9.63 us
    pallas_call x7, Pallas kernels, call(): pl.pallas_call(kernel, out_shape=outs, in_specs=[vmem()] * len(args), out...  9.5 us
    ppermute x2, waiting for transfers between devices, shift(): lax.ppermute(value, axis, [(i, (i + step) % count) for i in range(count)])  8.83 us
    ppermute x1, starting transfers between devices, relay(): return lax.ppermute(value, axis, pairs)  4.31 us
    unnamed x2, local copies, waits for them, and re-layouts  1.13 us
    select_n x1, other arithmetic, per_device(): packed = jnp.where(flags == 0, ranks, jnp.where(flags == 2, -2.0, -1.0))  1.07 us
  transfers between devices with their start and end apart: 10, of which 3 were waited for; matrix products, arithmetic and copies ran while one was open for 2% of the time, Pallas kernels for 9%

profile of v8, /device:TPU:0, one launch (start us, length us, event | category | flops | bytes accessed | tf_op | source)
XLA Modules:
  0.0 48.5 jit_solution(14738041089385304081)
XLA Ops:
  0.6 1.1 %copy-done = f32[3,8,16,512]{3,2,1,0:T(8,128)S(1)} copy-done((f32[3,8,16,512]{3,2,1,0:T(8,128)S(1)}, f32[3,8,16,512]{3,2,1,0:T(8,128)}, u32[]{:S(2)}) %copy-start) | copy-done | bytes 786456
  1.8 0.2 shard_map.50
  1.9 0.5 %collective-permute-start.1 = (f32[8,512]{1,0:T(8,128)S(1)}, f32[8,512]{1,0:T(8,128)S(1)}, u32[]{:S(2)}, u32[]{:S(2)}) collective-permute-start(f32[8,512]{1,0:T(8,128)S(1)} %get-tuple-element.23), channel_id=1, source_target_pairs={{0,1},{1,2},{2,3},{3,0},{4,5},{5,6},{6,7},{7,4},{8,9},{9,10},{10,1... | collective-permute-start | bytes 49160 | tf_op jit(solution)/shard_map/ppermute | solution.py:388
  2.5 1.1 %select_select_fusion.packed = f32[8,16,512]{2,1,0:T(8,128)S(1)} fusion(f32[8,16,512]{2,1,0:T(8,128)} %param.3, s32[8,16,512]{2,1,0:T(8,128)} %param.5), kind=kLoop, calls=%fused_computation | loop fusion | flops 262144 | bytes 786432 | tf_op jit(solution)/shard_map/jit(_where)/select_n | solution.py:433
  3.6 2.3 %collective-permute-done.1.sy_low = f32[8,512]{1,0:T(8,128)S(1)} collective-permute-done((f32[8,512]{1,0:T(8,128)S(1)}, f32[8,512]{1,0:T(8,128)S(1)}, u32[]{:S(2)}, u32[]{:S(2)}) %collective-permute-start.1) | collective-permute-done | bytes 16416 | tf_op jit(solution)/shard_map/ppermute | solution.py:388
  5.9 0.4 shard_map.53
  6.3 2.3 %collective-permute-start.4 = (f32[96,512]{1,0:T(8,128)S(1)}, f32[96,512]{1,0:T(8,128)S(1)}, u32[]{:S(2)}, u32[]{:S(2)}) collective-permute-start(f32[96,512]{1,0:T(8,128)S(1)} %shard_map.53), channel_id=1, source_target_pairs={{0,4},{4,0},{8,12},{12,8},{16,20},{20,16},{24,28},{28,24},{1,5},{5... | collective-permute-start | bytes 589832 | tf_op jit(solution)/shard_map/ppermute | solution.py:396
  8.6 0.1 collective-permute-start
  8.7 6.5 %collective-permute-done.sz_low = f32[16,512]{1,0:T(8,128)S(1)} collective-permute-done((f32[16,512]{1,0:T(8,128)S(1)}, f32[16,512]{1,0:T(8,128)S(1)}, u32[]{:S(2)}, u32[]{:S(2)}) %collective-permute-start) | collective-permute-done | bytes 32800 | tf_op jit(solution)/shard_map/ppermute | solution.py:388
  15.2 0.6 %shard_map.51 = (f32[96,512]{1,0:T(8,128)S(1)}, f32[96,512]{1,0:T(8,128)S(1)}, s32[8,16,512]{2,1,0:T(8,128)S(1)}, f32[8,16,512]{2,1,0:T(8,128)S(1)}) custom-call(f32[3,8,16,512]{3,2,1,0:T(8,128)S(1)} %get-tuple-element.20.twice, f32[8,16,512]{2,1,0:T(8,128)S(1)} %get-tuple-element.21.rm, f32[8,16,512]{2,1,0:T(8,128)S(1)} %select_select_fusion.packed, ...), custom_call_target="tpu_custom_call" | custom-call | flops 4000000 | bytes 4000000 | tf_op jit(solution)/shard_map/pallas_call | solution.py:406
  15.8 0.5 %collective-permute-start.5 = (f32[96,512]{1,0:T(8,128)S(1)}, f32[96,512]{1,0:T(8,128)S(1)}, u32[]{:S(2)}, u32[]{:S(2)}) collective-permute-start(f32[96,512]{1,0:T(8,128)S(1)} %get-tuple-element.28), channel_id=1, source_target_pairs={{0,4},{4,0},{8,12},{12,8},{16,20},{20,16},{24,28},{28,24},{1,5},{5... | collective-permute-start | bytes 589832 | tf_op jit(solution)/shard_map/ppermute | solution.py:396
  16.3 0.7 %collective-permute-start.6 = (f32[96,512]{1,0:T(8,128)S(1)}, f32[96,512]{1,0:T(8,128)S(1)}, u32[]{:S(2)}, u32[]{:S(2)}) collective-permute-start(f32[96,512]{1,0:T(8,128)S(1)} %get-tuple-element.29), channel_id=1, source_target_pairs={{0,0},{4,8},{8,4},{12,16},{16,12},{20,24},{24,20},{28,28},{1,1},{5... | collective-permute-start | bytes 589832 | tf_op jit(solution)/shard_map/ppermute | solution.py:396
  17.0 0.0 collective-permute-done.4.both
  17.0 4.3 %collective-permute-start.7 = (f32[96,512]{1,0:T(8,128)S(1)}, f32[96,512]{1,0:T(8,128)S(1)}, u32[]{:S(2)}, u32[]{:S(2)}) collective-permute-start(f32[96,512]{1,0:T(8,128)S(1)} %collective-permute-done.4.both), channel_id=1, source_target_pairs={{0,8},{4,0},{8,16},{12,4},{16,24},{20,12},{24,28},{28,20},{1,9},{5... | collective-permute-start | bytes 589832 | tf_op jit(solution)/shard_map/ppermute | solution.py:402
  21.4 0.7 %collective-permute-start.2 = (f32[88,512]{1,0:T(8,128)S(1)}, f32[88,512]{1,0:T(8,128)S(1)}, u32[]{:S(2)}, u32[]{:S(2)}) collective-permute-start(f32[88,512]{1,0:T(8,128)S(1)} %get-tuple-element.26), channel_id=1, source_target_pairs={{0,0},{1,2},{2,1},{3,3},{4,4},{5,6},{6,5},{7,7},{8,8},{9,10},{10,9... | collective-permute-start | bytes 540680 | tf_op jit(solution)/shard_map/ppermute | solution.py:396
  22.1 2.9 %collective-permute-start.3 = (f32[88,512]{1,0:T(8,128)S(1)}, f32[88,512]{1,0:T(8,128)S(1)}, u32[]{:S(2)}, u32[]{:S(2)}) collective-permute-start(f32[88,512]{1,0:T(8,128)S(1)} %get-tuple-element.27), channel_id=1, source_target_pairs={{0,1},{1,0},{2,3},{3,2},{4,5},{5,4},{6,7},{7,6},{8,9},{9,8},{10,11... | collective-permute-start | bytes 540680 | tf_op jit(solution)/shard_map/ppermute | solution.py:396
  25.0 0.8 %collective-permute-done.7.relayed = f32[96,512]{1,0:T(8,128)S(1)} collective-permute-done((f32[96,512]{1,0:T(8,128)S(1)}, f32[96,512]{1,0:T(8,128)S(1)}, u32[]{:S(2)}, u32[]{:S(2)}) %collective-permute-start.7) | collective-permute-done | bytes 196640 | tf_op jit(solution)/shard_map/ppermute | solution.py:402
  25.7 0.2 shard_map.54
  25.9 0.7 %collective-permute-start.8 = (f32[80,512]{1,0:T(8,128)S(1)}, f32[80,512]{1,0:T(8,128)S(1)}, u32[]{:S(2)}, u32[]{:S(2)}) collective-permute-start(f32[80,512]{1,0:T(8,128)S(1)} %get-tuple-element.30), channel_id=1, source_target_pairs={{0,0},{1,2},{2,1},{3,3},{4,4},{5,6},{6,5},{7,7},{8,8},{9,10},{10,9... | collective-permute-start | bytes 491528 | tf_op jit(solution)/shard_map/ppermute | solution.py:396
  26.6 1.8 %collective-permute-start.9 = (f32[80,512]{1,0:T(8,128)S(1)}, f32[80,512]{1,0:T(8,128)S(1)}, u32[]{:S(2)}, u32[]{:S(2)}) collective-permute-start(f32[80,512]{1,0:T(8,128)S(1)} %get-tuple-element.31), channel_id=1, source_target_pairs={{0,1},{1,0},{2,3},{3,2},{4,5},{5,4},{6,7},{7,6},{8,9},{9,8},{10,11... | collective-permute-start | bytes 491528 | tf_op jit(solution)/shard_map/ppermute | solution.py:396
  28.4 3.4 %shard_map.55 = (f32[9,20,4,32,128]{4,3,2,1,0:T(8,128)S(1)}, s32[4,20,4,32,128]{4,3,2,1,0:T(8,128)S(1)}) custom-call(s32[20,16,512]{2,1,0:T(8,128)S(1)} %get-tuple-element.32.d_ext, f32[20,16,512]{2,1,0:T(8,128)S(1)} %get-tuple-element.33.m_ext), custom_call_target="tpu_custom_call" | custom-call | flops 20000000 | bytes 20000000 | tf_op jit(solution)/shard_map/pallas_call | solution.py:406
  31.9 4.8 %shard_map.56 = (s32[8,16,512]{2,1,0:T(8,128)}, s32[32,1,128]{2,1,0:T(1,128)S(1)}, f32[9,20,4,32,128]{4,3,2,1,0:T(8,128)S(1)}, s32[4,20,4,32,128]{4,3,2,1,0:T(8,128)S(1)}) custom-call(f32[88,512]{1,0:T(8,128)S(1)} %collective-permute-done.2.ro1, f32[88,512]{1,0:T(8,128)S(1)} %collective-permute-done.3.re1, ...), custom_call_target="tpu_custom_call", output_to_operand_aliasing={{2}: (4, {}), {3}: (5, {})} | custom-call | flops 20000000 | bytes 20000000 | tf_op jit(solution)/shard_map/pallas_call | solution.py:406
  36.6 11.3 %all_to_all.5 = s32[32,1,128]{2,1,0:T(1,128)S(1)} all-to-all(s32[32,1,128]{2,1,0:T(1,128)S(1)} %get-tuple-element.37), channel_id=1, replica_groups=mesh['gz'=8,'gy'=4] {'gz','gy'}, dimensions={0} | all-to-all | bytes 32768 | tf_op jit(solution)/shard_map/all_to_all | solution.py:469
  47.9 0.6 %reduce_sum.9 = s32[128]{0:T(128)} reduce(s32[32,1,128]{2,1,0:T(1,128)S(1)} %all_to_all.5, s32[]{:T(128)} %constant.4.clone.1), dimensions={0,1}, to_apply=%region_0.1 | reduce | flops 3968 | bytes 16900 | tf_op jit(solution)/shard_map/reduce_sum | solution.py:470
  (8 shorter events, 0.1 us)
Async XLA Ops:
  0.6 1.1 %copy-start = (f32[3,8,16,512]{3,2,1,0:T(8,128)S(1)}, f32[3,8,16,512]{3,2,1,0:T(8,128)}, u32[]{:S(2)}) copy-start(f32[3,8,16,512]{3,2,1,0:T(8,128)} %seeds.1) | copy-start | bytes 2359300
  1.9 3.9 %collective-permute-start.1 = (f32[8,512]{1,0:T(8,128)S(1)}, f32[8,512]{1,0:T(8,128)S(1)}, u32[]{:S(2)}, u32[]{:S(2)}) collective-permute-start(f32[8,512]{1,0:T(8,128)S(1)} %get-tuple-element.23), channel_id=1, source_target_pairs={{0,1},{1,2},{2,3},{3,0},{4,5},{5,6},{6,7},{7,4},{8,9},{9,10},{10,1... | collective-permute-start | bytes 49160 | tf_op jit(solution)/shard_map/ppermute | solution.py:388
  6.3 10.7 %collective-permute-start.4 = (f32[96,512]{1,0:T(8,128)S(1)}, f32[96,512]{1,0:T(8,128)S(1)}, u32[]{:S(2)}, u32[]{:S(2)}) collective-permute-start(f32[96,512]{1,0:T(8,128)S(1)} %shard_map.53), channel_id=1, source_target_pairs={{0,4},{4,0},{8,12},{12,8},{16,20},{20,16},{24,28},{28,24},{1,5},{5... | collective-permute-start | bytes 589832 | tf_op jit(solution)/shard_map/ppermute | solution.py:396
  8.6 6.6 %collective-permute-start = (f32[16,512]{1,0:T(8,128)S(1)}, f32[16,512]{1,0:T(8,128)S(1)}, u32[]{:S(2)}, u32[]{:S(2)}) collective-permute-start(f32[16,512]{1,0:T(8,128)S(1)} %get-tuple-element.22), channel_id=1, source_target_pairs={{0,4},{4,8},{8,12},{12,16},{16,20},{20,24},{24,28},{28,0},{1,5},{5... | collective-permute-start | bytes 98312 | tf_op jit(solution)/shard_map/ppermute | solution.py:388
  15.8 9.2 %collective-permute-start.5 = (f32[96,512]{1,0:T(8,128)S(1)}, f32[96,512]{1,0:T(8,128)S(1)}, u32[]{:S(2)}, u32[]{:S(2)}) collective-permute-start(f32[96,512]{1,0:T(8,128)S(1)} %get-tuple-element.28), channel_id=1, source_target_pairs={{0,4},{4,0},{8,12},{12,8},{16,20},{20,16},{24,28},{28,24},{1,5},{5... | collective-permute-start | bytes 589832 | tf_op jit(solution)/shard_map/ppermute | solution.py:396
  16.3 8.7 %collective-permute-start.6 = (f32[96,512]{1,0:T(8,128)S(1)}, f32[96,512]{1,0:T(8,128)S(1)}, u32[]{:S(2)}, u32[]{:S(2)}) collective-permute-start(f32[96,512]{1,0:T(8,128)S(1)} %get-tuple-element.29), channel_id=1, source_target_pairs={{0,0},{4,8},{8,4},{12,16},{16,12},{20,24},{24,20},{28,28},{1,1},{5... | collective-permute-start | bytes 589832 | tf_op jit(solution)/shard_map/ppermute | solution.py:396
  17.0 8.7 %collective-permute-start.7 = (f32[96,512]{1,0:T(8,128)S(1)}, f32[96,512]{1,0:T(8,128)S(1)}, u32[]{:S(2)}, u32[]{:S(2)}) collective-permute-start(f32[96,512]{1,0:T(8,128)S(1)} %collective-permute-done.4.both), channel_id=1, source_target_pairs={{0,8},{4,0},{8,16},{12,4},{16,24},{20,12},{24,28},{28,20},{1,9},{5... | collective-permute-start | bytes 589832 | tf_op jit(solution)/shard_map/ppermute | solution.py:402
  21.4 10.4 %collective-permute-start.2 = (f32[88,512]{1,0:T(8,128)S(1)}, f32[88,512]{1,0:T(8,128)S(1)}, u32[]{:S(2)}, u32[]{:S(2)}) collective-permute-start(f32[88,512]{1,0:T(8,128)S(1)} %get-tuple-element.26), channel_id=1, source_target_pairs={{0,0},{1,2},{2,1},{3,3},{4,4},{5,6},{6,5},{7,7},{8,8},{9,10},{10,9... | collective-permute-start | bytes 540680 | tf_op jit(solution)/shard_map/ppermute | solution.py:396
  22.1 9.8 %collective-permute-start.3 = (f32[88,512]{1,0:T(8,128)S(1)}, f32[88,512]{1,0:T(8,128)S(1)}, u32[]{:S(2)}, u32[]{:S(2)}) collective-permute-start(f32[88,512]{1,0:T(8,128)S(1)} %get-tuple-element.27), channel_id=1, source_target_pairs={{0,1},{1,0},{2,3},{3,2},{4,5},{5,4},{6,7},{7,6},{8,9},{9,8},{10,11... | collective-permute-start | bytes 540680 | tf_op jit(solution)/shard_map/ppermute | solution.py:396
  25.9 5.9 %collective-permute-start.8 = (f32[80,512]{1,0:T(8,128)S(1)}, f32[80,512]{1,0:T(8,128)S(1)}, u32[]{:S(2)}, u32[]{:S(2)}) collective-permute-start(f32[80,512]{1,0:T(8,128)S(1)} %get-tuple-element.30), channel_id=1, source_target_pairs={{0,0},{1,2},{2,1},{3,3},{4,4},{5,6},{6,5},{7,7},{8,8},{9,10},{10,9... | collective-permute-start | bytes 491528 | tf_op jit(solution)/shard_map/ppermute | solution.py:396
  26.6 5.2 %collective-permute-start.9 = (f32[80,512]{1,0:T(8,128)S(1)}, f32[80,512]{1,0:T(8,128)S(1)}, u32[]{:S(2)}, u32[]{:S(2)}) collective-permute-start(f32[80,512]{1,0:T(8,128)S(1)} %get-tuple-element.31), channel_id=1, source_target_pairs={{0,1},{1,0},{2,3},{3,2},{4,5},{5,4},{6,7},{7,6},{8,9},{9,8},{10,11... | collective-permute-start | bytes 491528 | tf_op jit(solution)/shard_map/ppermute | solution.py:396

commit v9 on v8

--- a/solution.py
+++ b/solution.py
@@ -79,8 +79,10 @@
     ylo, _ = neighbours("gy")
     from_below = jnp.where(zlo, sz_low[...], 0.0) if sz_low is not None else jnp.zeros((rows, width), F32)
     row = lax.broadcasted_iota(I32, (rows, width), 0)
-    tz_prev = doubled(from_below)
-    for z in range(depth):
+    ms = range(depth) if sz_low is not None else range(depth - H, H)
+    ds = range(max(ms[0] - 1, 0), min(ms[-1] + 2, depth))
+    tz_prev = doubled(from_below) if ds[0] == 0 else twice[2, ds[0] - 1]
+    for z in ds:
         sy_prev = jnp.where(ylo, sy_low[pl.ds(z, 1), :], 0.0)
         r = jnp.maximum(rm[z], jnp.where(row == 0, sy_prev, 0.0))
         if z == 0:
@@ -92,7 +94,7 @@
         d += jnp.where(tz >= r, 16, 0) + jnp.where(tz_prev >= r, 32, 0)
         d_out[z] = d
         tz_prev = tz
-    for z in range(depth):
+    for z in ms:
         d = d_out[z]
         i = (pltpu.roll(d, width - 1, 1) & 2) | (pltpu.roll(d, 1, 1) & 1)
         i |= jnp.where(row == rows - 1, 0, pltpu.roll(d, rows - 1, 0) & 8)

time: 48.7 us -> 48.6 us (level)
  no operation moved by 1% of the time
where the time goes in v9:
time: 48.6 us; the launch traced here: 48.4 us
  starting transfers between devices  14.5 us (30%)
  blocking collectives  11.3 us (23%)
  waiting for transfers between devices  9.6 us (20%)
  Pallas kernels  9.42 us (19%)
  other arithmetic  1.63 us (3%)
  local copies, waits for them, and re-layouts  1.13 us (2%)
  between operations  0.76 us (2%)
    all_to_all x1, blocking collectives, per_device(): everyone = lax.all_to_all(counts, ('gz', 'gy'), 0, 0, tiled=True)  11.3 us
    ppermute x7, starting transfers between devices, swap(): return lax.ppermute(value, axis, pairs)  9.63 us
    pallas_call x7, Pallas kernels, call(): pl.pallas_call(kernel, out_shape=outs, in_specs=[vmem()] * len(args), out...  9.42 us
    ppermute x2, waiting for transfers between devices, shift(): lax.ppermute(value, axis, [(i, (i + step) % count) for i in range(count)])  8.83 us
    ppermute x1, starting transfers between devices, relay(): return lax.ppermute(value, axis, pairs)  4.31 us
    unnamed x2, local copies, waits for them, and re-layouts  1.13 us
    select_n x1, other arithmetic, per_device(): packed = jnp.where(flags == 0, ranks, jnp.where(flags == 2, -2.0, -1.0))  1.07 us
  transfers between devices with their start and end apart: 10, of which 3 were waited for; matrix products, arithmetic and copies ran while one was open for 2% of the time, Pallas kernels for 9%

profile of v9, /device:TPU:0, one launch (start us, length us, event | category | flops | bytes accessed | tf_op | source)
XLA Modules:
  0.0 48.4 jit_solution(15769678812964475252)
XLA Ops:
  0.6 1.1 %copy-done = f32[3,8,16,512]{3,2,1,0:T(8,128)S(1)} copy-done((f32[3,8,16,512]{3,2,1,0:T(8,128)S(1)}, f32[3,8,16,512]{3,2,1,0:T(8,128)}, u32[]{:S(2)}) %copy-start) | copy-done | bytes 786456
  1.8 0.2 shard_map.50
  1.9 0.5 %collective-permute-start.1 = (f32[8,512]{1,0:T(8,128)S(1)}, f32[8,512]{1,0:T(8,128)S(1)}, u32[]{:S(2)}, u32[]{:S(2)}) collective-permute-start(f32[8,512]{1,0:T(8,128)S(1)} %get-tuple-element.23), channel_id=1, source_target_pairs={{0,1},{1,2},{2,3},{3,0},{4,5},{5,6},{6,7},{7,4},{8,9},{9,10},{10,1... | collective-permute-start | bytes 49160 | tf_op jit(solution)/shard_map/ppermute | solution.py:390
  2.5 1.1 %select_select_fusion.packed = f32[8,16,512]{2,1,0:T(8,128)S(1)} fusion(f32[8,16,512]{2,1,0:T(8,128)} %param.3, s32[8,16,512]{2,1,0:T(8,128)} %param.5), kind=kLoop, calls=%fused_computation | loop fusion | flops 262144 | bytes 786432 | tf_op jit(solution)/shard_map/jit(_where)/select_n | solution.py:435
  3.6 2.3 %collective-permute-done.1.sy_low = f32[8,512]{1,0:T(8,128)S(1)} collective-permute-done((f32[8,512]{1,0:T(8,128)S(1)}, f32[8,512]{1,0:T(8,128)S(1)}, u32[]{:S(2)}, u32[]{:S(2)}) %collective-permute-start.1) | collective-permute-done | bytes 16416 | tf_op jit(solution)/shard_map/ppermute | solution.py:390
  5.9 0.3 shard_map.53
  6.2 2.3 %collective-permute-start.4 = (f32[96,512]{1,0:T(8,128)S(1)}, f32[96,512]{1,0:T(8,128)S(1)}, u32[]{:S(2)}, u32[]{:S(2)}) collective-permute-start(f32[96,512]{1,0:T(8,128)S(1)} %shard_map.53), channel_id=1, source_target_pairs={{0,4},{4,0},{8,12},{12,8},{16,20},{20,16},{24,28},{28,24},{1,5},{5... | collective-permute-start | bytes 589832 | tf_op jit(solution)/shard_map/ppermute | solution.py:398
  8.5 0.1 collective-permute-start
  8.6 6.5 %collective-permute-done.sz_low = f32[16,512]{1,0:T(8,128)S(1)} collective-permute-done((f32[16,512]{1,0:T(8,128)S(1)}, f32[16,512]{1,0:T(8,128)S(1)}, u32[]{:S(2)}, u32[]{:S(2)}) %collective-permute-start) | collective-permute-done | bytes 32800 | tf_op jit(solution)/shard_map/ppermute | solution.py:390
  15.1 0.6 %shard_map.51 = (f32[96,512]{1,0:T(8,128)S(1)}, f32[96,512]{1,0:T(8,128)S(1)}, s32[8,16,512]{2,1,0:T(8,128)S(1)}, f32[8,16,512]{2,1,0:T(8,128)S(1)}) custom-call(f32[3,8,16,512]{3,2,1,0:T(8,128)S(1)} %get-tuple-element.20.twice, f32[8,16,512]{2,1,0:T(8,128)S(1)} %get-tuple-element.21.rm, f32[8,16,512]{2,1,0:T(8,128)S(1)} %select_select_fusion.packed, ...), custom_call_target="tpu_custom_call" | custom-call | flops 4000000 | bytes 4000000 | tf_op jit(solution)/shard_map/pallas_call | solution.py:408
  15.7 0.5 %collective-permute-start.5 = (f32[96,512]{1,0:T(8,128)S(1)}, f32[96,512]{1,0:T(8,128)S(1)}, u32[]{:S(2)}, u32[]{:S(2)}) collective-permute-start(f32[96,512]{1,0:T(8,128)S(1)} %get-tuple-element.28), channel_id=1, source_target_pairs={{0,4},{4,0},{8,12},{12,8},{16,20},{20,16},{24,28},{28,24},{1,5},{5... | collective-permute-start | bytes 589832 | tf_op jit(solution)/shard_map/ppermute | solution.py:398
  16.2 0.7 %collective-permute-start.6 = (f32[96,512]{1,0:T(8,128)S(1)}, f32[96,512]{1,0:T(8,128)S(1)}, u32[]{:S(2)}, u32[]{:S(2)}) collective-permute-start(f32[96,512]{1,0:T(8,128)S(1)} %get-tuple-element.29), channel_id=1, source_target_pairs={{0,0},{4,8},{8,4},{12,16},{16,12},{20,24},{24,20},{28,28},{1,1},{5... | collective-permute-start | bytes 589832 | tf_op jit(solution)/shard_map/ppermute | solution.py:398
  16.9 4.3 %collective-permute-start.7 = (f32[96,512]{1,0:T(8,128)S(1)}, f32[96,512]{1,0:T(8,128)S(1)}, u32[]{:S(2)}, u32[]{:S(2)}) collective-permute-start(f32[96,512]{1,0:T(8,128)S(1)} %collective-permute-done.4.both), channel_id=1, source_target_pairs={{0,8},{4,0},{8,16},{12,4},{16,24},{20,12},{24,28},{28,20},{1,9},{5... | collective-permute-start | bytes 589832 | tf_op jit(solution)/shard_map/ppermute | solution.py:404
  21.3 0.7 %collective-permute-start.2 = (f32[88,512]{1,0:T(8,128)S(1)}, f32[88,512]{1,0:T(8,128)S(1)}, u32[]{:S(2)}, u32[]{:S(2)}) collective-permute-start(f32[88,512]{1,0:T(8,128)S(1)} %get-tuple-element.26), channel_id=1, source_target_pairs={{0,0},{1,2},{2,1},{3,3},{4,4},{5,6},{6,5},{7,7},{8,8},{9,10},{10,9... | collective-permute-start | bytes 540680 | tf_op jit(solution)/shard_map/ppermute | solution.py:398
  22.0 2.9 %collective-permute-start.3 = (f32[88,512]{1,0:T(8,128)S(1)}, f32[88,512]{1,0:T(8,128)S(1)}, u32[]{:S(2)}, u32[]{:S(2)}) collective-permute-start(f32[88,512]{1,0:T(8,128)S(1)} %get-tuple-element.27), channel_id=1, source_target_pairs={{0,1},{1,0},{2,3},{3,2},{4,5},{5,4},{6,7},{7,6},{8,9},{9,8},{10,11... | collective-permute-start | bytes 540680 | tf_op jit(solution)/shard_map/ppermute | solution.py:398
  24.9 0.8 %collective-permute-done.7.relayed = f32[96,512]{1,0:T(8,128)S(1)} collective-permute-done((f32[96,512]{1,0:T(8,128)S(1)}, f32[96,512]{1,0:T(8,128)S(1)}, u32[]{:S(2)}, u32[]{:S(2)}) %collective-permute-start.7) | collective-permute-done | bytes 196640 | tf_op jit(solution)/shard_map/ppermute | solution.py:404
  25.7 0.2 shard_map.54
  25.9 0.7 %collective-permute-start.8 = (f32[80,512]{1,0:T(8,128)S(1)}, f32[80,512]{1,0:T(8,128)S(1)}, u32[]{:S(2)}, u32[]{:S(2)}) collective-permute-start(f32[80,512]{1,0:T(8,128)S(1)} %get-tuple-element.30), channel_id=1, source_target_pairs={{0,0},{1,2},{2,1},{3,3},{4,4},{5,6},{6,5},{7,7},{8,8},{9,10},{10,9... | collective-permute-start | bytes 491528 | tf_op jit(solution)/shard_map/ppermute | solution.py:398
  26.5 1.8 %collective-permute-start.9 = (f32[80,512]{1,0:T(8,128)S(1)}, f32[80,512]{1,0:T(8,128)S(1)}, u32[]{:S(2)}, u32[]{:S(2)}) collective-permute-start(f32[80,512]{1,0:T(8,128)S(1)} %get-tuple-element.31), channel_id=1, source_target_pairs={{0,1},{1,0},{2,3},{3,2},{4,5},{5,4},{6,7},{7,6},{8,9},{9,8},{10,11... | collective-permute-start | bytes 491528 | tf_op jit(solution)/shard_map/ppermute | solution.py:398
  28.4 3.4 %shard_map.55 = (f32[9,20,4,32,128]{4,3,2,1,0:T(8,128)S(1)}, s32[4,20,4,32,128]{4,3,2,1,0:T(8,128)S(1)}) custom-call(s32[20,16,512]{2,1,0:T(8,128)S(1)} %get-tuple-element.32.d_ext, f32[20,16,512]{2,1,0:T(8,128)S(1)} %get-tuple-element.33.m_ext), custom_call_target="tpu_custom_call" | custom-call | flops 20000000 | bytes 20000000 | tf_op jit(solution)/shard_map/pallas_call | solution.py:408
  31.7 0.0 collective-permute-done.3.re1
  31.8 4.8 %shard_map.56 = (s32[8,16,512]{2,1,0:T(8,128)}, s32[32,1,128]{2,1,0:T(1,128)S(1)}, f32[9,20,4,32,128]{4,3,2,1,0:T(8,128)S(1)}, s32[4,20,4,32,128]{4,3,2,1,0:T(8,128)S(1)}) custom-call(f32[88,512]{1,0:T(8,128)S(1)} %collective-permute-done.2.ro1, f32[88,512]{1,0:T(8,128)S(1)} %collective-permute-done.3.re1, ...), custom_call_target="tpu_custom_call", output_to_operand_aliasing={{2}: (4, {}), {3}: (5, {})} | custom-call | flops 20000000 | bytes 20000000 | tf_op jit(solution)/shard_map/pallas_call | solution.py:408
  36.5 11.3 %all_to_all.5 = s32[32,1,128]{2,1,0:T(1,128)S(1)} all-to-all(s32[32,1,128]{2,1,0:T(1,128)S(1)} %get-tuple-element.37), channel_id=1, replica_groups=mesh['gz'=8,'gy'=4] {'gz','gy'}, dimensions={0} | all-to-all | bytes 32768 | tf_op jit(solution)/shard_map/all_to_all | solution.py:471
  47.8 0.6 %reduce_sum.9 = s32[128]{0:T(128)} reduce(s32[32,1,128]{2,1,0:T(1,128)S(1)} %all_to_all.5, s32[]{:T(128)} %constant.4.clone.1), dimensions={0,1}, to_apply=%region_0.1 | reduce | flops 3968 | bytes 16900 | tf_op jit(solution)/shard_map/reduce_sum | solution.py:472
  (8 shorter events, 0.1 us)
Async XLA Ops:
  0.6 1.1 %copy-start = (f32[3,8,16,512]{3,2,1,0:T(8,128)S(1)}, f32[3,8,16,512]{3,2,1,0:T(8,128)}, u32[]{:S(2)}) copy-start(f32[3,8,16,512]{3,2,1,0:T(8,128)} %seeds.1) | copy-start | bytes 2359300
  1.9 3.9 %collective-permute-start.1 = (f32[8,512]{1,0:T(8,128)S(1)}, f32[8,512]{1,0:T(8,128)S(1)}, u32[]{:S(2)}, u32[]{:S(2)}) collective-permute-start(f32[8,512]{1,0:T(8,128)S(1)} %get-tuple-element.23), channel_id=1, source_target_pairs={{0,1},{1,2},{2,3},{3,0},{4,5},{5,6},{6,7},{7,4},{8,9},{9,10},{10,1... | collective-permute-start | bytes 49160 | tf_op jit(solution)/shard_map/ppermute | solution.py:390
  6.2 10.7 %collective-permute-start.4 = (f32[96,512]{1,0:T(8,128)S(1)}, f32[96,512]{1,0:T(8,128)S(1)}, u32[]{:S(2)}, u32[]{:S(2)}) collective-permute-start(f32[96,512]{1,0:T(8,128)S(1)} %shard_map.53), channel_id=1, source_target_pairs={{0,4},{4,0},{8,12},{12,8},{16,20},{20,16},{24,28},{28,24},{1,5},{5... | collective-permute-start | bytes 589832 | tf_op jit(solution)/shard_map/ppermute | solution.py:398
  8.5 6.6 %collective-permute-start = (f32[16,512]{1,0:T(8,128)S(1)}, f32[16,512]{1,0:T(8,128)S(1)}, u32[]{:S(2)}, u32[]{:S(2)}) collective-permute-start(f32[16,512]{1,0:T(8,128)S(1)} %get-tuple-element.22), channel_id=1, source_target_pairs={{0,4},{4,8},{8,12},{12,16},{16,20},{20,24},{24,28},{28,0},{1,5},{5... | collective-permute-start | bytes 98312 | tf_op jit(solution)/shard_map/ppermute | solution.py:390
  15.7 9.2 %collective-permute-start.5 = (f32[96,512]{1,0:T(8,128)S(1)}, f32[96,512]{1,0:T(8,128)S(1)}, u32[]{:S(2)}, u32[]{:S(2)}) collective-permute-start(f32[96,512]{1,0:T(8,128)S(1)} %get-tuple-element.28), channel_id=1, source_target_pairs={{0,4},{4,0},{8,12},{12,8},{16,20},{20,16},{24,28},{28,24},{1,5},{5... | collective-permute-start | bytes 589832 | tf_op jit(solution)/shard_map/ppermute | solution.py:398
  16.2 8.7 %collective-permute-start.6 = (f32[96,512]{1,0:T(8,128)S(1)}, f32[96,512]{1,0:T(8,128)S(1)}, u32[]{:S(2)}, u32[]{:S(2)}) collective-permute-start(f32[96,512]{1,0:T(8,128)S(1)} %get-tuple-element.29), channel_id=1, source_target_pairs={{0,0},{4,8},{8,4},{12,16},{16,12},{20,24},{24,20},{28,28},{1,1},{5... | collective-permute-start | bytes 589832 | tf_op jit(solution)/shard_map/ppermute | solution.py:398
  16.9 8.7 %collective-permute-start.7 = (f32[96,512]{1,0:T(8,128)S(1)}, f32[96,512]{1,0:T(8,128)S(1)}, u32[]{:S(2)}, u32[]{:S(2)}) collective-permute-start(f32[96,512]{1,0:T(8,128)S(1)} %collective-permute-done.4.both), channel_id=1, source_target_pairs={{0,8},{4,0},{8,16},{12,4},{16,24},{20,12},{24,28},{28,20},{1,9},{5... | collective-permute-start | bytes 589832 | tf_op jit(solution)/shard_map/ppermute | solution.py:404
  21.3 10.4 %collective-permute-start.2 = (f32[88,512]{1,0:T(8,128)S(1)}, f32[88,512]{1,0:T(8,128)S(1)}, u32[]{:S(2)}, u32[]{:S(2)}) collective-permute-start(f32[88,512]{1,0:T(8,128)S(1)} %get-tuple-element.26), channel_id=1, source_target_pairs={{0,0},{1,2},{2,1},{3,3},{4,4},{5,6},{6,5},{7,7},{8,8},{9,10},{10,9... | collective-permute-start | bytes 540680 | tf_op jit(solution)/shard_map/ppermute | solution.py:398
  22.0 9.8 %collective-permute-start.3 = (f32[88,512]{1,0:T(8,128)S(1)}, f32[88,512]{1,0:T(8,128)S(1)}, u32[]{:S(2)}, u32[]{:S(2)}) collective-permute-start(f32[88,512]{1,0:T(8,128)S(1)} %get-tuple-element.27), channel_id=1, source_target_pairs={{0,1},{1,0},{2,3},{3,2},{4,5},{5,4},{6,7},{7,6},{8,9},{9,8},{10,11... | collective-permute-start | bytes 540680 | tf_op jit(solution)/shard_map/ppermute | solution.py:398
  25.9 5.9 %collective-permute-start.8 = (f32[80,512]{1,0:T(8,128)S(1)}, f32[80,512]{1,0:T(8,128)S(1)}, u32[]{:S(2)}, u32[]{:S(2)}) collective-permute-start(f32[80,512]{1,0:T(8,128)S(1)} %get-tuple-element.30), channel_id=1, source_target_pairs={{0,0},{1,2},{2,1},{3,3},{4,4},{5,6},{6,5},{7,7},{8,8},{9,10},{10,9... | collective-permute-start | bytes 491528 | tf_op jit(solution)/shard_map/ppermute | solution.py:398
  26.5 5.2 %collective-permute-start.9 = (f32[80,512]{1,0:T(8,128)S(1)}, f32[80,512]{1,0:T(8,128)S(1)}, u32[]{:S(2)}, u32[]{:S(2)}) collective-permute-start(f32[80,512]{1,0:T(8,128)S(1)} %get-tuple-element.31), channel_id=1, source_target_pairs={{0,1},{1,0},{2,3},{3,2},{4,5},{5,4},{6,7},{7,6},{8,9},{9,8},{10,11... | collective-permute-start | bytes 491528 | tf_op jit(solution)/shard_map/ppermute | solution.py:398
